TPU v7x, 32 devices: a whole 2x2x4 slice. The times are simulated.
32 devices in a mesh: turn: 4 (over y, core), blk: 4 (over z), strip: 2 (over x).
Axes of the slice: x: 2, y: 2, z: 4, core: 2. Of those that a mesh axis runs over, the one named last changes fastest.
Arguments:
- echoes: bfloat16 [2, 256, 32768], P(None, 'blk', ('turn', 'strip')), may hold values from -6 to 6
- filters: bfloat16 [2, 8, 32768], P(None, 'blk'), may hold values from -6 to 6
- slab_index: int32 [256], P(('blk', 'turn')), may hold values from 0 to 7
- shifts: int32 [256], P(('blk', 'turn')), may hold values from 0 to 32767
Outputs:
- focused: float32 [2, 256, 32768], P(None, ('blk', 'turn'), 'strip')
All inputs are finite; a program needn't handle non-finite values.
Results may differ from a plain program's by a relative error of at most 0.0003.
Values may be sent and summed in bfloat16 or wider, within the bound.
No kernel may reach another device: no remote copies, remote signals or barrier semaphores. Data moves between devices by JAX's collectives and lax.ppermute only.
A program may use at most 128 MiB of HBM per device.

v0:
```python
import functools
import math

import jax
import jax.numpy as jnp
import numpy as np
from jax import lax
from jax.experimental import pallas as pl
from jax.experimental.pallas import tpu as pltpu
from jax.sharding import PartitionSpec as P


LANES = 128
CHUNKS = (8, 8)


def hi_lo(table):
    high = table.astype(jnp.bfloat16)
    low = (table - high.astype(np.float64)).astype(jnp.bfloat16)
    return high, low


def block_matrix(phase, sign):
    cos, sin = np.cos(phase), sign * np.sin(phase)
    return np.concatenate([np.concatenate([cos, -sin], 1), np.concatenate([sin, cos], 1)], 0)


@functools.lru_cache(maxsize=None)
def tables(length, sources, out_len):
    slow = length // LANES
    half = slow // 2
    part = half // sources
    out_half = out_len // LANES // 2
    q = np.arange(slow)
    c = np.arange(half)
    lane = np.arange(LANES)
    lane_phase = 2 * np.pi * (lane[:, None] * lane[None, :] % LANES) / LANES
    twist = 2 * np.pi * (q[:, None] * lane[None, :]) / length
    first, last = [], []
    for parity in range(2):
        index = 2 * c + parity
        table = block_matrix(2 * np.pi * (c[:, None] * index[None, :] % slow) / slow, -1.0)
        table = table.reshape(slow, 2, sources, part).transpose(0, 2, 1, 3).reshape(slow, slow)
        first.append(np.stack(hi_lo(table)))
        table = block_matrix(2 * np.pi * (index[:out_half, None] * c[None, :] % slow) / slow, 1.0) / length
        last.append(np.stack(hi_lo(table)))
    middle = np.stack(hi_lo(block_matrix(lane_phase, -1.0).T))
    back = np.stack(hi_lo(block_matrix(lane_phase, 1.0).T))
    parts = [np.stack(first), middle, back, np.stack(last)]
    dots = np.concatenate([a.reshape(-1, a.shape[-1]) for a in parts], 0)
    return dots, np.stack([np.cos(twist), np.sin(twist)]).astype(np.float32)


def split(value):
    high = value.astype(jnp.bfloat16)
    return high, (value - high.astype(jnp.float32)).astype(jnp.bfloat16)


def dot(a, b):
    return jnp.dot(a, b, preferred_element_type=jnp.float32)


def pack_kernel(jobs, total, part, ids, echoes, *refs):
    turn, outs, spread = ids[0], refs[:-1], refs[-1]
    for k, (flip, row0, rows) in enumerate(jobs):
        for row in range(0, rows, 8):
            start = pl.multiple_of((turn ^ flip) * total + row0 + row, 8)
            for p in range(2):
                block = echoes[p, pl.ds(start, 8), :].astype(jnp.float32)
                for q in range(part):
                    spread[k, row // 8, p, q * 8 : (q + 1) * 8] = block[:, q * LANES : (q + 1) * LANES]
    for k, (flip, row0, rows) in enumerate(jobs):
        for row in range(rows):
            for p in range(2):
                for e in range(2):
                    start = e * 8 + row % 8
                    picked = spread[k, row // 8, p, pl.ds(start, part // 2, stride=16), :]
                    outs[k][p, row, e] = picked.astype(jnp.bfloat16)


def pack(ids, echoes, jobs, total, cost):
    part = echoes.shape[2] // LANES
    vm = pl.BlockSpec(memory_space=pltpu.VMEM)
    sm = pl.BlockSpec(memory_space=pltpu.SMEM)
    tiles = max(rows for _, _, rows in jobs) // 8
    return pl.pallas_call(
        functools.partial(pack_kernel, tuple(jobs), total, part),
        in_specs=[sm, vm],
        out_specs=[vm] * len(jobs),
        out_shape=[jax.ShapeDtypeStruct((2, rows, 2, part // 2, LANES), jnp.bfloat16) for _, _, rows in jobs],
        scratch_shapes=[pltpu.VMEM((len(jobs), tiles, 2, part * 8, LANES), jnp.float32)],
        compiler_params=pltpu.CompilerParams(vmem_limit_bytes=12 * 1024 * 1024),
        cost_estimate=pl.CostEstimate(flops=10**6, bytes_accessed=cost, transcendentals=0),
    )(ids, echoes)


def order_kernel(width, ids, dots, twist, out):
    size = dots.shape[1]
    row_ids = lax.broadcasted_iota(jnp.int32, (size, size), 0)
    col_ids = lax.broadcasted_iota(jnp.int32, (size, size), 1)
    order = jnp.where(row_ids == (col_ids ^ (ids[2] * width)), 1.0, 0.0).astype(jnp.bfloat16)
    out[...] = dot(dots[: 4 * size], order).astype(jnp.bfloat16)


def order_tables(ids, dots, twist, width):
    vm = pl.BlockSpec(memory_space=pltpu.VMEM)
    sm = pl.BlockSpec(memory_space=pltpu.SMEM)
    size = dots.shape[1]
    return pl.pallas_call(
        functools.partial(order_kernel, width),
        in_specs=[sm, vm, vm],
        out_specs=vm,
        out_shape=jax.ShapeDtypeStruct((4 * size, size), jnp.bfloat16),
        compiler_params=pltpu.CompilerParams(vmem_limit_bytes=8 * 1024 * 1024),
        cost_estimate=pl.CostEstimate(flops=10**6, bytes_accessed=4 * 10**6, transcendentals=0),
    )(ids, dots, twist)


def turn_kernel(ids, filters, out, turned):
    core = ids[1]
    slabs = filters.shape[1]
    for p in range(2):
        for d in range(LANES):
            at = pl.multiple_of((2 * d + core) * LANES, LANES)
            lanes = filters[p, :, pl.ds(at, LANES)].astype(jnp.float32)
            for slab in range(slabs):
                turned[slab, p, d : d + 1, :] = lanes[slab : slab + 1]
    for p in range(2):
        for slab in range(slabs):
            out[slab, p] = turned[slab, p].T.astype(jnp.bfloat16)


def turn_filters(ids, filters):
    vm = pl.BlockSpec(memory_space=pltpu.VMEM)
    sm = pl.BlockSpec(memory_space=pltpu.SMEM)
    shape = (filters.shape[1], 2, LANES, LANES)
    return pl.pallas_call(
        turn_kernel,
        in_specs=[sm, vm],
        out_specs=vm,
        out_shape=jax.ShapeDtypeStruct(shape, jnp.bfloat16),
        scratch_shapes=[pltpu.VMEM(shape, jnp.float32)],
        compiler_params=pltpu.CompilerParams(vmem_limit_bytes=4 * 1024 * 1024),
        cost_estimate=pl.CostEstimate(flops=10**6, bytes_accessed=2 * 10**6, transcendentals=0),
    )(ids, filters)


def focus_kernel(bases, pieces, rows, row0, slow, out_slow, *refs):
    sources = len(bases)
    scalars = refs[0]
    blocks = refs[1 : 1 + sources]
    own = refs[1 + sources : 1 + sources + pieces]
    other = refs[1 + sources + pieces : 1 + sources + 2 * pieces]
    (
        slow_cos, slow_sin, fast_cos, fast_sin, first_dots_ref, dots, twist, _, out,
        s1, y1, s2, y2, s3, y3, s4, slow_ramp, filt,
    ) = refs[1 + sources + 2 * pieces :]
    core = scalars[0]
    per_zone = own[0].shape[0]
    for k in range(pieces):
        filt[core, k * per_zone : (k + 1) * per_zone] = own[k][...]
        filt[1 - core, k * per_zone : (k + 1) * per_zone] = other[k][...]
    slow_ramp[0] = slow_cos[...].T
    slow_ramp[1] = slow_sin[...].T
    half = slow // 2
    wide = 2 * LANES
    first = [[first_dots_ref.at[pl.ds((2 * e + k) * slow, slow)] for k in range(2)] for e in range(2)]
    base = 4 * slow
    middle = [dots.at[pl.ds(base + k * wide, wide)] for k in range(2)]
    back = [dots.at[pl.ds(base + (2 + k) * wide, wide)] for k in range(2)]
    base += 4 * wide
    last = [[dots.at[pl.ds(base + (2 * e + k) * out_slow, out_slow)] for k in range(2)] for e in range(2)]

    def first_dots(pair):
        for e in range(2):
            data = jnp.concatenate(
                [
                    jnp.concatenate([block[p, base + r, e] for block, base in zip(blocks, bases) for p in range(2)], 0)
                    for r in (2 * pair, 2 * pair + 1)
                ],
                1,
            )
            s1[pair, e] = dot(first[e][0][...], data) + dot(first[e][1][...], data)

    def first_twist(pair):
        for i in range(2):
            lanes = slice(i * LANES, (i + 1) * LANES)
            for part in range(2):
                rows_c = slice(part * half, (part + 1) * half)
                even_re, even_im = s1[pair, 0, :half, lanes], s1[pair, 0, half:, lanes]
                odd_re, odd_im = s1[pair, 1, :half, lanes], s1[pair, 1, half:, lanes]
                if part == 0:
                    re, im = even_re + odd_re, even_im + odd_im
                else:
                    re, im = even_re - odd_re, even_im - odd_im
                tw_re, tw_im = twist[0, rows_c], twist[1, rows_c]
                (rh, rl), (ih, il) = split(re * tw_re + im * tw_im), split(im * tw_re - re * tw_im)
                y1[pair, i, rows_c] = jnp.concatenate([rh, ih, rl, il], 1)

    def lane_dots(pair, source, table, target):
        mix = source[pair].reshape(2 * slow, 2 * wide)
        target[pair] = (
            dot(mix[:, :wide], table[0][...]) + dot(mix[:, wide:], table[0][...]) + dot(mix[:, :wide], table[1][...])
        )

    def respond(pair):
        for i in range(2):
            r = row0 + 2 * pair + i
            slab = scalars[1 + r]
            v_re, v_im = fast_cos[r : r + 1], fast_sin[r : r + 1]
            for part in range(2):
                rows_s = slice(i * slow + part * half, i * slow + (part + 1) * half)
                re, im = s2[pair, rows_s, :LANES], s2[pair, rows_s, LANES:]
                h_re = filt[part, slab, 0].astype(jnp.float32)
                h_im = filt[part, slab, 1].astype(jnp.float32)
                re, im = re * h_re - im * h_im, re * h_im + im * h_re
                (rh, rl), (ih, il) = split(re * v_re - im * v_im), split(re * v_im + im * v_re)
                y2[pair, i, part * half : (part + 1) * half] = jnp.concatenate([rh, ih, rl, il], 1)

    def back_twist(pair):
        for i in range(2):
            r = row0 + 2 * pair + i
            lanes = slice(i * LANES, (i + 1) * LANES)
            parts = []
            for part in range(2):
                rows_c = slice(part * half, (part + 1) * half)
                rows_s = slice(i * slow + part * half, i * slow + (part + 1) * half)
                re, im = s3[pair, rows_s, :LANES], s3[pair, rows_s, LANES:]
                tw_re, tw_im = twist[0, rows_c], twist[1, rows_c]
                re, im = re * tw_re - im * tw_im, re * tw_im + im * tw_re
                u_re, u_im = slow_ramp[0, rows_c, r : r + 1], slow_ramp[1, rows_c, r : r + 1]
                parts.append((re * u_re - im * u_im, re * u_im + im * u_re))
            (a_re, a_im), (b_re, b_im) = parts
            for e, (re, im) in enumerate(((a_re + b_re, a_im + b_im), (a_re - b_re, a_im - b_im))):
                (rh, rl), (ih, il) = split(re), split(im)
                y3[pair, e, 0, :, lanes] = jnp.concatenate([rh, ih], 0)
                y3[pair, e, 1, :, lanes] = jnp.concatenate([rl, il], 0)

    def last_dots(pair):
        for e in range(2):
            high, low = y3[pair, e, 0], y3[pair, e, 1]
            s4[pair, e] = (
                dot(last[e][0][...], high) + dot(last[e][1][...], high) + dot(last[e][0][...], low)
            )

    def store(pair):
        count = out_slow // 2
        for i in range(2):
            r = (row0 + 2 * pair + i) % 8
            for e in range(2):
                for p in range(2):
                    for q in range(0, count, 8):
                        out[p, 0, pl.ds((2 * q + e) * 8 + r, 8, stride=16), :] = s4[
                            pair, e, p * count + q : p * count + q + 8, i * LANES : (i + 1) * LANES
                        ]

    steps = [
        first_dots,
        first_twist,
        lambda pair: lane_dots(pair, y1, middle, s2),
        respond,
        lambda pair: lane_dots(pair, y2, back, s3),
        back_twist,
        last_dots,
        store,
    ]
    streams = [[(step, pair) for pair in range(k, rows // 2, 2) for step in range(8)] for k in range(2)]
    for t in range(len(streams[0]) + 1):
        now = [s[t - k] for k, s in enumerate(streams) if 0 <= t - k < len(s)]
        for step, pair in sorted(now, key=lambda job: job[0] % 2):
            steps[step](pair)


def focus(blocks, bases, own, other, ramps, first, t, scalars, held, rows, row0, total, slow, out_slow):
    slots, pieces = rows // 2, len(own)
    hbm = pl.BlockSpec(memory_space=pltpu.HBM)
    sm = pl.BlockSpec(memory_space=pltpu.SMEM)
    tile = row0 // 8
    whole = pl.BlockSpec((2, 1, out_slow * 8, LANES), lambda i: (0, tile, 0, 0))

    def full(a):
        return pl.BlockSpec(a.shape, lambda i: (0,) * a.ndim)

    operands = [*own, *other, *ramps, first, *t]
    aliases = {}
    if held is None:
        held = jnp.zeros((8, LANES), jnp.float32)
    else:
        aliases = {1 + len(blocks) + len(operands): 0}
    return pl.pallas_call(
        functools.partial(focus_kernel, tuple(bases), pieces, rows, row0, slow, out_slow),
        grid=(1,),
        in_specs=[sm] + [full(a) for a in blocks + operands] + [hbm],
        out_specs=whole,
        out_shape=jax.ShapeDtypeStruct((2, total // 8, out_slow * 8, LANES), jnp.float32),
        scratch_shapes=[
            pltpu.VMEM((slots, 2, slow, 2 * LANES), jnp.float32),
            pltpu.VMEM((slots, 2, slow, 4 * LANES), jnp.bfloat16),
            pltpu.VMEM((slots, 2 * slow, 2 * LANES), jnp.float32),
            pltpu.VMEM((slots, 2, slow, 4 * LANES), jnp.bfloat16),
            pltpu.VMEM((slots, 2 * slow, 2 * LANES), jnp.float32),
            pltpu.VMEM((slots, 2, 2, slow, 2 * LANES), jnp.bfloat16),
            pltpu.VMEM((slots, 2, out_slow, 2 * LANES), jnp.float32),
            pltpu.VMEM((2, slow, total), jnp.float32),
            pltpu.VMEM((2, pieces * own[0].shape[0], *own[0].shape[1:]), jnp.bfloat16),
        ],
        input_output_aliases=aliases,
        compiler_params=pltpu.CompilerParams(vmem_limit_bytes=24 * 1024 * 1024),
        cost_estimate=pl.CostEstimate(flops=3 * 10**9, bytes_accessed=8 * 10**6, transcendentals=0),
    )(scalars, *blocks, *operands, held)


def swap(value, axis, flip):
    size = lax.axis_size(axis)
    return lax.ppermute(value, axis, [(a, a ^ flip) for a in range(size)])


def per_device(echoes, filters, slab_index, shifts):
    turns, strips, zones = lax.axis_size("turn"), lax.axis_size("strip"), lax.axis_size("blk")
    turn, strip, zone = lax.axis_index("turn"), lax.axis_index("strip"), lax.axis_index("blk")
    sources = turns * strips
    length = echoes.shape[2] * sources
    slow = length // LANES
    total = slab_index.shape[0]
    out_slow = slow // strips
    per_zone = filters.shape[1]
    width = slow // sources
    me = turn * strips + strip
    core = turn % 2
    ids = jnp.stack([turn, core, me]).astype(jnp.int32)
    t = [jnp.asarray(a) for a in tables(length, sources, length // strips)]

    jobs = [[(0, 0, total), (1, 0, total)], []]
    starts = [sum(CHUNKS[:k]) for k in range(len(CHUNKS))]
    for k, rows in enumerate(CHUNKS):
        jobs[min(k, 1)] += [(flip, starts[k], rows) for flip in range(2, turns)]
    sent = pack(ids, echoes, jobs[0], total, 32 * 10**6)
    more = pack(ids, echoes, jobs[1], total, 4 * 10**6)
    half = turn_filters(ids, filters)
    first = order_tables(ids, *t, width)
    held = {}
    for (flip, start, rows), block in zip(jobs[0] + jobs[1], [*sent, *more]):
        if flip:
            block = swap(block, "turn", flip)
        for ds in range(strips):
            mine = swap(block, "strip", ds) if ds else block
            held[flip * strips + ds, start] = mine

    own = [half] + [swap(half, "blk", d) for d in range(1, zones)]
    other = [swap(piece, "turn", 1) for piece in own]
    local_slab = (slab_index // per_zone ^ zone) * per_zone + slab_index % per_zone

    c = jnp.arange(slow, dtype=jnp.int32)[None, :]
    offset = (shifts + (strips - strip) * (length // strips)) % length
    c_angle = (offset[:, None] * c % length).astype(jnp.float32) * (2.0 * math.pi / length)
    d = jnp.arange(LANES, dtype=jnp.int32)[None, :]
    d_angle = (d * (shifts[:, None] % LANES) % LANES).astype(jnp.float32) * (2.0 * math.pi / LANES)
    ramps = (jnp.cos(c_angle), -jnp.sin(c_angle), jnp.cos(d_angle), -jnp.sin(d_angle))
    scalars = jnp.concatenate([core[None].astype(jnp.int32), local_slab])

    image = None
    for start, rows in zip(starts, CHUNKS):
        blocks, bases = [], []
        for slot in range(sources):
            whole = slot // strips < 2
            blocks.append(held[slot, 0 if whole else start])
            bases.append(start if whole else 0)
        image = focus(blocks, bases, own, other, ramps, first, t, scalars, image, rows, start, total, slow, out_slow)
    image = image.reshape(2, total // 8, out_slow, 8, LANES).transpose(0, 1, 3, 2, 4)
    return image.reshape(2, total, out_slow * LANES)


def solution(mesh):
    in_specs = (
        P(None, "blk", ("turn", "strip")),
        P(None, "blk", None),
        P(("blk", "turn")),
        P(("blk", "turn")),
    )
    out_specs = P(None, ("blk", "turn"), "strip")

    return jax.shard_map(per_device, mesh=mesh, in_specs=in_specs, out_specs=out_specs, check_vma=False)
```

profile of v0, /device:TPU:0, one launch (start us, length us, event | category | flops | bytes accessed | tf_op | source)
XLA Modules:
  0.0 54.6 jit_solution(2637338264597508839)
XLA Ops:
  0.0 0.0 copy-start.4
  0.0 0.1 pad_add_fusion.1.ids
  0.1 0.0 copy-start.5
  0.1 0.9 %copy-done.5 = bf16[2,2,32768]{2,1,0:T(2,128)(2,1)S(1)} copy-done((bf16[2,2,32768]{2,1,0:T(2,128)(2,1)S(1)}, bf16[2,2,32768]{2,1,0:T(2,128)(2,1)}, u32[]{:S(2)}) %copy-start.5) | copy-done | bytes 262168
  1.0 0.0 copy-start.6
  1.0 0.0 copy-start.7
  1.0 0.8 %shard_map.66.refs_9_ = bf16[2,2,128,128]{3,2,1,0:T(8,128)(2,1)S(1)} custom-call(s32[3]{0:T(128)S(1)} %pad_add_fusion.1.ids, bf16[2,2,32768]{2,1,0:T(2,128)(2,1)S(1)} %copy-done.5), custom_call_target="tpu_custom_call" | custom-call | flops 1000000 | bytes 2000000 | tf_op jit(solution)/shard_map/pallas_call | solution.py:137
  1.8 0.6 %collective-permute-start.10 = (bf16[2,2,128,128]{3,2,1,0:T(8,128)(2,1)S(1)}, bf16[2,2,128,128]{3,2,1,0:T(8,128)(2,1)S(1)}, u32[]{:S(2)}, u32[]{:S(2)}) collective-permute-start(bf16[2,2,128,128]{3,2,1,0:T(8,128)(2,1)S(1)} %shard_map.66.refs_9_), channel_id=1, source_target_pairs={{0,8},{8,0},{16,24},{24,16},{1,9},{9,1},{17,25},{25,17},{2,10},{10... | collective-permute-start | bytes 393224 | tf_op jit(solution)/shard_map/ppermute | solution.py:315
  2.4 4.7 %collective-permute-start.9 = (bf16[2,2,128,128]{3,2,1,0:T(8,128)(2,1)S(1)}, bf16[2,2,128,128]{3,2,1,0:T(8,128)(2,1)S(1)}, u32[]{:S(2)}, u32[]{:S(2)}) collective-permute-start(bf16[2,2,128,128]{3,2,1,0:T(8,128)(2,1)S(1)} %shard_map.66.refs_9_), channel_id=1, source_target_pairs={{0,6},{2,4},{4,2},{6,0},{1,7},{3,5},{5,3},{7,1},{8,14},{10,12},{12... | collective-permute-start | bytes 393224 | tf_op jit(solution)/shard_map/ppermute | solution.py:315
  7.1 0.0 collective-permute-start.8
  7.1 0.6 %collective-permute-start.7 = (bf16[2,2,128,128]{3,2,1,0:T(8,128)(2,1)S(1)}, bf16[2,2,128,128]{3,2,1,0:T(8,128)(2,1)S(1)}, u32[]{:S(2)}, u32[]{:S(2)}) collective-permute-start(bf16[2,2,128,128]{3,2,1,0:T(8,128)(2,1)S(1)} %shard_map.66.refs_9_), channel_id=1, source_target_pairs={{0,2},{2,0},{4,6},{6,4},{1,3},{3,1},{5,7},{7,5},{8,10},{10,8},{12,... | collective-permute-start | bytes 393224 | tf_op jit(solution)/shard_map/ppermute | solution.py:315
  7.7 0.0 copy-start
  7.7 1.2 %copy-done = bf16[2,64,4096]{2,1,0:T(8,128)(2,1)S(1)} copy-done((bf16[2,64,4096]{2,1,0:T(8,128)(2,1)S(1)}, bf16[2,64,4096]{2,1,0:T(8,128)(2,1)}, u32[]{:S(2)}) %copy-start) | copy-done | bytes 1048600
  8.9 0.7 %shard_map.65 = (bf16[2,8,2,16,128]{4,3,2,1,0:T(8,128)(2,1)S(1)}, bf16[2,8,2,16,128]{4,3,2,1,0:T(8,128)(2,1)S(1)}) custom-call(s32[3]{0:T(128)S(1)} %pad_add_fusion.1.ids, bf16[2,64,4096]{2,1,0:T(8,128)(2,1)S(1)} %copy-done), custom_call_target="tpu_custom_call" | custom-call | flops 1000000 | bytes 4000000 | tf_op jit(solution)/shard_map/pallas_call | solution.py:86
  9.7 1.7 %collective-permute-start.3 = (bf16[2,8,2,16,128]{4,3,2,1,0:T(8,128)(2,1)S(1)}, bf16[2,8,2,16,128]{4,3,2,1,0:T(8,128)(2,1)S(1)}, u32[]{:S(2)}, u32[]{:S(2)}) collective-permute-start(bf16[2,8,2,16,128]{4,3,2,1,0:T(8,128)(2,1)S(1)} %get-tuple-element.13), channel_id=1, source_target_pairs={{0,16},{8,24},{16,0},{24,8},{1,17},{9,25},{17,1},{25,9},{2,18},{10... | collective-permute-start | bytes 393224 | tf_op jit(solution)/shard_map/ppermute | solution.py:315
  11.4 0.0 copy-start.1
  11.4 1.2 %copy-done.1 = bf16[2,64,4096]{2,1,0:T(8,128)(2,1)S(1)} copy-done((bf16[2,64,4096]{2,1,0:T(8,128)(2,1)S(1)}, bf16[2,64,4096]{2,1,0:T(8,128)(2,1)}, u32[]{:S(2)}) %copy-start.1) | copy-done | bytes 1048600
  12.6 1.1 %shard_map.64 = (bf16[2,16,2,16,128]{4,3,2,1,0:T(8,128)(2,1)S(1)}, bf16[2,16,2,16,128]{4,3,2,1,0:T(8,128)(2,1)S(1)}, bf16[2,8,2,16,128]{4,3,2,1,0:T(8,128)(2,1)S(1)}, bf16[2,8,2,16,128]{4,3,2,1,0:T(8,128)(2,1)S(1)}) custom-call(s32[3]{0:T(128)S(1)} %pad_add_fusion.1.ids, bf16[2,64,4096]{2,1,0:T(8,128)(2,1)S(1)} %copy-done.1), custom_call_target="tpu_custom_call" | custom-call | flops 1000000 | bytes 32000000 | tf_op jit(solution)/shard_map/pallas_call | solution.py:86
  13.7 0.0 copy-done.6
  13.7 0.0 collective-permute-done.10.refs_13_
  13.7 0.1 collective-permute-start.5
  13.8 0.0 collective-permute-done.9.refs_12_
  13.8 0.5 collective-permute-start.1
  14.3 0.2 sine_negate_fusion
  14.5 4.3 %collective-permute-done.8.refs_11_ = bf16[2,2,128,128]{3,2,1,0:T(8,128)(2,1)S(1)} collective-permute-done((bf16[2,2,128,128]{3,2,1,0:T(8,128)(2,1)S(1)}, bf16[2,2,128,128]{3,2,1,0:T(8,128)(2,1)S(1)}, u32[]{:S(2)}, u32[]{:S(2)}) %collective-permute-start.8) | collective-permute-done | bytes 131104 | tf_op jit(solution)/shard_map/ppermute | solution.py:315
  18.7 1.5 %collective-permute-start.14 = (bf16[2,8,2,16,128]{4,3,2,1,0:T(8,128)(2,1)S(1)}, bf16[2,8,2,16,128]{4,3,2,1,0:T(8,128)(2,1)S(1)}, u32[]{:S(2)}, u32[]{:S(2)}) collective-permute-start(bf16[2,8,2,16,128]{4,3,2,1,0:T(8,128)(2,1)S(1)} %get-tuple-element.15), channel_id=1, source_target_pairs={{0,16},{8,24},{16,0},{24,8},{1,17},{9,25},{17,1},{25,9},{2,18},{10... | collective-permute-start | bytes 393224 | tf_op jit(solution)/shard_map/ppermute | solution.py:315
  20.2 0.0 collective-permute-done.7.refs_10_
  20.2 0.0 collective-permute-start.16
  20.2 0.0 collective-permute-done.3.refs_5_
  20.3 0.6 %collective-permute-start.13 = (bf16[2,2,128,128]{3,2,1,0:T(8,128)(2,1)S(1)}, bf16[2,2,128,128]{3,2,1,0:T(8,128)(2,1)S(1)}, u32[]{:S(2)}, u32[]{:S(2)}) collective-permute-start(bf16[2,2,128,128]{3,2,1,0:T(8,128)(2,1)S(1)} %collective-permute-done.9.refs_12_), channel_id=1, source_target_pairs={{0,8},{8,0},{16,24},{24,16},{1,9},{9,1},{17,25},{25,17},{2,10},{10... | collective-permute-start | bytes 393224 | tf_op jit(solution)/shard_map/ppermute | solution.py:315
  20.9 0.0 collective-permute-done.5.refs_7_
  20.9 0.1 collective-permute-start.12
  20.9 0.1 sine_negate_fusion.1
  21.1 3.1 %collective-permute-done.14.refs_5_ = bf16[2,8,2,16,128]{4,3,2,1,0:T(8,128)(2,1)S(1)} collective-permute-done((bf16[2,8,2,16,128]{4,3,2,1,0:T(8,128)(2,1)S(1)}, bf16[2,8,2,16,128]{4,3,2,1,0:T(8,128)(2,1)S(1)}, u32[]{:S(2)}, u32[]{:S(2)}) %collective-permute-start.14) | collective-permute-done | bytes 131104 | tf_op jit(solution)/shard_map/ppermute | solution.py:315
  24.2 1.5 %collective-permute-start = (bf16[2,16,2,16,128]{4,3,2,1,0:T(8,128)(2,1)S(1)}, bf16[2,16,2,16,128]{4,3,2,1,0:T(8,128)(2,1)S(1)}, u32[]{:S(2)}, u32[]{:S(2)}) collective-permute-start(bf16[2,16,2,16,128]{4,3,2,1,0:T(8,128)(2,1)S(1)} %get-tuple-element.11.refs_1_), channel_id=1, source_target_pairs={{0,1},{1,0},{2,3},{3,2},{4,5},{5,4},{6,7},{7,6},{8,9},{9,8},{10,11... | collective-permute-start | bytes 786440 | tf_op jit(solution)/shard_map/ppermute | solution.py:315
  25.6 0.4 collective-permute-done.16.refs_7_
  26.0 0.3 collective-permute-start.11
  26.3 0.0 collective-permute-done.13.refs_16_
  26.3 1.5 %collective-permute-start.15 = (bf16[2,8,2,16,128]{4,3,2,1,0:T(8,128)(2,1)S(1)}, bf16[2,8,2,16,128]{4,3,2,1,0:T(8,128)(2,1)S(1)}, u32[]{:S(2)}, u32[]{:S(2)}) collective-permute-start(bf16[2,8,2,16,128]{4,3,2,1,0:T(8,128)(2,1)S(1)} %collective-permute-done.14.refs_5_), channel_id=1, source_target_pairs={{0,1},{1,0},{2,3},{3,2},{4,5},{5,4},{6,7},{7,6},{8,9},{9,8},{10,11... | collective-permute-start | bytes 393224 | tf_op jit(solution)/shard_map/ppermute | solution.py:315
  27.8 0.0 collective-permute-done.12.refs_15_
  27.8 0.5 collective-permute-start.17
  28.4 0.0 collective-permute-done.1.refs_3_
  28.4 1.5 %collective-permute-start.2 = (bf16[2,16,2,16,128]{4,3,2,1,0:T(8,128)(2,1)S(1)}, bf16[2,16,2,16,128]{4,3,2,1,0:T(8,128)(2,1)S(1)}, u32[]{:S(2)}, u32[]{:S(2)}) collective-permute-start(bf16[2,16,2,16,128]{4,3,2,1,0:T(8,128)(2,1)S(1)} %collective-permute-done.1.refs_3_), channel_id=1, source_target_pairs={{0,1},{1,0},{2,3},{3,2},{4,5},{5,4},{6,7},{7,6},{8,9},{9,8},{10,11... | collective-permute-start | bytes 786440 | tf_op jit(solution)/shard_map/ppermute | solution.py:315
  29.9 0.0 copy-done.7
  29.9 0.0 copy-done.4
  29.9 0.0 copy-start.2
  29.9 1.3 %copy-done.2 = bf16[2560,256]{1,0:T(8,128)(2,1)S(1)} copy-done((bf16[2560,256]{1,0:T(8,128)(2,1)S(1)}, bf16[2560,256]{1,0:T(8,128)(2,1)}, u32[]{:S(2)}) %copy-start.2) | copy-done | bytes 1310744
  31.2 0.0 copy-start.3
  31.2 0.8 %shard_map.67.refs_21_ = bf16[1024,256]{1,0:T(8,128)(2,1)S(1)} custom-call(s32[3]{0:T(128)S(1)} %pad_add_fusion.1.ids, bf16[2560,256]{1,0:T(8,128)(2,1)S(1)} %copy-done.2, f32[2,256,128]{2,1,0:T(8,128)S(1)} %copy-done.4), custom_call_target="tpu_custom_call" | custom-call | flops 1000000 | bytes 4000000 | tf_op jit(solution)/shard_map/pallas_call | solution.py:109
  32.0 0.1 pad_add_fusion.refs_0_
  32.1 0.0 collective-permute-done.11.refs_14_
  32.1 0.6 %collective-permute-start.4 = (bf16[2,8,2,16,128]{4,3,2,1,0:T(8,128)(2,1)S(1)}, bf16[2,8,2,16,128]{4,3,2,1,0:T(8,128)(2,1)S(1)}, u32[]{:S(2)}, u32[]{:S(2)}) collective-permute-start(bf16[2,8,2,16,128]{4,3,2,1,0:T(8,128)(2,1)S(1)} %collective-permute-done.3.refs_5_), channel_id=1, source_target_pairs={{0,1},{1,0},{2,3},{3,2},{4,5},{5,4},{6,7},{7,6},{8,9},{9,8},{10,11... | collective-permute-start | bytes 393224 | tf_op jit(solution)/shard_map/ppermute | solution.py:315
  32.7 2.2 %collective-permute-done.15.refs_6_ = bf16[2,8,2,16,128]{4,3,2,1,0:T(8,128)(2,1)S(1)} collective-permute-done((bf16[2,8,2,16,128]{4,3,2,1,0:T(8,128)(2,1)S(1)}, bf16[2,8,2,16,128]{4,3,2,1,0:T(8,128)(2,1)S(1)}, u32[]{:S(2)}, u32[]{:S(2)}) %collective-permute-start.15) | collective-permute-done | bytes 131104 | tf_op jit(solution)/shard_map/ppermute | solution.py:315
  34.9 1.5 %collective-permute-start.6 = (bf16[2,8,2,16,128]{4,3,2,1,0:T(8,128)(2,1)S(1)}, bf16[2,8,2,16,128]{4,3,2,1,0:T(8,128)(2,1)S(1)}, u32[]{:S(2)}, u32[]{:S(2)}) collective-permute-start(bf16[2,8,2,16,128]{4,3,2,1,0:T(8,128)(2,1)S(1)} %collective-permute-done.5.refs_7_), channel_id=1, source_target_pairs={{0,1},{1,0},{2,3},{3,2},{4,5},{5,4},{6,7},{7,6},{8,9},{9,8},{10,11... | collective-permute-start | bytes 393224 | tf_op jit(solution)/shard_map/ppermute | solution.py:315
  36.4 1.3 %collective-permute-done.17.refs_8_ = bf16[2,8,2,16,128]{4,3,2,1,0:T(8,128)(2,1)S(1)} collective-permute-done((bf16[2,8,2,16,128]{4,3,2,1,0:T(8,128)(2,1)S(1)}, bf16[2,8,2,16,128]{4,3,2,1,0:T(8,128)(2,1)S(1)}, u32[]{:S(2)}, u32[]{:S(2)}) %collective-permute-start.17) | collective-permute-done | bytes 131104 | tf_op jit(solution)/shard_map/ppermute | solution.py:315
  37.7 0.0 collective-permute-done.refs_2_
  37.7 5.6 %collective-permute-done.2.refs_4_ = bf16[2,16,2,16,128]{4,3,2,1,0:T(8,128)(2,1)S(1)} collective-permute-done((bf16[2,16,2,16,128]{4,3,2,1,0:T(8,128)(2,1)S(1)}, bf16[2,16,2,16,128]{4,3,2,1,0:T(8,128)(2,1)S(1)}, u32[]{:S(2)}, u32[]{:S(2)}) %collective-permute-start.2) | collective-permute-done | bytes 262176 | tf_op jit(solution)/shard_map/ppermute | solution.py:315
  43.3 0.0 copy-done.3
  43.3 5.6 %shard_map.68.refs_24_ = f32[2,2,1024,128]{3,2,1,0:T(8,128)} custom-call(s32[17]{0:T(128)S(1)} %pad_add_fusion.refs_0_, bf16[2,16,2,16,128]{4,3,2,1,0:T(8,128)(2,1)S(1)} %get-tuple-element.11.refs_1_, bf16[2,16,2,16,128]{4,3,2,1,0:T(8,128)(2,1)S(1)} %collective-permute-done.refs_2_, bf16[2,16,2,16,128]{4,3,2,1,0:T(8,128)(2,1)S(1)} %collective-permute-done.1.refs_3_, ...), custom_call_target="tpu_custom_call" | custom-call | flops 3000000000 | bytes 8000000 | tf_op jit(solution)/shard_map/pallas_call | solution.py:290
  48.9 0.0 collective-permute-done.4.refs_6_
  48.9 0.0 collective-permute-done.6.refs_8_
  49.0 5.6 %shard_map.69 = f32[2,2,1024,128]{3,2,1,0:T(8,128)} custom-call(s32[17]{0:T(128)S(1)} %pad_add_fusion.refs_0_, bf16[2,16,2,16,128]{4,3,2,1,0:T(8,128)(2,1)S(1)} %get-tuple-element.11.refs_1_, bf16[2,16,2,16,128]{4,3,2,1,0:T(8,128)(2,1)S(1)} %collective-permute-done.refs_2_, ...), custom_call_target="tpu_custom_call", output_to_operand_aliasing={{}: (24, {})} | custom-call | flops 3000000000 | bytes 8000000 | tf_op jit(solution)/shard_map/pallas_call | solution.py:290
  (3 shorter events, 0.0 us)
Async XLA Ops:
  0.0 29.9 %copy-start.4 = (f32[2,256,128]{2,1,0:T(8,128)S(1)}, f32[2,256,128]{2,1,0:T(8,128)}, u32[]{:S(2)}) copy-start(f32[2,256,128]{2,1,0:T(8,128)} %constant.98.clone.twist.refs_23_) | copy-start | bytes 786436
  0.1 1.0 %copy-start.5 = (bf16[2,2,32768]{2,1,0:T(2,128)(2,1)S(1)}, bf16[2,2,32768]{2,1,0:T(2,128)(2,1)}, u32[]{:S(2)}) copy-start(bf16[2,2,32768]{2,1,0:T(2,128)(2,1)} %filters.1) | copy-start | bytes 786436
  1.0 12.7 %copy-start.6 = (s32[16]{0:T(128)S(1)}, s32[16]{0:T(128)}, u32[]{:S(2)}) copy-start(s32[16]{0:T(128)} %param.9) | copy-start | bytes 196
  1.0 28.8 %copy-start.7 = (s32[16]{0:T(128)S(1)}, s32[16]{0:T(128)}, u32[]{:S(2)}) copy-start(s32[16]{0:T(128)} %param.8) | copy-start | bytes 196
  1.8 11.9 %collective-permute-start.10 = (bf16[2,2,128,128]{3,2,1,0:T(8,128)(2,1)S(1)}, bf16[2,2,128,128]{3,2,1,0:T(8,128)(2,1)S(1)}, u32[]{:S(2)}, u32[]{:S(2)}) collective-permute-start(bf16[2,2,128,128]{3,2,1,0:T(8,128)(2,1)S(1)} %shard_map.66.refs_9_), channel_id=1, source_target_pairs={{0,8},{8,0},{16,24},{24,16},{1,9},{9,1},{17,25},{25,17},{2,10},{10... | collective-permute-start | bytes 393224 | tf_op jit(solution)/shard_map/ppermute | solution.py:315
  2.4 11.4 %collective-permute-start.9 = (bf16[2,2,128,128]{3,2,1,0:T(8,128)(2,1)S(1)}, bf16[2,2,128,128]{3,2,1,0:T(8,128)(2,1)S(1)}, u32[]{:S(2)}, u32[]{:S(2)}) collective-permute-start(bf16[2,2,128,128]{3,2,1,0:T(8,128)(2,1)S(1)} %shard_map.66.refs_9_), channel_id=1, source_target_pairs={{0,6},{2,4},{4,2},{6,0},{1,7},{3,5},{5,3},{7,1},{8,14},{10,12},{12... | collective-permute-start | bytes 393224 | tf_op jit(solution)/shard_map/ppermute | solution.py:315
  7.1 11.7 %collective-permute-start.8 = (bf16[2,2,128,128]{3,2,1,0:T(8,128)(2,1)S(1)}, bf16[2,2,128,128]{3,2,1,0:T(8,128)(2,1)S(1)}, u32[]{:S(2)}, u32[]{:S(2)}) collective-permute-start(bf16[2,2,128,128]{3,2,1,0:T(8,128)(2,1)S(1)} %shard_map.66.refs_9_), channel_id=1, source_target_pairs={{0,4},{2,6},{4,0},{6,2},{1,5},{3,7},{5,1},{7,3},{8,12},{10,14},{12... | collective-permute-start | bytes 393224 | tf_op jit(solution)/shard_map/ppermute | solution.py:315
  7.1 13.2 %collective-permute-start.7 = (bf16[2,2,128,128]{3,2,1,0:T(8,128)(2,1)S(1)}, bf16[2,2,128,128]{3,2,1,0:T(8,128)(2,1)S(1)}, u32[]{:S(2)}, u32[]{:S(2)}) collective-permute-start(bf16[2,2,128,128]{3,2,1,0:T(8,128)(2,1)S(1)} %shard_map.66.refs_9_), channel_id=1, source_target_pairs={{0,2},{2,0},{4,6},{6,4},{1,3},{3,1},{5,7},{7,5},{8,10},{10,8},{12,... | collective-permute-start | bytes 393224 | tf_op jit(solution)/shard_map/ppermute | solution.py:315
  7.7 1.2 %copy-start = (bf16[2,64,4096]{2,1,0:T(8,128)(2,1)S(1)}, bf16[2,64,4096]{2,1,0:T(8,128)(2,1)}, u32[]{:S(2)}) copy-start(bf16[2,64,4096]{2,1,0:T(8,128)(2,1)} %echoes.3) | copy-start | bytes 3145732
  9.7 10.6 %collective-permute-start.3 = (bf16[2,8,2,16,128]{4,3,2,1,0:T(8,128)(2,1)S(1)}, bf16[2,8,2,16,128]{4,3,2,1,0:T(8,128)(2,1)S(1)}, u32[]{:S(2)}, u32[]{:S(2)}) collective-permute-start(bf16[2,8,2,16,128]{4,3,2,1,0:T(8,128)(2,1)S(1)} %get-tuple-element.13), channel_id=1, source_target_pairs={{0,16},{8,24},{16,0},{24,8},{1,17},{9,25},{17,1},{25,9},{2,18},{10... | collective-permute-start | bytes 393224 | tf_op jit(solution)/shard_map/ppermute | solution.py:315
  11.4 1.2 %copy-start.1 = (bf16[2,64,4096]{2,1,0:T(8,128)(2,1)S(1)}, bf16[2,64,4096]{2,1,0:T(8,128)(2,1)}, u32[]{:S(2)}) copy-start(bf16[2,64,4096]{2,1,0:T(8,128)(2,1)} %echoes.3) | copy-start | bytes 3145732
  13.7 7.1 %collective-permute-start.5 = (bf16[2,8,2,16,128]{4,3,2,1,0:T(8,128)(2,1)S(1)}, bf16[2,8,2,16,128]{4,3,2,1,0:T(8,128)(2,1)S(1)}, u32[]{:S(2)}, u32[]{:S(2)}) collective-permute-start(bf16[2,8,2,16,128]{4,3,2,1,0:T(8,128)(2,1)S(1)} %get-tuple-element.14), channel_id=1, source_target_pairs={{0,24},{8,16},{16,8},{24,0},{1,25},{9,17},{17,9},{25,1},{2,26},{10... | collective-permute-start | bytes 393224 | tf_op jit(solution)/shard_map/ppermute | solution.py:315
  13.8 14.5 %collective-permute-start.1 = (bf16[2,16,2,16,128]{4,3,2,1,0:T(8,128)(2,1)S(1)}, bf16[2,16,2,16,128]{4,3,2,1,0:T(8,128)(2,1)S(1)}, u32[]{:S(2)}, u32[]{:S(2)}) collective-permute-start(bf16[2,16,2,16,128]{4,3,2,1,0:T(8,128)(2,1)S(1)} %get-tuple-element.12), channel_id=1, source_target_pairs={{0,8},{8,0},{16,24},{24,16},{1,9},{9,1},{17,25},{25,17},{2,10},{10... | collective-permute-start | bytes 786440 | tf_op jit(solution)/shard_map/ppermute | solution.py:315
  18.7 5.4 %collective-permute-start.14 = (bf16[2,8,2,16,128]{4,3,2,1,0:T(8,128)(2,1)S(1)}, bf16[2,8,2,16,128]{4,3,2,1,0:T(8,128)(2,1)S(1)}, u32[]{:S(2)}, u32[]{:S(2)}) collective-permute-start(bf16[2,8,2,16,128]{4,3,2,1,0:T(8,128)(2,1)S(1)} %get-tuple-element.15), channel_id=1, source_target_pairs={{0,16},{8,24},{16,0},{24,8},{1,17},{9,25},{17,1},{25,9},{2,18},{10... | collective-permute-start | bytes 393224 | tf_op jit(solution)/shard_map/ppermute | solution.py:315
  20.2 5.8 %collective-permute-start.16 = (bf16[2,8,2,16,128]{4,3,2,1,0:T(8,128)(2,1)S(1)}, bf16[2,8,2,16,128]{4,3,2,1,0:T(8,128)(2,1)S(1)}, u32[]{:S(2)}, u32[]{:S(2)}) collective-permute-start(bf16[2,8,2,16,128]{4,3,2,1,0:T(8,128)(2,1)S(1)} %get-tuple-element.16), channel_id=1, source_target_pairs={{0,24},{8,16},{16,8},{24,0},{1,25},{9,17},{17,9},{25,1},{2,26},{10... | collective-permute-start | bytes 393224 | tf_op jit(solution)/shard_map/ppermute | solution.py:315
  20.3 6.1 %collective-permute-start.13 = (bf16[2,2,128,128]{3,2,1,0:T(8,128)(2,1)S(1)}, bf16[2,2,128,128]{3,2,1,0:T(8,128)(2,1)S(1)}, u32[]{:S(2)}, u32[]{:S(2)}) collective-permute-start(bf16[2,2,128,128]{3,2,1,0:T(8,128)(2,1)S(1)} %collective-permute-done.9.refs_12_), channel_id=1, source_target_pairs={{0,8},{8,0},{16,24},{24,16},{1,9},{9,1},{17,25},{25,17},{2,10},{10... | collective-permute-start | bytes 393224 | tf_op jit(solution)/shard_map/ppermute | solution.py:315
  20.9 6.9 %collective-permute-start.12 = (bf16[2,2,128,128]{3,2,1,0:T(8,128)(2,1)S(1)}, bf16[2,2,128,128]{3,2,1,0:T(8,128)(2,1)S(1)}, u32[]{:S(2)}, u32[]{:S(2)}) collective-permute-start(bf16[2,2,128,128]{3,2,1,0:T(8,128)(2,1)S(1)} %collective-permute-done.8.refs_11_), channel_id=1, source_target_pairs={{0,8},{8,0},{16,24},{24,16},{1,9},{9,1},{17,25},{25,17},{2,10},{10... | collective-permute-start | bytes 393224 | tf_op jit(solution)/shard_map/ppermute | solution.py:315
  24.2 13.6 %collective-permute-start = (bf16[2,16,2,16,128]{4,3,2,1,0:T(8,128)(2,1)S(1)}, bf16[2,16,2,16,128]{4,3,2,1,0:T(8,128)(2,1)S(1)}, u32[]{:S(2)}, u32[]{:S(2)}) collective-permute-start(bf16[2,16,2,16,128]{4,3,2,1,0:T(8,128)(2,1)S(1)} %get-tuple-element.11.refs_1_), channel_id=1, source_target_pairs={{0,1},{1,0},{2,3},{3,2},{4,5},{5,4},{6,7},{7,6},{8,9},{9,8},{10,11... | collective-permute-start | bytes 786440 | tf_op jit(solution)/shard_map/ppermute | solution.py:315
  26.0 6.1 %collective-permute-start.11 = (bf16[2,2,128,128]{3,2,1,0:T(8,128)(2,1)S(1)}, bf16[2,2,128,128]{3,2,1,0:T(8,128)(2,1)S(1)}, u32[]{:S(2)}, u32[]{:S(2)}) collective-permute-start(bf16[2,2,128,128]{3,2,1,0:T(8,128)(2,1)S(1)} %collective-permute-done.7.refs_10_), channel_id=1, source_target_pairs={{0,8},{8,0},{16,24},{24,16},{1,9},{9,1},{17,25},{25,17},{2,10},{10... | collective-permute-start | bytes 393224 | tf_op jit(solution)/shard_map/ppermute | solution.py:315
  26.3 8.6 %collective-permute-start.15 = (bf16[2,8,2,16,128]{4,3,2,1,0:T(8,128)(2,1)S(1)}, bf16[2,8,2,16,128]{4,3,2,1,0:T(8,128)(2,1)S(1)}, u32[]{:S(2)}, u32[]{:S(2)}) collective-permute-start(bf16[2,8,2,16,128]{4,3,2,1,0:T(8,128)(2,1)S(1)} %collective-permute-done.14.refs_5_), channel_id=1, source_target_pairs={{0,1},{1,0},{2,3},{3,2},{4,5},{5,4},{6,7},{7,6},{8,9},{9,8},{10,11... | collective-permute-start | bytes 393224 | tf_op jit(solution)/shard_map/ppermute | solution.py:315
  27.8 9.9 %collective-permute-start.17 = (bf16[2,8,2,16,128]{4,3,2,1,0:T(8,128)(2,1)S(1)}, bf16[2,8,2,16,128]{4,3,2,1,0:T(8,128)(2,1)S(1)}, u32[]{:S(2)}, u32[]{:S(2)}) collective-permute-start(bf16[2,8,2,16,128]{4,3,2,1,0:T(8,128)(2,1)S(1)} %collective-permute-done.16.refs_7_), channel_id=1, source_target_pairs={{0,1},{1,0},{2,3},{3,2},{4,5},{5,4},{6,7},{7,6},{8,9},{9,8},{10,11... | collective-permute-start | bytes 393224 | tf_op jit(solution)/shard_map/ppermute | solution.py:315
  28.4 15.0 %collective-permute-start.2 = (bf16[2,16,2,16,128]{4,3,2,1,0:T(8,128)(2,1)S(1)}, bf16[2,16,2,16,128]{4,3,2,1,0:T(8,128)(2,1)S(1)}, u32[]{:S(2)}, u32[]{:S(2)}) collective-permute-start(bf16[2,16,2,16,128]{4,3,2,1,0:T(8,128)(2,1)S(1)} %collective-permute-done.1.refs_3_), channel_id=1, source_target_pairs={{0,1},{1,0},{2,3},{3,2},{4,5},{5,4},{6,7},{7,6},{8,9},{9,8},{10,11... | collective-permute-start | bytes 786440 | tf_op jit(solution)/shard_map/ppermute | solution.py:315
  29.9 1.3 %copy-start.2 = (bf16[2560,256]{1,0:T(8,128)(2,1)S(1)}, bf16[2560,256]{1,0:T(8,128)(2,1)}, u32[]{:S(2)}) copy-start(bf16[2560,256]{1,0:T(8,128)(2,1)} %constant.97.clone.dots.refs_22_) | copy-start | bytes 3932164
  31.2 12.1 %copy-start.3 = (bf16[2560,256]{1,0:T(8,128)(2,1)S(1)}, bf16[2560,256]{1,0:T(8,128)(2,1)}, u32[]{:S(2)}) copy-start(bf16[2560,256]{1,0:T(8,128)(2,1)} %constant.97.clone.dots.refs_22_) | copy-start | bytes 3932164
  32.1 16.8 %collective-permute-start.4 = (bf16[2,8,2,16,128]{4,3,2,1,0:T(8,128)(2,1)S(1)}, bf16[2,8,2,16,128]{4,3,2,1,0:T(8,128)(2,1)S(1)}, u32[]{:S(2)}, u32[]{:S(2)}) collective-permute-start(bf16[2,8,2,16,128]{4,3,2,1,0:T(8,128)(2,1)S(1)} %collective-permute-done.3.refs_5_), channel_id=1, source_target_pairs={{0,1},{1,0},{2,3},{3,2},{4,5},{5,4},{6,7},{7,6},{8,9},{9,8},{10,11... | collective-permute-start | bytes 393224 | tf_op jit(solution)/shard_map/ppermute | solution.py:315
  34.9 14.0 %collective-permute-start.6 = (bf16[2,8,2,16,128]{4,3,2,1,0:T(8,128)(2,1)S(1)}, bf16[2,8,2,16,128]{4,3,2,1,0:T(8,128)(2,1)S(1)}, u32[]{:S(2)}, u32[]{:S(2)}) collective-permute-start(bf16[2,8,2,16,128]{4,3,2,1,0:T(8,128)(2,1)S(1)} %collective-permute-done.5.refs_7_), channel_id=1, source_target_pairs={{0,1},{1,0},{2,3},{3,2},{4,5},{5,4},{6,7},{7,6},{8,9},{9,8},{10,11... | collective-permute-start | bytes 393224 | tf_op jit(solution)/shard_map/ppermute | solution.py:315
where the time goes:
time: 55.2 us; the launch traced here: 54.6 us
  starting transfers between devices  17.7 us (32%)
  waiting for transfers between devices  16.9 us (31%)
  Pallas kernels  14.7 us (27%)
  local copies, waits for them, and re-layouts  4.73 us (9%)
    ppermute x18, starting transfers between devices, swap(): return lax.ppermute(value, axis, [(a, a ^ flip) for a in range(size)])  17.7 us
    ppermute x18, waiting for transfers between devices, swap(): return lax.ppermute(value, axis, [(a, a ^ flip) for a in range(size)])  16.9 us
    pallas_call x2, Pallas kernels, focus(): pl.pallas_call(functools.partial(focus_kernel, tuple(bases), pieces, rows...  11.2 us
    unnamed x16, local copies, waits for them, and re-layouts  4.73 us
    pallas_call x2, Pallas kernels, pack(): pl.pallas_call(functools.partial(pack_kernel, tuple(jobs), total, part),...  1.82 us
  transfers between devices with their start and end apart: 18, of which 6 were waited for; matrix products, arithmetic and copies ran while one was open for 1% of the time, Pallas kernels for 15%

commit v1 on v0

--- a/solution.py
+++ b/solution.py
@@ -60,8 +60,8 @@
     return jnp.dot(a, b, preferred_element_type=jnp.float32)
 
 
-def pack_kernel(jobs, total, part, ids, echoes, *refs):
-    turn, outs, spread = ids[0], refs[:-1], refs[-1]
+def pack_kernel(jobs, total, part, echoes, *refs):
+    turn, outs, spread = lax.axis_index("turn"), refs[:-1], refs[-1]
     for k, (flip, row0, rows) in enumerate(jobs):
         for row in range(0, rows, 8):
             start = pl.multiple_of((turn ^ flip) * total + row0 + row, 8)
@@ -78,46 +78,45 @@
                     outs[k][p, row, e] = picked.astype(jnp.bfloat16)
 
 
-def pack(ids, echoes, jobs, total, cost):
+def pack(echoes, jobs, total, cost):
     part = echoes.shape[2] // LANES
     vm = pl.BlockSpec(memory_space=pltpu.VMEM)
-    sm = pl.BlockSpec(memory_space=pltpu.SMEM)
     tiles = max(rows for _, _, rows in jobs) // 8
     return pl.pallas_call(
         functools.partial(pack_kernel, tuple(jobs), total, part),
-        in_specs=[sm, vm],
+        in_specs=[vm],
         out_specs=[vm] * len(jobs),
         out_shape=[jax.ShapeDtypeStruct((2, rows, 2, part // 2, LANES), jnp.bfloat16) for _, _, rows in jobs],
         scratch_shapes=[pltpu.VMEM((len(jobs), tiles, 2, part * 8, LANES), jnp.float32)],
         compiler_params=pltpu.CompilerParams(vmem_limit_bytes=12 * 1024 * 1024),
         cost_estimate=pl.CostEstimate(flops=10**6, bytes_accessed=cost, transcendentals=0),
-    )(ids, echoes)
-
-
-def order_kernel(width, ids, dots, twist, out):
+    )(echoes)
+
+
+def order_kernel(width, strips, dots, twist, out):
+    me = lax.axis_index("turn") * strips + lax.axis_index("strip")
     size = dots.shape[1]
     row_ids = lax.broadcasted_iota(jnp.int32, (size, size), 0)
     col_ids = lax.broadcasted_iota(jnp.int32, (size, size), 1)
-    order = jnp.where(row_ids == (col_ids ^ (ids[2] * width)), 1.0, 0.0).astype(jnp.bfloat16)
+    order = jnp.where(row_ids == (col_ids ^ (me * width)), 1.0, 0.0).astype(jnp.bfloat16)
     out[...] = dot(dots[: 4 * size], order).astype(jnp.bfloat16)
 
 
-def order_tables(ids, dots, twist, width):
+def order_tables(dots, twist, width, strips):
     vm = pl.BlockSpec(memory_space=pltpu.VMEM)
-    sm = pl.BlockSpec(memory_space=pltpu.SMEM)
     size = dots.shape[1]
     return pl.pallas_call(
-        functools.partial(order_kernel, width),
-        in_specs=[sm, vm, vm],
+        functools.partial(order_kernel, width, strips),
+        in_specs=[vm, vm],
         out_specs=vm,
         out_shape=jax.ShapeDtypeStruct((4 * size, size), jnp.bfloat16),
         compiler_params=pltpu.CompilerParams(vmem_limit_bytes=8 * 1024 * 1024),
         cost_estimate=pl.CostEstimate(flops=10**6, bytes_accessed=4 * 10**6, transcendentals=0),
-    )(ids, dots, twist)
-
-
-def turn_kernel(ids, filters, out, turned):
-    core = ids[1]
+    )(dots, twist)
+
+
+def turn_kernel(filters, out, turned):
+    core = lax.axis_index("turn") % 2
     slabs = filters.shape[1]
     for p in range(2):
         for d in range(LANES):
@@ -130,32 +129,41 @@
             out[slab, p] = turned[slab, p].T.astype(jnp.bfloat16)
 
 
-def turn_filters(ids, filters):
+def turn_filters(filters):
     vm = pl.BlockSpec(memory_space=pltpu.VMEM)
-    sm = pl.BlockSpec(memory_space=pltpu.SMEM)
     shape = (filters.shape[1], 2, LANES, LANES)
     return pl.pallas_call(
         turn_kernel,
-        in_specs=[sm, vm],
+        in_specs=[vm],
         out_specs=vm,
         out_shape=jax.ShapeDtypeStruct(shape, jnp.bfloat16),
         scratch_shapes=[pltpu.VMEM(shape, jnp.float32)],
         compiler_params=pltpu.CompilerParams(vmem_limit_bytes=4 * 1024 * 1024),
-        cost_estimate=pl.CostEstimate(flops=10**6, bytes_accessed=2 * 10**6, transcendentals=0),
-    )(ids, filters)
-
-
-def focus_kernel(bases, pieces, rows, row0, slow, out_slow, *refs):
+        cost_estimate=pl.CostEstimate(flops=10**6, bytes_accessed=16 * 10**6, transcendentals=0),
+    )(filters)
+
+
+def focus_kernel(bases, pieces, earlier, rows, row0, slow, out_slow, *refs):
     sources = len(bases)
-    scalars = refs[0]
-    blocks = refs[1 : 1 + sources]
+    slabs, blocks = refs[0], refs[1 : 1 + sources]
     own = refs[1 + sources : 1 + sources + pieces]
     other = refs[1 + sources + pieces : 1 + sources + 2 * pieces]
-    (
-        slow_cos, slow_sin, fast_cos, fast_sin, first_dots_ref, dots, twist, _, out,
-        s1, y1, s2, y2, s3, y3, s4, slow_ramp, filt,
-    ) = refs[1 + sources + 2 * pieces :]
-    core = scalars[0]
+    slow_cos, slow_sin, fast_cos, fast_sin, first_dots_ref, dots, twist = refs[1 + sources + 2 * pieces :][:7]
+    rest = refs[8 + sources + 2 * pieces :]
+    images, out = rest[:earlier], rest[earlier]
+    s1, y1, s2, y2, s3, y3, s4, slow_ramp, filt, slab_ids, slab_sem = rest[earlier + 1 :][:11]
+    fetch = pltpu.make_async_copy(slabs, slab_ids, slab_sem)
+    fetch.start()
+    tile = out
+    writes = []
+    if earlier:
+        tile, write_sem = rest[earlier + 12 :]
+        for k, source in enumerate((*images, tile)):
+            for p in range(2):
+                writes.append(pltpu.make_async_copy(source.at[p], out.at[p, k], write_sem.at[2 * k + p]))
+        for write in writes[:-2]:
+            write.start()
+    core = lax.axis_index("turn") % 2
     per_zone = own[0].shape[0]
     for k in range(pieces):
         filt[core, k * per_zone : (k + 1) * per_zone] = own[k][...]
@@ -206,7 +214,7 @@
     def respond(pair):
         for i in range(2):
             r = row0 + 2 * pair + i
-            slab = scalars[1 + r]
+            slab = slab_ids[r]
             v_re, v_im = fast_cos[r : r + 1], fast_sin[r : r + 1]
             for part in range(2):
                 rows_s = slice(i * slow + part * half, i * slow + (part + 1) * half)
@@ -250,7 +258,7 @@
             for e in range(2):
                 for p in range(2):
                     for q in range(0, count, 8):
-                        out[p, 0, pl.ds((2 * q + e) * 8 + r, 8, stride=16), :] = s4[
+                        tile[p, pl.ds((2 * q + e) * 8 + r, 8, stride=16), :] = s4[
                             pair, e, p * count + q : p * count + q + 8, i * LANES : (i + 1) * LANES
                         ]
 
@@ -265,34 +273,33 @@
         store,
     ]
     streams = [[(step, pair) for pair in range(k, rows // 2, 2) for step in range(8)] for k in range(2)]
+    fetch.wait()
     for t in range(len(streams[0]) + 1):
         now = [s[t - k] for k, s in enumerate(streams) if 0 <= t - k < len(s)]
         for step, pair in sorted(now, key=lambda job: job[0] % 2):
             steps[step](pair)
-
-
-def focus(blocks, bases, own, other, ramps, first, t, scalars, held, rows, row0, total, slow, out_slow):
+    for write in writes[-2:]:
+        write.start()
+    for write in writes:
+        write.wait()
+
+
+def focus(blocks, bases, own, other, ramps, first, t, slabs, images, rows, row0, total, slow, out_slow, final):
     slots, pieces = rows // 2, len(own)
-    hbm = pl.BlockSpec(memory_space=pltpu.HBM)
-    sm = pl.BlockSpec(memory_space=pltpu.SMEM)
-    tile = row0 // 8
-    whole = pl.BlockSpec((2, 1, out_slow * 8, LANES), lambda i: (0, tile, 0, 0))
 
     def full(a):
         return pl.BlockSpec(a.shape, lambda i: (0,) * a.ndim)
 
-    operands = [*own, *other, *ramps, first, *t]
-    aliases = {}
-    if held is None:
-        held = jnp.zeros((8, LANES), jnp.float32)
-    else:
-        aliases = {1 + len(blocks) + len(operands): 0}
+    image = (2, out_slow * 8, LANES)
+    shape = (2, total // 8, *image[1:]) if final else image
+    operands = [slabs, *blocks, *own, *other, *ramps, first, *t, *images]
+    extra = [pltpu.VMEM(image, jnp.float32), pltpu.SemaphoreType.DMA((total // 4,))] if final else []
     return pl.pallas_call(
-        functools.partial(focus_kernel, tuple(bases), pieces, rows, row0, slow, out_slow),
+        functools.partial(focus_kernel, tuple(bases), pieces, len(images), rows, row0, slow, out_slow),
         grid=(1,),
-        in_specs=[sm] + [full(a) for a in blocks + operands] + [hbm],
-        out_specs=whole,
-        out_shape=jax.ShapeDtypeStruct((2, total // 8, out_slow * 8, LANES), jnp.float32),
+        in_specs=[full(a) for a in operands],
+        out_specs=pl.BlockSpec(memory_space=pl.ANY) if final else pl.BlockSpec(image, lambda i: (0, 0, 0)),
+        out_shape=jax.ShapeDtypeStruct(shape, jnp.float32),
         scratch_shapes=[
             pltpu.VMEM((slots, 2, slow, 2 * LANES), jnp.float32),
             pltpu.VMEM((slots, 2, slow, 4 * LANES), jnp.bfloat16),
@@ -303,11 +310,13 @@
             pltpu.VMEM((slots, 2, out_slow, 2 * LANES), jnp.float32),
             pltpu.VMEM((2, slow, total), jnp.float32),
             pltpu.VMEM((2, pieces * own[0].shape[0], *own[0].shape[1:]), jnp.bfloat16),
+            pltpu.SMEM(slabs.shape, jnp.int32),
+            pltpu.SemaphoreType.DMA,
+            *extra,
         ],
-        input_output_aliases=aliases,
-        compiler_params=pltpu.CompilerParams(vmem_limit_bytes=24 * 1024 * 1024),
+        compiler_params=pltpu.CompilerParams(vmem_limit_bytes=28 * 1024 * 1024),
         cost_estimate=pl.CostEstimate(flops=3 * 10**9, bytes_accessed=8 * 10**6, transcendentals=0),
-    )(scalars, *blocks, *operands, held)
+    )(*operands)
 
 
 def swap(value, axis, flip):
@@ -317,7 +326,7 @@
 
 def per_device(echoes, filters, slab_index, shifts):
     turns, strips, zones = lax.axis_size("turn"), lax.axis_size("strip"), lax.axis_size("blk")
-    turn, strip, zone = lax.axis_index("turn"), lax.axis_index("strip"), lax.axis_index("blk")
+    strip, zone = lax.axis_index("strip"), lax.axis_index("blk")
     sources = turns * strips
     length = echoes.shape[2] * sources
     slow = length // LANES
@@ -325,19 +334,18 @@
     out_slow = slow // strips
     per_zone = filters.shape[1]
     width = slow // sources
-    me = turn * strips + strip
-    core = turn % 2
-    ids = jnp.stack([turn, core, me]).astype(jnp.int32)
+    behind = (strips - strip) * (length // strips)
+    echoes, zone, behind = lax.optimization_barrier((echoes, zone, behind))
     t = [jnp.asarray(a) for a in tables(length, sources, length // strips)]
 
     jobs = [[(0, 0, total), (1, 0, total)], []]
     starts = [sum(CHUNKS[:k]) for k in range(len(CHUNKS))]
     for k, rows in enumerate(CHUNKS):
         jobs[min(k, 1)] += [(flip, starts[k], rows) for flip in range(2, turns)]
-    sent = pack(ids, echoes, jobs[0], total, 32 * 10**6)
-    more = pack(ids, echoes, jobs[1], total, 4 * 10**6)
-    half = turn_filters(ids, filters)
-    first = order_tables(ids, *t, width)
+    sent = pack(echoes, jobs[0], total, 32 * 10**6)
+    more = pack(echoes, jobs[1], total, 4 * 10**6)
+    half = turn_filters(filters)
+    first = order_tables(*t, width, strips)
     held = {}
     for (flip, start, rows), block in zip(jobs[0] + jobs[1], [*sent, *more]):
         if flip:
@@ -351,21 +359,24 @@
     local_slab = (slab_index // per_zone ^ zone) * per_zone + slab_index % per_zone
 
     c = jnp.arange(slow, dtype=jnp.int32)[None, :]
-    offset = (shifts + (strips - strip) * (length // strips)) % length
-    c_angle = (offset[:, None] * c % length).astype(jnp.float32) * (2.0 * math.pi / length)
+    offset = (shifts + behind) & (length - 1)
+    c_angle = (offset[:, None] * c & (length - 1)).astype(jnp.float32) * (2.0 * math.pi / length)
     d = jnp.arange(LANES, dtype=jnp.int32)[None, :]
-    d_angle = (d * (shifts[:, None] % LANES) % LANES).astype(jnp.float32) * (2.0 * math.pi / LANES)
+    d_angle = (d * shifts[:, None] & (LANES - 1)).astype(jnp.float32) * (2.0 * math.pi / LANES)
     ramps = (jnp.cos(c_angle), -jnp.sin(c_angle), jnp.cos(d_angle), -jnp.sin(d_angle))
-    scalars = jnp.concatenate([core[None].astype(jnp.int32), local_slab])
-
-    image = None
-    for start, rows in zip(starts, CHUNKS):
+
+    images = []
+    for k, (start, rows) in enumerate(zip(starts, CHUNKS)):
         blocks, bases = [], []
         for slot in range(sources):
             whole = slot // strips < 2
             blocks.append(held[slot, 0 if whole else start])
             bases.append(start if whole else 0)
-        image = focus(blocks, bases, own, other, ramps, first, t, scalars, image, rows, start, total, slow, out_slow)
+        final = k == len(CHUNKS) - 1
+        image = focus(
+            blocks, bases, own, other, ramps, first, t, local_slab, images, rows, start, total, slow, out_slow, final
+        )
+        images.append(image)
     image = image.reshape(2, total // 8, out_slow, 8, LANES).transpose(0, 1, 3, 2, 4)
     return image.reshape(2, total, out_slow * LANES)
 

time: 55.2 us -> 51.3 us (0.929)
  Pallas kernels: 14.7 us -> 11.4 us
  local copies, waits for them, and re-layouts: 4.73 us -> 2.19 us
  waiting for transfers between devices: 16.9 us -> 18.3 us
    unnamed x16 -> x12, local copies, waits for them, and re-layouts: 4.73 us -> 2.19 us
    pallas_call x4, Pallas kernels: 12.8 us -> 10.6 us  [the longest x2 10.1 us: focus(): pl.pallas_call(functools.partial(focus_kernel, tuple(bases), pieces, len(...]
    ppermute x18, waiting for transfers between devices: 16.9 us -> 18.3 us  [swap(): return lax.ppermute(value, axis, [(a, a ^ flip) for a in range(size)])]
    pallas_call x2, Pallas kernels: 1.82 us -> 0.73 us  [pack(): pl.pallas_call(functools.partial(pack_kernel, tuple(jobs), total, part),...]
    and x0 -> x1, other arithmetic: none -> 0.66 us  [per_device(): offset = shifts + behind & length - 1]
  transfers between devices with their start and end apart: 18 -> 18, of which waited for: 6 -> 6; matrix products, arithmetic and copies ran while one was open for 1% -> 2% of each run, Pallas kernels for 15% -> 11%
where the time goes in v1:
time: 51.3 us; the launch traced here: 51.1 us
  waiting for transfers between devices  18.3 us (36%)
  starting transfers between devices  18.2 us (35%)
  Pallas kernels  11.4 us (22%)
  local copies, waits for them, and re-layouts  2.19 us (4%)
  other arithmetic  0.94 us (2%)
    ppermute x18, waiting for transfers between devices, swap(): return lax.ppermute(value, axis, [(a, a ^ flip) for a in range(size)])  18.3 us
    ppermute x18, starting transfers between devices, swap(): return lax.ppermute(value, axis, [(a, a ^ flip) for a in range(size)])  18.2 us
    pallas_call x2, Pallas kernels, focus(): pl.pallas_call(functools.partial(focus_kernel, tuple(bases), pieces, len(...  10.1 us
    unnamed x12, local copies, waits for them, and re-layouts  2.19 us
  transfers between devices with their start and end apart: 18, of which 6 were waited for; matrix products, arithmetic and copies ran while one was open for 2% of the time, Pallas kernels for 11%

profile of v1, /device:TPU:0, one launch (start us, length us, event | category | flops | bytes accessed | tf_op | source)
XLA Modules:
  0.0 51.1 jit_solution(14329239773734489856)
XLA Ops:
  0.0 0.0 copy-start.2
  0.0 0.9 %copy-done.2 = bf16[2,2,32768]{2,1,0:T(2,128)(2,1)S(1)} copy-done((bf16[2,2,32768]{2,1,0:T(2,128)(2,1)S(1)}, bf16[2,2,32768]{2,1,0:T(2,128)(2,1)}, u32[]{:S(2)}) %copy-start.2) | copy-done | bytes 262168
  1.0 0.0 copy-start.4
  1.0 0.0 copy-start.3
  1.0 0.3 shard_map.66.refs_9_
  1.2 0.6 %collective-permute-start.10 = (bf16[2,2,128,128]{3,2,1,0:T(8,128)(2,1)S(1)}, bf16[2,2,128,128]{3,2,1,0:T(8,128)(2,1)S(1)}, u32[]{:S(2)}, u32[]{:S(2)}) collective-permute-start(bf16[2,2,128,128]{3,2,1,0:T(8,128)(2,1)S(1)} %shard_map.66.refs_9_), channel_id=1, source_target_pairs={{0,8},{8,0},{16,24},{24,16},{1,9},{9,1},{17,25},{25,17},{2,10},{10... | collective-permute-start | bytes 393224 | tf_op jit(solution)/shard_map/ppermute | solution.py:324
  1.8 4.7 %collective-permute-start.9 = (bf16[2,2,128,128]{3,2,1,0:T(8,128)(2,1)S(1)}, bf16[2,2,128,128]{3,2,1,0:T(8,128)(2,1)S(1)}, u32[]{:S(2)}, u32[]{:S(2)}) collective-permute-start(bf16[2,2,128,128]{3,2,1,0:T(8,128)(2,1)S(1)} %shard_map.66.refs_9_), channel_id=1, source_target_pairs={{0,6},{2,4},{4,2},{6,0},{1,7},{3,5},{5,3},{7,1},{8,14},{10,12},{12... | collective-permute-start | bytes 393224 | tf_op jit(solution)/shard_map/ppermute | solution.py:324
  6.4 0.0 collective-permute-start.8
  6.4 0.6 %collective-permute-start.7 = (bf16[2,2,128,128]{3,2,1,0:T(8,128)(2,1)S(1)}, bf16[2,2,128,128]{3,2,1,0:T(8,128)(2,1)S(1)}, u32[]{:S(2)}, u32[]{:S(2)}) collective-permute-start(bf16[2,2,128,128]{3,2,1,0:T(8,128)(2,1)S(1)} %shard_map.66.refs_9_), channel_id=1, source_target_pairs={{0,2},{2,0},{4,6},{6,4},{1,3},{3,1},{5,7},{7,5},{8,10},{10,8},{12,... | collective-permute-start | bytes 393224 | tf_op jit(solution)/shard_map/ppermute | solution.py:324
  7.1 0.0 copy-start
  7.1 1.2 %copy-done = bf16[2,64,4096]{2,1,0:T(8,128)(2,1)S(1)} copy-done((bf16[2,64,4096]{2,1,0:T(8,128)(2,1)S(1)}, bf16[2,64,4096]{2,1,0:T(8,128)(2,1)}, u32[]{:S(2)}) %copy-start) | copy-done | bytes 1048600
  8.3 0.0 copy-start.1
  8.3 0.0 copy-start.5
  8.3 0.5 %shard_map.64 = (bf16[2,16,2,16,128]{4,3,2,1,0:T(8,128)(2,1)S(1)}, bf16[2,16,2,16,128]{4,3,2,1,0:T(8,128)(2,1)S(1)}, bf16[2,8,2,16,128]{4,3,2,1,0:T(8,128)(2,1)S(1)}, bf16[2,8,2,16,128]{4,3,2,1,0:T(8,128)(2,1)S(1)}) custom-call(bf16[2,64,4096]{2,1,0:T(8,128)(2,1)S(1)} %copy-done), custom_call_target="tpu_custom_call" | custom-call | flops 1000000 | bytes 32000000 | tf_op jit(solution)/shard_map/pallas_call | solution.py:85
  8.9 0.1 collective-permute-start.1
  8.9 0.7 %add_and_fusion = s32[16]{0:T(128)S(1)} fusion(s32[16]{0:T(128)} %param.9, s32[]{:T(128)S(6)} %mul.44), kind=kLoop, calls=%fused_computation.12 | loop fusion | flops 32 | bytes 132 | tf_op jit(solution)/shard_map/and | solution.py:362
  9.6 0.2 shard_map.65
  9.8 0.0 collective-permute-done.10.refs_13_
  9.8 1.7 %collective-permute-start.3 = (bf16[2,8,2,16,128]{4,3,2,1,0:T(8,128)(2,1)S(1)}, bf16[2,8,2,16,128]{4,3,2,1,0:T(8,128)(2,1)S(1)}, u32[]{:S(2)}, u32[]{:S(2)}) collective-permute-start(bf16[2,8,2,16,128]{4,3,2,1,0:T(8,128)(2,1)S(1)} %get-tuple-element.18), channel_id=1, source_target_pairs={{0,16},{8,24},{16,0},{24,8},{1,17},{9,25},{17,1},{25,9},{2,18},{10... | collective-permute-start | bytes 393224 | tf_op jit(solution)/shard_map/ppermute | solution.py:324
  11.5 0.0 collective-permute-done.9.refs_12_
  11.5 0.2 collective-permute-start.5
  11.7 6.4 %collective-permute-done.8.refs_11_ = bf16[2,2,128,128]{3,2,1,0:T(8,128)(2,1)S(1)} collective-permute-done((bf16[2,2,128,128]{3,2,1,0:T(8,128)(2,1)S(1)}, bf16[2,2,128,128]{3,2,1,0:T(8,128)(2,1)S(1)}, u32[]{:S(2)}, u32[]{:S(2)}) %collective-permute-start.8) | collective-permute-done | bytes 131104 | tf_op jit(solution)/shard_map/ppermute | solution.py:324
  18.1 1.5 %collective-permute-start.14 = (bf16[2,8,2,16,128]{4,3,2,1,0:T(8,128)(2,1)S(1)}, bf16[2,8,2,16,128]{4,3,2,1,0:T(8,128)(2,1)S(1)}, u32[]{:S(2)}, u32[]{:S(2)}) collective-permute-start(bf16[2,8,2,16,128]{4,3,2,1,0:T(8,128)(2,1)S(1)} %get-tuple-element.21), channel_id=1, source_target_pairs={{0,16},{8,24},{16,0},{24,8},{1,17},{9,25},{17,1},{25,9},{2,18},{10... | collective-permute-start | bytes 393224 | tf_op jit(solution)/shard_map/ppermute | solution.py:324
  19.6 0.1 sine_negate_fusion
  19.8 0.0 collective-permute-done.7.refs_10_
  19.8 0.1 collective-permute-start.16
  19.9 0.0 collective-permute-done.3.refs_5_
  19.9 1.6 %collective-permute-start = (bf16[2,16,2,16,128]{4,3,2,1,0:T(8,128)(2,1)S(1)}, bf16[2,16,2,16,128]{4,3,2,1,0:T(8,128)(2,1)S(1)}, u32[]{:S(2)}, u32[]{:S(2)}) collective-permute-start(bf16[2,16,2,16,128]{4,3,2,1,0:T(8,128)(2,1)S(1)} %get-tuple-element.16.refs_1_), channel_id=1, source_target_pairs={{0,1},{1,0},{2,3},{3,2},{4,5},{5,4},{6,7},{7,6},{8,9},{9,8},{10,11... | collective-permute-start | bytes 786440 | tf_op jit(solution)/shard_map/ppermute | solution.py:324
  21.4 0.0 collective-permute-done.5.refs_7_
  21.4 0.3 collective-permute-start.13
  21.7 1.7 %collective-permute-done.14.refs_5_ = bf16[2,8,2,16,128]{4,3,2,1,0:T(8,128)(2,1)S(1)} collective-permute-done((bf16[2,8,2,16,128]{4,3,2,1,0:T(8,128)(2,1)S(1)}, bf16[2,8,2,16,128]{4,3,2,1,0:T(8,128)(2,1)S(1)}, u32[]{:S(2)}, u32[]{:S(2)}) %collective-permute-start.14) | collective-permute-done | bytes 131104 | tf_op jit(solution)/shard_map/ppermute | solution.py:324
  23.4 0.0 collective-permute-start.12
  23.4 0.0 collective-permute-done.1.refs_3_
  23.4 1.5 %collective-permute-start.2 = (bf16[2,16,2,16,128]{4,3,2,1,0:T(8,128)(2,1)S(1)}, bf16[2,16,2,16,128]{4,3,2,1,0:T(8,128)(2,1)S(1)}, u32[]{:S(2)}, u32[]{:S(2)}) collective-permute-start(bf16[2,16,2,16,128]{4,3,2,1,0:T(8,128)(2,1)S(1)} %collective-permute-done.1.refs_3_), channel_id=1, source_target_pairs={{0,1},{1,0},{2,3},{3,2},{4,5},{5,4},{6,7},{7,6},{8,9},{9,8},{10,11... | collective-permute-start | bytes 786440 | tf_op jit(solution)/shard_map/ppermute | solution.py:324
  24.9 0.0 copy-done.4
  24.9 0.1 sine_negate_fusion.1
  25.0 0.0 copy-done.3
  25.0 0.0 copy-done.1
  25.0 0.3 shard_map.67.refs_21_
  25.3 0.3 collective-permute-done.16.refs_7_
  25.6 0.4 collective-permute-start.11
  26.0 0.0 collective-permute-done.13.refs_16_
  26.0 1.5 %collective-permute-start.15 = (bf16[2,8,2,16,128]{4,3,2,1,0:T(8,128)(2,1)S(1)}, bf16[2,8,2,16,128]{4,3,2,1,0:T(8,128)(2,1)S(1)}, u32[]{:S(2)}, u32[]{:S(2)}) collective-permute-start(bf16[2,8,2,16,128]{4,3,2,1,0:T(8,128)(2,1)S(1)} %collective-permute-done.14.refs_5_), channel_id=1, source_target_pairs={{0,1},{1,0},{2,3},{3,2},{4,5},{5,4},{6,7},{7,6},{8,9},{9,8},{10,11... | collective-permute-start | bytes 393224 | tf_op jit(solution)/shard_map/ppermute | solution.py:324
  27.5 0.0 collective-permute-done.12.refs_15_
  27.5 0.5 %collective-permute-start.17 = (bf16[2,8,2,16,128]{4,3,2,1,0:T(8,128)(2,1)S(1)}, bf16[2,8,2,16,128]{4,3,2,1,0:T(8,128)(2,1)S(1)}, u32[]{:S(2)}, u32[]{:S(2)}) collective-permute-start(bf16[2,8,2,16,128]{4,3,2,1,0:T(8,128)(2,1)S(1)} %collective-permute-done.16.refs_7_), channel_id=1, source_target_pairs={{0,1},{1,0},{2,3},{3,2},{4,5},{5,4},{6,7},{7,6},{8,9},{9,8},{10,11... | collective-permute-start | bytes 393224 | tf_op jit(solution)/shard_map/ppermute | solution.py:324
  28.0 0.0 copy-done.5
  28.1 0.0 collective-permute-done.11.refs_14_
  28.1 1.6 %collective-permute-start.4 = (bf16[2,8,2,16,128]{4,3,2,1,0:T(8,128)(2,1)S(1)}, bf16[2,8,2,16,128]{4,3,2,1,0:T(8,128)(2,1)S(1)}, u32[]{:S(2)}, u32[]{:S(2)}) collective-permute-start(bf16[2,8,2,16,128]{4,3,2,1,0:T(8,128)(2,1)S(1)} %collective-permute-done.3.refs_5_), channel_id=1, source_target_pairs={{0,1},{1,0},{2,3},{3,2},{4,5},{5,4},{6,7},{7,6},{8,9},{9,8},{10,11... | collective-permute-start | bytes 393224 | tf_op jit(solution)/shard_map/ppermute | solution.py:324
  29.6 7.9 %collective-permute-done.15.refs_6_ = bf16[2,8,2,16,128]{4,3,2,1,0:T(8,128)(2,1)S(1)} collective-permute-done((bf16[2,8,2,16,128]{4,3,2,1,0:T(8,128)(2,1)S(1)}, bf16[2,8,2,16,128]{4,3,2,1,0:T(8,128)(2,1)S(1)}, u32[]{:S(2)}, u32[]{:S(2)}) %collective-permute-start.15) | collective-permute-done | bytes 131104 | tf_op jit(solution)/shard_map/ppermute | solution.py:324
  37.5 1.5 %collective-permute-start.6 = (bf16[2,8,2,16,128]{4,3,2,1,0:T(8,128)(2,1)S(1)}, bf16[2,8,2,16,128]{4,3,2,1,0:T(8,128)(2,1)S(1)}, u32[]{:S(2)}, u32[]{:S(2)}) collective-permute-start(bf16[2,8,2,16,128]{4,3,2,1,0:T(8,128)(2,1)S(1)} %collective-permute-done.5.refs_7_), channel_id=1, source_target_pairs={{0,1},{1,0},{2,3},{3,2},{4,5},{5,4},{6,7},{7,6},{8,9},{9,8},{10,11... | collective-permute-start | bytes 393224 | tf_op jit(solution)/shard_map/ppermute | solution.py:324
  39.0 1.3 %collective-permute-done.17.refs_8_ = bf16[2,8,2,16,128]{4,3,2,1,0:T(8,128)(2,1)S(1)} collective-permute-done((bf16[2,8,2,16,128]{4,3,2,1,0:T(8,128)(2,1)S(1)}, bf16[2,8,2,16,128]{4,3,2,1,0:T(8,128)(2,1)S(1)}, u32[]{:S(2)}, u32[]{:S(2)}) %collective-permute-start.17) | collective-permute-done | bytes 131104 | tf_op jit(solution)/shard_map/ppermute | solution.py:324
  40.4 0.0 collective-permute-done.refs_2_
  40.4 0.0 collective-permute-done.2.refs_4_
  40.4 4.5 %shard_map.68.refs_24_ = f32[2,1024,128]{2,1,0:T(8,128)S(1)} custom-call(s32[16]{0:T(128)S(1)} %fusion.2.refs_0_, bf16[2,16,2,16,128]{4,3,2,1,0:T(8,128)(2,1)S(1)} %get-tuple-element.16.refs_1_, bf16[2,16,2,16,128]{4,3,2,1,0:T(8,128)(2,1)S(1)} %collective-permute-done.refs_2_, bf16[2,16,2,16,128]{4,3,2,1,0:T(8,128)(2,1)S(1)} %collective-permute-done.1.refs_3_, ...), custom_call_target="tpu_custom_call" | custom-call | flops 3000000000 | bytes 8000000 | tf_op jit(solution)/shard_map/pallas_call | solution.py:297
  44.9 0.0 collective-permute-done.4.refs_6_
  44.9 0.6 %collective-permute-done.6.refs_8_ = bf16[2,8,2,16,128]{4,3,2,1,0:T(8,128)(2,1)S(1)} collective-permute-done((bf16[2,8,2,16,128]{4,3,2,1,0:T(8,128)(2,1)S(1)}, bf16[2,8,2,16,128]{4,3,2,1,0:T(8,128)(2,1)S(1)}, u32[]{:S(2)}, u32[]{:S(2)}) %collective-permute-start.6) | collective-permute-done | bytes 131104 | tf_op jit(solution)/shard_map/ppermute | solution.py:324
  45.5 5.5 %shard_map.69 = f32[2,2,1024,128]{3,2,1,0:T(8,128)} custom-call(s32[16]{0:T(128)S(1)} %fusion.2.refs_0_, bf16[2,16,2,16,128]{4,3,2,1,0:T(8,128)(2,1)S(1)} %get-tuple-element.16.refs_1_, bf16[2,16,2,16,128]{4,3,2,1,0:T(8,128)(2,1)S(1)} %collective-permute-done.refs_2_, bf16[2,16,2,16,128]{4,3,2,1,0:T(8,128)(2,1)S(1)} %collective-permute-done.1.refs_3_, ...), custom_call_target="tpu_custom_call" | custom-call | flops 3000000000 | bytes 8000000 | tf_op jit(solution)/shard_map/pallas_call | solution.py:297
  (1 shorter events, 0.0 us)
Async XLA Ops:
  0.0 0.9 %copy-start.2 = (bf16[2,2,32768]{2,1,0:T(2,128)(2,1)S(1)}, bf16[2,2,32768]{2,1,0:T(2,128)(2,1)}, u32[]{:S(2)}) copy-start(bf16[2,2,32768]{2,1,0:T(2,128)(2,1)} %filters.1) | copy-start | bytes 786436
  1.0 23.9 %copy-start.4 = (s32[16]{0:T(128)S(1)}, s32[16]{0:T(128)}, u32[]{:S(2)}) copy-start(s32[16]{0:T(128)} %param.9) | copy-start | bytes 196
  1.0 24.0 %copy-start.3 = (f32[2,256,128]{2,1,0:T(8,128)S(1)}, f32[2,256,128]{2,1,0:T(8,128)}, u32[]{:S(2)}) copy-start(f32[2,256,128]{2,1,0:T(8,128)} %constant.51.clone.twist.refs_23_) | copy-start | bytes 786436
  1.2 8.6 %collective-permute-start.10 = (bf16[2,2,128,128]{3,2,1,0:T(8,128)(2,1)S(1)}, bf16[2,2,128,128]{3,2,1,0:T(8,128)(2,1)S(1)}, u32[]{:S(2)}, u32[]{:S(2)}) collective-permute-start(bf16[2,2,128,128]{3,2,1,0:T(8,128)(2,1)S(1)} %shard_map.66.refs_9_), channel_id=1, source_target_pairs={{0,8},{8,0},{16,24},{24,16},{1,9},{9,1},{17,25},{25,17},{2,10},{10... | collective-permute-start | bytes 393224 | tf_op jit(solution)/shard_map/ppermute | solution.py:324
  1.8 9.8 %collective-permute-start.9 = (bf16[2,2,128,128]{3,2,1,0:T(8,128)(2,1)S(1)}, bf16[2,2,128,128]{3,2,1,0:T(8,128)(2,1)S(1)}, u32[]{:S(2)}, u32[]{:S(2)}) collective-permute-start(bf16[2,2,128,128]{3,2,1,0:T(8,128)(2,1)S(1)} %shard_map.66.refs_9_), channel_id=1, source_target_pairs={{0,6},{2,4},{4,2},{6,0},{1,7},{3,5},{5,3},{7,1},{8,14},{10,12},{12... | collective-permute-start | bytes 393224 | tf_op jit(solution)/shard_map/ppermute | solution.py:324
  6.4 11.7 %collective-permute-start.8 = (bf16[2,2,128,128]{3,2,1,0:T(8,128)(2,1)S(1)}, bf16[2,2,128,128]{3,2,1,0:T(8,128)(2,1)S(1)}, u32[]{:S(2)}, u32[]{:S(2)}) collective-permute-start(bf16[2,2,128,128]{3,2,1,0:T(8,128)(2,1)S(1)} %shard_map.66.refs_9_), channel_id=1, source_target_pairs={{0,4},{2,6},{4,0},{6,2},{1,5},{3,7},{5,1},{7,3},{8,12},{10,14},{12... | collective-permute-start | bytes 393224 | tf_op jit(solution)/shard_map/ppermute | solution.py:324
  6.4 13.3 %collective-permute-start.7 = (bf16[2,2,128,128]{3,2,1,0:T(8,128)(2,1)S(1)}, bf16[2,2,128,128]{3,2,1,0:T(8,128)(2,1)S(1)}, u32[]{:S(2)}, u32[]{:S(2)}) collective-permute-start(bf16[2,2,128,128]{3,2,1,0:T(8,128)(2,1)S(1)} %shard_map.66.refs_9_), channel_id=1, source_target_pairs={{0,2},{2,0},{4,6},{6,4},{1,3},{3,1},{5,7},{7,5},{8,10},{10,8},{12,... | collective-permute-start | bytes 393224 | tf_op jit(solution)/shard_map/ppermute | solution.py:324
  7.1 1.2 %copy-start = (bf16[2,64,4096]{2,1,0:T(8,128)(2,1)S(1)}, bf16[2,64,4096]{2,1,0:T(8,128)(2,1)}, u32[]{:S(2)}) copy-start(bf16[2,64,4096]{2,1,0:T(8,128)(2,1)} %echoes.1) | copy-start | bytes 3145732
  8.3 16.7 %copy-start.1 = (bf16[2560,256]{1,0:T(8,128)(2,1)S(1)}, bf16[2560,256]{1,0:T(8,128)(2,1)}, u32[]{:S(2)}) copy-start(bf16[2560,256]{1,0:T(8,128)(2,1)} %constant.50.clone.dots.refs_22_) | copy-start | bytes 3932164
  8.3 19.7 %copy-start.5 = (s32[16]{0:T(128)S(1)}, s32[16]{0:T(128)}, u32[]{:S(2)}) copy-start(s32[16]{0:T(128)} %param.8) | copy-start | bytes 196
  8.9 14.5 %collective-permute-start.1 = (bf16[2,16,2,16,128]{4,3,2,1,0:T(8,128)(2,1)S(1)}, bf16[2,16,2,16,128]{4,3,2,1,0:T(8,128)(2,1)S(1)}, u32[]{:S(2)}, u32[]{:S(2)}) collective-permute-start(bf16[2,16,2,16,128]{4,3,2,1,0:T(8,128)(2,1)S(1)} %get-tuple-element.17), channel_id=1, source_target_pairs={{0,8},{8,0},{16,24},{24,16},{1,9},{9,1},{17,25},{25,17},{2,10},{10... | collective-permute-start | bytes 786440 | tf_op jit(solution)/shard_map/ppermute | solution.py:324
  9.8 10.1 %collective-permute-start.3 = (bf16[2,8,2,16,128]{4,3,2,1,0:T(8,128)(2,1)S(1)}, bf16[2,8,2,16,128]{4,3,2,1,0:T(8,128)(2,1)S(1)}, u32[]{:S(2)}, u32[]{:S(2)}) collective-permute-start(bf16[2,8,2,16,128]{4,3,2,1,0:T(8,128)(2,1)S(1)} %get-tuple-element.18), channel_id=1, source_target_pairs={{0,16},{8,24},{16,0},{24,8},{1,17},{9,25},{17,1},{25,9},{2,18},{10... | collective-permute-start | bytes 393224 | tf_op jit(solution)/shard_map/ppermute | solution.py:324
  11.5 9.9 %collective-permute-start.5 = (bf16[2,8,2,16,128]{4,3,2,1,0:T(8,128)(2,1)S(1)}, bf16[2,8,2,16,128]{4,3,2,1,0:T(8,128)(2,1)S(1)}, u32[]{:S(2)}, u32[]{:S(2)}) collective-permute-start(bf16[2,8,2,16,128]{4,3,2,1,0:T(8,128)(2,1)S(1)} %get-tuple-element.19), channel_id=1, source_target_pairs={{0,24},{8,16},{16,8},{24,0},{1,25},{9,17},{17,9},{25,1},{2,26},{10... | collective-permute-start | bytes 393224 | tf_op jit(solution)/shard_map/ppermute | solution.py:324
  18.1 5.3 %collective-permute-start.14 = (bf16[2,8,2,16,128]{4,3,2,1,0:T(8,128)(2,1)S(1)}, bf16[2,8,2,16,128]{4,3,2,1,0:T(8,128)(2,1)S(1)}, u32[]{:S(2)}, u32[]{:S(2)}) collective-permute-start(bf16[2,8,2,16,128]{4,3,2,1,0:T(8,128)(2,1)S(1)} %get-tuple-element.21), channel_id=1, source_target_pairs={{0,16},{8,24},{16,0},{24,8},{1,17},{9,25},{17,1},{25,9},{2,18},{10... | collective-permute-start | bytes 393224 | tf_op jit(solution)/shard_map/ppermute | solution.py:324
  19.8 5.9 %collective-permute-start.16 = (bf16[2,8,2,16,128]{4,3,2,1,0:T(8,128)(2,1)S(1)}, bf16[2,8,2,16,128]{4,3,2,1,0:T(8,128)(2,1)S(1)}, u32[]{:S(2)}, u32[]{:S(2)}) collective-permute-start(bf16[2,8,2,16,128]{4,3,2,1,0:T(8,128)(2,1)S(1)} %get-tuple-element.22), channel_id=1, source_target_pairs={{0,24},{8,16},{16,8},{24,0},{1,25},{9,17},{17,9},{25,1},{2,26},{10... | collective-permute-start | bytes 393224 | tf_op jit(solution)/shard_map/ppermute | solution.py:324
  19.9 20.5 %collective-permute-start = (bf16[2,16,2,16,128]{4,3,2,1,0:T(8,128)(2,1)S(1)}, bf16[2,16,2,16,128]{4,3,2,1,0:T(8,128)(2,1)S(1)}, u32[]{:S(2)}, u32[]{:S(2)}) collective-permute-start(bf16[2,16,2,16,128]{4,3,2,1,0:T(8,128)(2,1)S(1)} %get-tuple-element.16.refs_1_), channel_id=1, source_target_pairs={{0,1},{1,0},{2,3},{3,2},{4,5},{5,4},{6,7},{7,6},{8,9},{9,8},{10,11... | collective-permute-start | bytes 786440 | tf_op jit(solution)/shard_map/ppermute | solution.py:324
  21.4 4.6 %collective-permute-start.13 = (bf16[2,2,128,128]{3,2,1,0:T(8,128)(2,1)S(1)}, bf16[2,2,128,128]{3,2,1,0:T(8,128)(2,1)S(1)}, u32[]{:S(2)}, u32[]{:S(2)}) collective-permute-start(bf16[2,2,128,128]{3,2,1,0:T(8,128)(2,1)S(1)} %collective-permute-done.9.refs_12_), channel_id=1, source_target_pairs={{0,8},{8,0},{16,24},{24,16},{1,9},{9,1},{17,25},{25,17},{2,10},{10... | collective-permute-start | bytes 393224 | tf_op jit(solution)/shard_map/ppermute | solution.py:324
  23.4 4.1 %collective-permute-start.12 = (bf16[2,2,128,128]{3,2,1,0:T(8,128)(2,1)S(1)}, bf16[2,2,128,128]{3,2,1,0:T(8,128)(2,1)S(1)}, u32[]{:S(2)}, u32[]{:S(2)}) collective-permute-start(bf16[2,2,128,128]{3,2,1,0:T(8,128)(2,1)S(1)} %collective-permute-done.8.refs_11_), channel_id=1, source_target_pairs={{0,8},{8,0},{16,24},{24,16},{1,9},{9,1},{17,25},{25,17},{2,10},{10... | collective-permute-start | bytes 393224 | tf_op jit(solution)/shard_map/ppermute | solution.py:324
  23.4 17.0 %collective-permute-start.2 = (bf16[2,16,2,16,128]{4,3,2,1,0:T(8,128)(2,1)S(1)}, bf16[2,16,2,16,128]{4,3,2,1,0:T(8,128)(2,1)S(1)}, u32[]{:S(2)}, u32[]{:S(2)}) collective-permute-start(bf16[2,16,2,16,128]{4,3,2,1,0:T(8,128)(2,1)S(1)} %collective-permute-done.1.refs_3_), channel_id=1, source_target_pairs={{0,1},{1,0},{2,3},{3,2},{4,5},{5,4},{6,7},{7,6},{8,9},{9,8},{10,11... | collective-permute-start | bytes 786440 | tf_op jit(solution)/shard_map/ppermute | solution.py:324
  25.6 2.4 %collective-permute-start.11 = (bf16[2,2,128,128]{3,2,1,0:T(8,128)(2,1)S(1)}, bf16[2,2,128,128]{3,2,1,0:T(8,128)(2,1)S(1)}, u32[]{:S(2)}, u32[]{:S(2)}) collective-permute-start(bf16[2,2,128,128]{3,2,1,0:T(8,128)(2,1)S(1)} %collective-permute-done.7.refs_10_), channel_id=1, source_target_pairs={{0,8},{8,0},{16,24},{24,16},{1,9},{9,1},{17,25},{25,17},{2,10},{10... | collective-permute-start | bytes 393224 | tf_op jit(solution)/shard_map/ppermute | solution.py:324
  26.0 11.5 %collective-permute-start.15 = (bf16[2,8,2,16,128]{4,3,2,1,0:T(8,128)(2,1)S(1)}, bf16[2,8,2,16,128]{4,3,2,1,0:T(8,128)(2,1)S(1)}, u32[]{:S(2)}, u32[]{:S(2)}) collective-permute-start(bf16[2,8,2,16,128]{4,3,2,1,0:T(8,128)(2,1)S(1)} %collective-permute-done.14.refs_5_), channel_id=1, source_target_pairs={{0,1},{1,0},{2,3},{3,2},{4,5},{5,4},{6,7},{7,6},{8,9},{9,8},{10,11... | collective-permute-start | bytes 393224 | tf_op jit(solution)/shard_map/ppermute | solution.py:324
  27.5 12.9 %collective-permute-start.17 = (bf16[2,8,2,16,128]{4,3,2,1,0:T(8,128)(2,1)S(1)}, bf16[2,8,2,16,128]{4,3,2,1,0:T(8,128)(2,1)S(1)}, u32[]{:S(2)}, u32[]{:S(2)}) collective-permute-start(bf16[2,8,2,16,128]{4,3,2,1,0:T(8,128)(2,1)S(1)} %collective-permute-done.16.refs_7_), channel_id=1, source_target_pairs={{0,1},{1,0},{2,3},{3,2},{4,5},{5,4},{6,7},{7,6},{8,9},{9,8},{10,11... | collective-permute-start | bytes 393224 | tf_op jit(solution)/shard_map/ppermute | solution.py:324
  28.1 16.9 %collective-permute-start.4 = (bf16[2,8,2,16,128]{4,3,2,1,0:T(8,128)(2,1)S(1)}, bf16[2,8,2,16,128]{4,3,2,1,0:T(8,128)(2,1)S(1)}, u32[]{:S(2)}, u32[]{:S(2)}) collective-permute-start(bf16[2,8,2,16,128]{4,3,2,1,0:T(8,128)(2,1)S(1)} %collective-permute-done.3.refs_5_), channel_id=1, source_target_pairs={{0,1},{1,0},{2,3},{3,2},{4,5},{5,4},{6,7},{7,6},{8,9},{9,8},{10,11... | collective-permute-start | bytes 393224 | tf_op jit(solution)/shard_map/ppermute | solution.py:324
  37.5 8.0 %collective-permute-start.6 = (bf16[2,8,2,16,128]{4,3,2,1,0:T(8,128)(2,1)S(1)}, bf16[2,8,2,16,128]{4,3,2,1,0:T(8,128)(2,1)S(1)}, u32[]{:S(2)}, u32[]{:S(2)}) collective-permute-start(bf16[2,8,2,16,128]{4,3,2,1,0:T(8,128)(2,1)S(1)} %collective-permute-done.5.refs_7_), channel_id=1, source_target_pairs={{0,1},{1,0},{2,3},{3,2},{4,5},{5,4},{6,7},{7,6},{8,9},{9,8},{10,11... | collective-permute-start | bytes 393224 | tf_op jit(solution)/shard_map/ppermute | solution.py:324

commit v2 on v1

--- a/solution.py
+++ b/solution.py
@@ -47,8 +47,11 @@
     middle = np.stack(hi_lo(block_matrix(lane_phase, -1.0).T))
     back = np.stack(hi_lo(block_matrix(lane_phase, 1.0).T))
     parts = [np.stack(first), middle, back, np.stack(last)]
-    dots = np.concatenate([a.reshape(-1, a.shape[-1]) for a in parts], 0)
-    return dots, np.stack([np.cos(twist), np.sin(twist)]).astype(np.float32)
+    left = np.concatenate([np.cos(twist), np.sin(twist)], 1).astype(np.float32)
+    for _ in range(3):
+        parts.append(left.astype(jnp.bfloat16))
+        left = left - parts[-1].astype(np.float32)
+    return np.concatenate([a.reshape(-1, a.shape[-1]) for a in parts], 0)
 
 
 def split(value):
@@ -93,26 +96,32 @@
     )(echoes)
 
 
-def order_kernel(width, strips, dots, twist, out):
+def order_kernel(width, strips, slow, dots, out, twist):
     me = lax.axis_index("turn") * strips + lax.axis_index("strip")
     size = dots.shape[1]
     row_ids = lax.broadcasted_iota(jnp.int32, (size, size), 0)
     col_ids = lax.broadcasted_iota(jnp.int32, (size, size), 1)
     order = jnp.where(row_ids == (col_ids ^ (me * width)), 1.0, 0.0).astype(jnp.bfloat16)
     out[...] = dot(dots[: 4 * size], order).astype(jnp.bfloat16)
-
-
-def order_tables(dots, twist, width, strips):
+    base = dots.shape[0] - 3 * slow
+    terms = [dots[base + k * slow : base + (k + 1) * slow].astype(jnp.float32) for k in range(3)]
+    twist[...] = terms[0] + terms[1] + terms[2]
+
+
+def order_tables(dots, width, strips, slow):
     vm = pl.BlockSpec(memory_space=pltpu.VMEM)
     size = dots.shape[1]
     return pl.pallas_call(
-        functools.partial(order_kernel, width, strips),
-        in_specs=[vm, vm],
-        out_specs=vm,
-        out_shape=jax.ShapeDtypeStruct((4 * size, size), jnp.bfloat16),
+        functools.partial(order_kernel, width, strips, slow),
+        in_specs=[vm],
+        out_specs=[vm, vm],
+        out_shape=[
+            jax.ShapeDtypeStruct((4 * size, size), jnp.bfloat16),
+            jax.ShapeDtypeStruct((slow, 2 * LANES), jnp.float32),
+        ],
         compiler_params=pltpu.CompilerParams(vmem_limit_bytes=8 * 1024 * 1024),
-        cost_estimate=pl.CostEstimate(flops=10**6, bytes_accessed=4 * 10**6, transcendentals=0),
-    )(dots, twist)
+        cost_estimate=pl.CostEstimate(flops=10**6, bytes_accessed=2 * 10**6, transcendentals=0),
+    )(dots)
 
 
 def turn_kernel(filters, out, turned):
@@ -139,7 +148,7 @@
         out_shape=jax.ShapeDtypeStruct(shape, jnp.bfloat16),
         scratch_shapes=[pltpu.VMEM(shape, jnp.float32)],
         compiler_params=pltpu.CompilerParams(vmem_limit_bytes=4 * 1024 * 1024),
-        cost_estimate=pl.CostEstimate(flops=10**6, bytes_accessed=16 * 10**6, transcendentals=0),
+        cost_estimate=pl.CostEstimate(flops=10**6, bytes_accessed=2 * 10**6, transcendentals=0),
     )(filters)
 
 
@@ -201,7 +210,7 @@
                     re, im = even_re + odd_re, even_im + odd_im
                 else:
                     re, im = even_re - odd_re, even_im - odd_im
-                tw_re, tw_im = twist[0, rows_c], twist[1, rows_c]
+                tw_re, tw_im = twist[rows_c, :LANES], twist[rows_c, LANES:]
                 (rh, rl), (ih, il) = split(re * tw_re + im * tw_im), split(im * tw_re - re * tw_im)
                 y1[pair, i, rows_c] = jnp.concatenate([rh, ih, rl, il], 1)
 
@@ -234,7 +243,7 @@
                 rows_c = slice(part * half, (part + 1) * half)
                 rows_s = slice(i * slow + part * half, i * slow + (part + 1) * half)
                 re, im = s3[pair, rows_s, :LANES], s3[pair, rows_s, LANES:]
-                tw_re, tw_im = twist[0, rows_c], twist[1, rows_c]
+                tw_re, tw_im = twist[rows_c, :LANES], twist[rows_c, LANES:]
                 re, im = re * tw_re - im * tw_im, re * tw_im + im * tw_re
                 u_re, u_im = slow_ramp[0, rows_c, r : r + 1], slow_ramp[1, rows_c, r : r + 1]
                 parts.append((re * u_re - im * u_im, re * u_im + im * u_re))
@@ -284,7 +293,7 @@
         write.wait()
 
 
-def focus(blocks, bases, own, other, ramps, first, t, slabs, images, rows, row0, total, slow, out_slow, final):
+def focus(blocks, bases, own, other, ramps, tables, slabs, images, rows, row0, total, slow, out_slow, final):
     slots, pieces = rows // 2, len(own)
 
     def full(a):
@@ -292,7 +301,7 @@
 
     image = (2, out_slow * 8, LANES)
     shape = (2, total // 8, *image[1:]) if final else image
-    operands = [slabs, *blocks, *own, *other, *ramps, first, *t, *images]
+    operands = [slabs, *blocks, *own, *other, *ramps, *tables, *images]
     extra = [pltpu.VMEM(image, jnp.float32), pltpu.SemaphoreType.DMA((total // 4,))] if final else []
     return pl.pallas_call(
         functools.partial(focus_kernel, tuple(bases), pieces, len(images), rows, row0, slow, out_slow),
@@ -336,16 +345,16 @@
     width = slow // sources
     behind = (strips - strip) * (length // strips)
     echoes, zone, behind = lax.optimization_barrier((echoes, zone, behind))
-    t = [jnp.asarray(a) for a in tables(length, sources, length // strips)]
+    dots = jnp.asarray(tables(length, sources, length // strips))
 
     jobs = [[(0, 0, total), (1, 0, total)], []]
     starts = [sum(CHUNKS[:k]) for k in range(len(CHUNKS))]
     for k, rows in enumerate(CHUNKS):
         jobs[min(k, 1)] += [(flip, starts[k], rows) for flip in range(2, turns)]
-    sent = pack(echoes, jobs[0], total, 32 * 10**6)
-    more = pack(echoes, jobs[1], total, 4 * 10**6)
+    sent = pack(echoes, jobs[0], total, 8 * 10**6)
+    more = pack(echoes, jobs[1], total, 2 * 10**6)
     half = turn_filters(filters)
-    first = order_tables(*t, width, strips)
+    first, twist = order_tables(dots, width, strips, slow)
     held = {}
     for (flip, start, rows), block in zip(jobs[0] + jobs[1], [*sent, *more]):
         if flip:
@@ -374,7 +383,7 @@
             bases.append(start if whole else 0)
         final = k == len(CHUNKS) - 1
         image = focus(
-            blocks, bases, own, other, ramps, first, t, local_slab, images, rows, start, total, slow, out_slow, final
+            blocks, bases, own, other, ramps, (first, dots, twist), local_slab, images, rows, start, total, slow, out_slow, final
         )
         images.append(image)
     image = image.reshape(2, total // 8, out_slow, 8, LANES).transpose(0, 1, 3, 2, 4)

time: 51.3 us -> 51.3 us (level)
    unnamed x12 -> x10, local copies, waits for them, and re-layouts: 2.19 us -> 2.18 us
where the time goes in v2:
time: 51.3 us; the launch traced here: 51.1 us
  starting transfers between devices  18.2 us (35%)
  waiting for transfers between devices  18.2 us (35%)
  Pallas kernels  11.6 us (23%)
  local copies, waits for them, and re-layouts  2.18 us (4%)
  other arithmetic  0.94 us (2%)
    ppermute x18, starting transfers between devices, swap(): return lax.ppermute(value, axis, [(a, a ^ flip) for a in range(size)])  18.2 us
    ppermute x18, waiting for transfers between devices, swap(): return lax.ppermute(value, axis, [(a, a ^ flip) for a in range(size)])  18.2 us
    pallas_call x2, Pallas kernels, focus(): pl.pallas_call(functools.partial(focus_kernel, tuple(bases), pieces, len(...  10.2 us
    unnamed x10, local copies, waits for them, and re-layouts  2.18 us
  transfers between devices with their start and end apart: 18, of which 6 were waited for; matrix products, arithmetic and copies ran while one was open for 2% of the time, Pallas kernels for 11%

profile of v2, /device:TPU:0, one launch (start us, length us, event | category | flops | bytes accessed | tf_op | source)
XLA Modules:
  0.0 51.1 jit_solution(5448424115079838971)
XLA Ops:
  0.0 0.0 copy-start.2
  0.0 0.9 %copy-done.2 = bf16[2,2,32768]{2,1,0:T(2,128)(2,1)S(1)} copy-done((bf16[2,2,32768]{2,1,0:T(2,128)(2,1)S(1)}, bf16[2,2,32768]{2,1,0:T(2,128)(2,1)}, u32[]{:S(2)}) %copy-start.2) | copy-done | bytes 262168
  1.0 0.0 copy-start.3
  1.0 0.0 copy-start.4
  1.0 0.3 shard_map.57.refs_9_
  1.2 0.6 %collective-permute-start.10 = (bf16[2,2,128,128]{3,2,1,0:T(8,128)(2,1)S(1)}, bf16[2,2,128,128]{3,2,1,0:T(8,128)(2,1)S(1)}, u32[]{:S(2)}, u32[]{:S(2)}) collective-permute-start(bf16[2,2,128,128]{3,2,1,0:T(8,128)(2,1)S(1)} %shard_map.57.refs_9_), channel_id=1, source_target_pairs={{0,8},{8,0},{16,24},{24,16},{1,9},{9,1},{17,25},{25,17},{2,10},{10... | collective-permute-start | bytes 393224 | tf_op jit(solution)/shard_map/ppermute | solution.py:333
  1.8 4.7 %collective-permute-start.9 = (bf16[2,2,128,128]{3,2,1,0:T(8,128)(2,1)S(1)}, bf16[2,2,128,128]{3,2,1,0:T(8,128)(2,1)S(1)}, u32[]{:S(2)}, u32[]{:S(2)}) collective-permute-start(bf16[2,2,128,128]{3,2,1,0:T(8,128)(2,1)S(1)} %shard_map.57.refs_9_), channel_id=1, source_target_pairs={{0,6},{2,4},{4,2},{6,0},{1,7},{3,5},{5,3},{7,1},{8,14},{10,12},{12... | collective-permute-start | bytes 393224 | tf_op jit(solution)/shard_map/ppermute | solution.py:333
  6.4 0.0 collective-permute-start.8
  6.4 0.6 %collective-permute-start.7 = (bf16[2,2,128,128]{3,2,1,0:T(8,128)(2,1)S(1)}, bf16[2,2,128,128]{3,2,1,0:T(8,128)(2,1)S(1)}, u32[]{:S(2)}, u32[]{:S(2)}) collective-permute-start(bf16[2,2,128,128]{3,2,1,0:T(8,128)(2,1)S(1)} %shard_map.57.refs_9_), channel_id=1, source_target_pairs={{0,2},{2,0},{4,6},{6,4},{1,3},{3,1},{5,7},{7,5},{8,10},{10,8},{12,... | collective-permute-start | bytes 393224 | tf_op jit(solution)/shard_map/ppermute | solution.py:333
  7.1 0.0 copy-start
  7.1 1.2 %copy-done = bf16[2,64,4096]{2,1,0:T(8,128)(2,1)S(1)} copy-done((bf16[2,64,4096]{2,1,0:T(8,128)(2,1)S(1)}, bf16[2,64,4096]{2,1,0:T(8,128)(2,1)}, u32[]{:S(2)}) %copy-start) | copy-done | bytes 1048600
  8.3 0.0 copy-start.1
  8.3 0.5 %shard_map.55 = (bf16[2,16,2,16,128]{4,3,2,1,0:T(8,128)(2,1)S(1)}, bf16[2,16,2,16,128]{4,3,2,1,0:T(8,128)(2,1)S(1)}, bf16[2,8,2,16,128]{4,3,2,1,0:T(8,128)(2,1)S(1)}, bf16[2,8,2,16,128]{4,3,2,1,0:T(8,128)(2,1)S(1)}) custom-call(bf16[2,64,4096]{2,1,0:T(8,128)(2,1)S(1)} %copy-done), custom_call_target="tpu_custom_call" | custom-call | flops 1000000 | bytes 8000000 | tf_op jit(solution)/shard_map/pallas_call | solution.py:88
  8.9 0.1 collective-permute-start.1
  8.9 0.7 %add_and_fusion = s32[16]{0:T(128)S(1)} fusion(s32[16]{0:T(128)} %param.8, s32[]{:T(128)S(6)} %mul.44), kind=kLoop, calls=%fused_computation.12 | loop fusion | flops 32 | bytes 132 | tf_op jit(solution)/shard_map/and | solution.py:371
  9.6 0.2 shard_map.56
  9.8 0.0 collective-permute-done.10.refs_13_
  9.8 1.7 %collective-permute-start.3 = (bf16[2,8,2,16,128]{4,3,2,1,0:T(8,128)(2,1)S(1)}, bf16[2,8,2,16,128]{4,3,2,1,0:T(8,128)(2,1)S(1)}, u32[]{:S(2)}, u32[]{:S(2)}) collective-permute-start(bf16[2,8,2,16,128]{4,3,2,1,0:T(8,128)(2,1)S(1)} %get-tuple-element.20), channel_id=1, source_target_pairs={{0,16},{8,24},{16,0},{24,8},{1,17},{9,25},{17,1},{25,9},{2,18},{10... | collective-permute-start | bytes 393224 | tf_op jit(solution)/shard_map/ppermute | solution.py:333
  11.5 0.0 collective-permute-done.9.refs_12_
  11.5 0.2 collective-permute-start.5
  11.7 6.4 %collective-permute-done.8.refs_11_ = bf16[2,2,128,128]{3,2,1,0:T(8,128)(2,1)S(1)} collective-permute-done((bf16[2,2,128,128]{3,2,1,0:T(8,128)(2,1)S(1)}, bf16[2,2,128,128]{3,2,1,0:T(8,128)(2,1)S(1)}, u32[]{:S(2)}, u32[]{:S(2)}) %collective-permute-start.8) | collective-permute-done | bytes 131104 | tf_op jit(solution)/shard_map/ppermute | solution.py:333
  18.1 1.5 %collective-permute-start.14 = (bf16[2,8,2,16,128]{4,3,2,1,0:T(8,128)(2,1)S(1)}, bf16[2,8,2,16,128]{4,3,2,1,0:T(8,128)(2,1)S(1)}, u32[]{:S(2)}, u32[]{:S(2)}) collective-permute-start(bf16[2,8,2,16,128]{4,3,2,1,0:T(8,128)(2,1)S(1)} %get-tuple-element.25), channel_id=1, source_target_pairs={{0,16},{8,24},{16,0},{24,8},{1,17},{9,25},{17,1},{25,9},{2,18},{10... | collective-permute-start | bytes 393224 | tf_op jit(solution)/shard_map/ppermute | solution.py:333
  19.6 0.1 sine_negate_fusion
  19.8 0.0 collective-permute-done.7.refs_10_
  19.8 0.1 collective-permute-start.16
  19.9 0.0 collective-permute-done.3.refs_5_
  19.9 1.6 %collective-permute-start = (bf16[2,16,2,16,128]{4,3,2,1,0:T(8,128)(2,1)S(1)}, bf16[2,16,2,16,128]{4,3,2,1,0:T(8,128)(2,1)S(1)}, u32[]{:S(2)}, u32[]{:S(2)}) collective-permute-start(bf16[2,16,2,16,128]{4,3,2,1,0:T(8,128)(2,1)S(1)} %get-tuple-element.18.refs_1_), channel_id=1, source_target_pairs={{0,1},{1,0},{2,3},{3,2},{4,5},{5,4},{6,7},{7,6},{8,9},{9,8},{10,11... | collective-permute-start | bytes 786440 | tf_op jit(solution)/shard_map/ppermute | solution.py:333
  21.4 0.0 collective-permute-done.5.refs_7_
  21.4 0.3 collective-permute-start.13
  21.7 1.7 %collective-permute-done.14.refs_5_ = bf16[2,8,2,16,128]{4,3,2,1,0:T(8,128)(2,1)S(1)} collective-permute-done((bf16[2,8,2,16,128]{4,3,2,1,0:T(8,128)(2,1)S(1)}, bf16[2,8,2,16,128]{4,3,2,1,0:T(8,128)(2,1)S(1)}, u32[]{:S(2)}, u32[]{:S(2)}) %collective-permute-start.14) | collective-permute-done | bytes 131104 | tf_op jit(solution)/shard_map/ppermute | solution.py:333
  23.4 0.0 collective-permute-start.12
  23.4 0.0 collective-permute-done.1.refs_3_
  23.4 1.5 %collective-permute-start.2 = (bf16[2,16,2,16,128]{4,3,2,1,0:T(8,128)(2,1)S(1)}, bf16[2,16,2,16,128]{4,3,2,1,0:T(8,128)(2,1)S(1)}, u32[]{:S(2)}, u32[]{:S(2)}) collective-permute-start(bf16[2,16,2,16,128]{4,3,2,1,0:T(8,128)(2,1)S(1)} %collective-permute-done.1.refs_3_), channel_id=1, source_target_pairs={{0,1},{1,0},{2,3},{3,2},{4,5},{5,4},{6,7},{7,6},{8,9},{9,8},{10,11... | collective-permute-start | bytes 786440 | tf_op jit(solution)/shard_map/ppermute | solution.py:333
  24.9 0.0 copy-done.3
  24.9 0.1 sine_negate_fusion.1
  25.0 0.0 copy-done.1
  25.0 0.3 shard_map.58
  25.3 0.3 collective-permute-done.16.refs_7_
  25.6 0.4 collective-permute-start.11
  26.0 0.0 collective-permute-done.13.refs_16_
  26.0 1.5 %collective-permute-start.15 = (bf16[2,8,2,16,128]{4,3,2,1,0:T(8,128)(2,1)S(1)}, bf16[2,8,2,16,128]{4,3,2,1,0:T(8,128)(2,1)S(1)}, u32[]{:S(2)}, u32[]{:S(2)}) collective-permute-start(bf16[2,8,2,16,128]{4,3,2,1,0:T(8,128)(2,1)S(1)} %collective-permute-done.14.refs_5_), channel_id=1, source_target_pairs={{0,1},{1,0},{2,3},{3,2},{4,5},{5,4},{6,7},{7,6},{8,9},{9,8},{10,11... | collective-permute-start | bytes 393224 | tf_op jit(solution)/shard_map/ppermute | solution.py:333
  27.5 0.0 collective-permute-done.12.refs_15_
  27.5 0.5 %collective-permute-start.17 = (bf16[2,8,2,16,128]{4,3,2,1,0:T(8,128)(2,1)S(1)}, bf16[2,8,2,16,128]{4,3,2,1,0:T(8,128)(2,1)S(1)}, u32[]{:S(2)}, u32[]{:S(2)}) collective-permute-start(bf16[2,8,2,16,128]{4,3,2,1,0:T(8,128)(2,1)S(1)} %collective-permute-done.16.refs_7_), channel_id=1, source_target_pairs={{0,1},{1,0},{2,3},{3,2},{4,5},{5,4},{6,7},{7,6},{8,9},{9,8},{10,11... | collective-permute-start | bytes 393224 | tf_op jit(solution)/shard_map/ppermute | solution.py:333
  28.0 0.0 copy-done.4
  28.1 0.0 collective-permute-done.11.refs_14_
  28.1 1.6 %collective-permute-start.4 = (bf16[2,8,2,16,128]{4,3,2,1,0:T(8,128)(2,1)S(1)}, bf16[2,8,2,16,128]{4,3,2,1,0:T(8,128)(2,1)S(1)}, u32[]{:S(2)}, u32[]{:S(2)}) collective-permute-start(bf16[2,8,2,16,128]{4,3,2,1,0:T(8,128)(2,1)S(1)} %collective-permute-done.3.refs_5_), channel_id=1, source_target_pairs={{0,1},{1,0},{2,3},{3,2},{4,5},{5,4},{6,7},{7,6},{8,9},{9,8},{10,11... | collective-permute-start | bytes 393224 | tf_op jit(solution)/shard_map/ppermute | solution.py:333
  29.6 7.9 %collective-permute-done.15.refs_6_ = bf16[2,8,2,16,128]{4,3,2,1,0:T(8,128)(2,1)S(1)} collective-permute-done((bf16[2,8,2,16,128]{4,3,2,1,0:T(8,128)(2,1)S(1)}, bf16[2,8,2,16,128]{4,3,2,1,0:T(8,128)(2,1)S(1)}, u32[]{:S(2)}, u32[]{:S(2)}) %collective-permute-start.15) | collective-permute-done | bytes 131104 | tf_op jit(solution)/shard_map/ppermute | solution.py:333
  37.5 1.5 %collective-permute-start.6 = (bf16[2,8,2,16,128]{4,3,2,1,0:T(8,128)(2,1)S(1)}, bf16[2,8,2,16,128]{4,3,2,1,0:T(8,128)(2,1)S(1)}, u32[]{:S(2)}, u32[]{:S(2)}) collective-permute-start(bf16[2,8,2,16,128]{4,3,2,1,0:T(8,128)(2,1)S(1)} %collective-permute-done.5.refs_7_), channel_id=1, source_target_pairs={{0,1},{1,0},{2,3},{3,2},{4,5},{5,4},{6,7},{7,6},{8,9},{9,8},{10,11... | collective-permute-start | bytes 393224 | tf_op jit(solution)/shard_map/ppermute | solution.py:333
  39.0 1.3 %collective-permute-done.17.refs_8_ = bf16[2,8,2,16,128]{4,3,2,1,0:T(8,128)(2,1)S(1)} collective-permute-done((bf16[2,8,2,16,128]{4,3,2,1,0:T(8,128)(2,1)S(1)}, bf16[2,8,2,16,128]{4,3,2,1,0:T(8,128)(2,1)S(1)}, u32[]{:S(2)}, u32[]{:S(2)}) %collective-permute-start.17) | collective-permute-done | bytes 131104 | tf_op jit(solution)/shard_map/ppermute | solution.py:333
  40.4 0.0 collective-permute-done.refs_2_
  40.4 0.0 collective-permute-done.2.refs_4_
  40.4 4.6 %shard_map.59.refs_24_ = f32[2,1024,128]{2,1,0:T(8,128)S(1)} custom-call(s32[16]{0:T(128)S(1)} %fusion.2.refs_0_, bf16[2,16,2,16,128]{4,3,2,1,0:T(8,128)(2,1)S(1)} %get-tuple-element.18.refs_1_, bf16[2,16,2,16,128]{4,3,2,1,0:T(8,128)(2,1)S(1)} %collective-permute-done.refs_2_, bf16[2,16,2,16,128]{4,3,2,1,0:T(8,128)(2,1)S(1)} %collective-permute-done.1.refs_3_, ...), custom_call_target="tpu_custom_call" | custom-call | flops 3000000000 | bytes 8000000 | tf_op jit(solution)/shard_map/pallas_call | solution.py:306
  45.0 0.0 collective-permute-done.4.refs_6_
  45.0 0.5 %collective-permute-done.6.refs_8_ = bf16[2,8,2,16,128]{4,3,2,1,0:T(8,128)(2,1)S(1)} collective-permute-done((bf16[2,8,2,16,128]{4,3,2,1,0:T(8,128)(2,1)S(1)}, bf16[2,8,2,16,128]{4,3,2,1,0:T(8,128)(2,1)S(1)}, u32[]{:S(2)}, u32[]{:S(2)}) %collective-permute-start.6) | collective-permute-done | bytes 131104 | tf_op jit(solution)/shard_map/ppermute | solution.py:333
  45.5 5.6 %shard_map.60 = f32[2,2,1024,128]{3,2,1,0:T(8,128)} custom-call(s32[16]{0:T(128)S(1)} %fusion.2.refs_0_, bf16[2,16,2,16,128]{4,3,2,1,0:T(8,128)(2,1)S(1)} %get-tuple-element.18.refs_1_, bf16[2,16,2,16,128]{4,3,2,1,0:T(8,128)(2,1)S(1)} %collective-permute-done.refs_2_, bf16[2,16,2,16,128]{4,3,2,1,0:T(8,128)(2,1)S(1)} %collective-permute-done.1.refs_3_, ...), custom_call_target="tpu_custom_call" | custom-call | flops 3000000000 | bytes 8000000 | tf_op jit(solution)/shard_map/pallas_call | solution.py:306
  (1 shorter events, 0.0 us)
Async XLA Ops:
  0.0 0.9 %copy-start.2 = (bf16[2,2,32768]{2,1,0:T(2,128)(2,1)S(1)}, bf16[2,2,32768]{2,1,0:T(2,128)(2,1)}, u32[]{:S(2)}) copy-start(bf16[2,2,32768]{2,1,0:T(2,128)(2,1)} %filters.1) | copy-start | bytes 786436
  1.0 23.9 %copy-start.3 = (s32[16]{0:T(128)S(1)}, s32[16]{0:T(128)}, u32[]{:S(2)}) copy-start(s32[16]{0:T(128)} %param.8) | copy-start | bytes 196
  1.0 27.1 %copy-start.4 = (s32[16]{0:T(128)S(1)}, s32[16]{0:T(128)}, u32[]{:S(2)}) copy-start(s32[16]{0:T(128)} %param.7) | copy-start | bytes 196
  1.2 8.6 %collective-permute-start.10 = (bf16[2,2,128,128]{3,2,1,0:T(8,128)(2,1)S(1)}, bf16[2,2,128,128]{3,2,1,0:T(8,128)(2,1)S(1)}, u32[]{:S(2)}, u32[]{:S(2)}) collective-permute-start(bf16[2,2,128,128]{3,2,1,0:T(8,128)(2,1)S(1)} %shard_map.57.refs_9_), channel_id=1, source_target_pairs={{0,8},{8,0},{16,24},{24,16},{1,9},{9,1},{17,25},{25,17},{2,10},{10... | collective-permute-start | bytes 393224 | tf_op jit(solution)/shard_map/ppermute | solution.py:333
  1.8 9.8 %collective-permute-start.9 = (bf16[2,2,128,128]{3,2,1,0:T(8,128)(2,1)S(1)}, bf16[2,2,128,128]{3,2,1,0:T(8,128)(2,1)S(1)}, u32[]{:S(2)}, u32[]{:S(2)}) collective-permute-start(bf16[2,2,128,128]{3,2,1,0:T(8,128)(2,1)S(1)} %shard_map.57.refs_9_), channel_id=1, source_target_pairs={{0,6},{2,4},{4,2},{6,0},{1,7},{3,5},{5,3},{7,1},{8,14},{10,12},{12... | collective-permute-start | bytes 393224 | tf_op jit(solution)/shard_map/ppermute | solution.py:333
  6.4 11.7 %collective-permute-start.8 = (bf16[2,2,128,128]{3,2,1,0:T(8,128)(2,1)S(1)}, bf16[2,2,128,128]{3,2,1,0:T(8,128)(2,1)S(1)}, u32[]{:S(2)}, u32[]{:S(2)}) collective-permute-start(bf16[2,2,128,128]{3,2,1,0:T(8,128)(2,1)S(1)} %shard_map.57.refs_9_), channel_id=1, source_target_pairs={{0,4},{2,6},{4,0},{6,2},{1,5},{3,7},{5,1},{7,3},{8,12},{10,14},{12... | collective-permute-start | bytes 393224 | tf_op jit(solution)/shard_map/ppermute | solution.py:333
  6.4 13.3 %collective-permute-start.7 = (bf16[2,2,128,128]{3,2,1,0:T(8,128)(2,1)S(1)}, bf16[2,2,128,128]{3,2,1,0:T(8,128)(2,1)S(1)}, u32[]{:S(2)}, u32[]{:S(2)}) collective-permute-start(bf16[2,2,128,128]{3,2,1,0:T(8,128)(2,1)S(1)} %shard_map.57.refs_9_), channel_id=1, source_target_pairs={{0,2},{2,0},{4,6},{6,4},{1,3},{3,1},{5,7},{7,5},{8,10},{10,8},{12,... | collective-permute-start | bytes 393224 | tf_op jit(solution)/shard_map/ppermute | solution.py:333
  7.1 1.2 %copy-start = (bf16[2,64,4096]{2,1,0:T(8,128)(2,1)S(1)}, bf16[2,64,4096]{2,1,0:T(8,128)(2,1)}, u32[]{:S(2)}) copy-start(bf16[2,64,4096]{2,1,0:T(8,128)(2,1)} %echoes.1) | copy-start | bytes 3145732
  8.3 16.7 %copy-start.1 = (bf16[3328,256]{1,0:T(8,128)(2,1)S(1)}, bf16[3328,256]{1,0:T(8,128)(2,1)}, u32[]{:S(2)}) copy-start(bf16[3328,256]{1,0:T(8,128)(2,1)} %constant.48.clone.dots.refs_22_) | copy-start | bytes 5111812
  8.9 14.5 %collective-permute-start.1 = (bf16[2,16,2,16,128]{4,3,2,1,0:T(8,128)(2,1)S(1)}, bf16[2,16,2,16,128]{4,3,2,1,0:T(8,128)(2,1)S(1)}, u32[]{:S(2)}, u32[]{:S(2)}) collective-permute-start(bf16[2,16,2,16,128]{4,3,2,1,0:T(8,128)(2,1)S(1)} %get-tuple-element.19), channel_id=1, source_target_pairs={{0,8},{8,0},{16,24},{24,16},{1,9},{9,1},{17,25},{25,17},{2,10},{10... | collective-permute-start | bytes 786440 | tf_op jit(solution)/shard_map/ppermute | solution.py:333
  9.8 10.1 %collective-permute-start.3 = (bf16[2,8,2,16,128]{4,3,2,1,0:T(8,128)(2,1)S(1)}, bf16[2,8,2,16,128]{4,3,2,1,0:T(8,128)(2,1)S(1)}, u32[]{:S(2)}, u32[]{:S(2)}) collective-permute-start(bf16[2,8,2,16,128]{4,3,2,1,0:T(8,128)(2,1)S(1)} %get-tuple-element.20), channel_id=1, source_target_pairs={{0,16},{8,24},{16,0},{24,8},{1,17},{9,25},{17,1},{25,9},{2,18},{10... | collective-permute-start | bytes 393224 | tf_op jit(solution)/shard_map/ppermute | solution.py:333
  11.5 9.9 %collective-permute-start.5 = (bf16[2,8,2,16,128]{4,3,2,1,0:T(8,128)(2,1)S(1)}, bf16[2,8,2,16,128]{4,3,2,1,0:T(8,128)(2,1)S(1)}, u32[]{:S(2)}, u32[]{:S(2)}) collective-permute-start(bf16[2,8,2,16,128]{4,3,2,1,0:T(8,128)(2,1)S(1)} %get-tuple-element.21), channel_id=1, source_target_pairs={{0,24},{8,16},{16,8},{24,0},{1,25},{9,17},{17,9},{25,1},{2,26},{10... | collective-permute-start | bytes 393224 | tf_op jit(solution)/shard_map/ppermute | solution.py:333
  18.1 5.3 %collective-permute-start.14 = (bf16[2,8,2,16,128]{4,3,2,1,0:T(8,128)(2,1)S(1)}, bf16[2,8,2,16,128]{4,3,2,1,0:T(8,128)(2,1)S(1)}, u32[]{:S(2)}, u32[]{:S(2)}) collective-permute-start(bf16[2,8,2,16,128]{4,3,2,1,0:T(8,128)(2,1)S(1)} %get-tuple-element.25), channel_id=1, source_target_pairs={{0,16},{8,24},{16,0},{24,8},{1,17},{9,25},{17,1},{25,9},{2,18},{10... | collective-permute-start | bytes 393224 | tf_op jit(solution)/shard_map/ppermute | solution.py:333
  19.8 5.9 %collective-permute-start.16 = (bf16[2,8,2,16,128]{4,3,2,1,0:T(8,128)(2,1)S(1)}, bf16[2,8,2,16,128]{4,3,2,1,0:T(8,128)(2,1)S(1)}, u32[]{:S(2)}, u32[]{:S(2)}) collective-permute-start(bf16[2,8,2,16,128]{4,3,2,1,0:T(8,128)(2,1)S(1)} %get-tuple-element.26), channel_id=1, source_target_pairs={{0,24},{8,16},{16,8},{24,0},{1,25},{9,17},{17,9},{25,1},{2,26},{10... | collective-permute-start | bytes 393224 | tf_op jit(solution)/shard_map/ppermute | solution.py:333
  19.9 20.5 %collective-permute-start = (bf16[2,16,2,16,128]{4,3,2,1,0:T(8,128)(2,1)S(1)}, bf16[2,16,2,16,128]{4,3,2,1,0:T(8,128)(2,1)S(1)}, u32[]{:S(2)}, u32[]{:S(2)}) collective-permute-start(bf16[2,16,2,16,128]{4,3,2,1,0:T(8,128)(2,1)S(1)} %get-tuple-element.18.refs_1_), channel_id=1, source_target_pairs={{0,1},{1,0},{2,3},{3,2},{4,5},{5,4},{6,7},{7,6},{8,9},{9,8},{10,11... | collective-permute-start | bytes 786440 | tf_op jit(solution)/shard_map/ppermute | solution.py:333
  21.4 4.6 %collective-permute-start.13 = (bf16[2,2,128,128]{3,2,1,0:T(8,128)(2,1)S(1)}, bf16[2,2,128,128]{3,2,1,0:T(8,128)(2,1)S(1)}, u32[]{:S(2)}, u32[]{:S(2)}) collective-permute-start(bf16[2,2,128,128]{3,2,1,0:T(8,128)(2,1)S(1)} %collective-permute-done.9.refs_12_), channel_id=1, source_target_pairs={{0,8},{8,0},{16,24},{24,16},{1,9},{9,1},{17,25},{25,17},{2,10},{10... | collective-permute-start | bytes 393224 | tf_op jit(solution)/shard_map/ppermute | solution.py:333
  23.4 4.1 %collective-permute-start.12 = (bf16[2,2,128,128]{3,2,1,0:T(8,128)(2,1)S(1)}, bf16[2,2,128,128]{3,2,1,0:T(8,128)(2,1)S(1)}, u32[]{:S(2)}, u32[]{:S(2)}) collective-permute-start(bf16[2,2,128,128]{3,2,1,0:T(8,128)(2,1)S(1)} %collective-permute-done.8.refs_11_), channel_id=1, source_target_pairs={{0,8},{8,0},{16,24},{24,16},{1,9},{9,1},{17,25},{25,17},{2,10},{10... | collective-permute-start | bytes 393224 | tf_op jit(solution)/shard_map/ppermute | solution.py:333
  23.4 17.0 %collective-permute-start.2 = (bf16[2,16,2,16,128]{4,3,2,1,0:T(8,128)(2,1)S(1)}, bf16[2,16,2,16,128]{4,3,2,1,0:T(8,128)(2,1)S(1)}, u32[]{:S(2)}, u32[]{:S(2)}) collective-permute-start(bf16[2,16,2,16,128]{4,3,2,1,0:T(8,128)(2,1)S(1)} %collective-permute-done.1.refs_3_), channel_id=1, source_target_pairs={{0,1},{1,0},{2,3},{3,2},{4,5},{5,4},{6,7},{7,6},{8,9},{9,8},{10,11... | collective-permute-start | bytes 786440 | tf_op jit(solution)/shard_map/ppermute | solution.py:333
  25.6 2.4 %collective-permute-start.11 = (bf16[2,2,128,128]{3,2,1,0:T(8,128)(2,1)S(1)}, bf16[2,2,128,128]{3,2,1,0:T(8,128)(2,1)S(1)}, u32[]{:S(2)}, u32[]{:S(2)}) collective-permute-start(bf16[2,2,128,128]{3,2,1,0:T(8,128)(2,1)S(1)} %collective-permute-done.7.refs_10_), channel_id=1, source_target_pairs={{0,8},{8,0},{16,24},{24,16},{1,9},{9,1},{17,25},{25,17},{2,10},{10... | collective-permute-start | bytes 393224 | tf_op jit(solution)/shard_map/ppermute | solution.py:333
  26.0 11.5 %collective-permute-start.15 = (bf16[2,8,2,16,128]{4,3,2,1,0:T(8,128)(2,1)S(1)}, bf16[2,8,2,16,128]{4,3,2,1,0:T(8,128)(2,1)S(1)}, u32[]{:S(2)}, u32[]{:S(2)}) collective-permute-start(bf16[2,8,2,16,128]{4,3,2,1,0:T(8,128)(2,1)S(1)} %collective-permute-done.14.refs_5_), channel_id=1, source_target_pairs={{0,1},{1,0},{2,3},{3,2},{4,5},{5,4},{6,7},{7,6},{8,9},{9,8},{10,11... | collective-permute-start | bytes 393224 | tf_op jit(solution)/shard_map/ppermute | solution.py:333
  27.5 12.9 %collective-permute-start.17 = (bf16[2,8,2,16,128]{4,3,2,1,0:T(8,128)(2,1)S(1)}, bf16[2,8,2,16,128]{4,3,2,1,0:T(8,128)(2,1)S(1)}, u32[]{:S(2)}, u32[]{:S(2)}) collective-permute-start(bf16[2,8,2,16,128]{4,3,2,1,0:T(8,128)(2,1)S(1)} %collective-permute-done.16.refs_7_), channel_id=1, source_target_pairs={{0,1},{1,0},{2,3},{3,2},{4,5},{5,4},{6,7},{7,6},{8,9},{9,8},{10,11... | collective-permute-start | bytes 393224 | tf_op jit(solution)/shard_map/ppermute | solution.py:333
  28.1 16.9 %collective-permute-start.4 = (bf16[2,8,2,16,128]{4,3,2,1,0:T(8,128)(2,1)S(1)}, bf16[2,8,2,16,128]{4,3,2,1,0:T(8,128)(2,1)S(1)}, u32[]{:S(2)}, u32[]{:S(2)}) collective-permute-start(bf16[2,8,2,16,128]{4,3,2,1,0:T(8,128)(2,1)S(1)} %collective-permute-done.3.refs_5_), channel_id=1, source_target_pairs={{0,1},{1,0},{2,3},{3,2},{4,5},{5,4},{6,7},{7,6},{8,9},{9,8},{10,11... | collective-permute-start | bytes 393224 | tf_op jit(solution)/shard_map/ppermute | solution.py:333
  37.5 8.0 %collective-permute-start.6 = (bf16[2,8,2,16,128]{4,3,2,1,0:T(8,128)(2,1)S(1)}, bf16[2,8,2,16,128]{4,3,2,1,0:T(8,128)(2,1)S(1)}, u32[]{:S(2)}, u32[]{:S(2)}) collective-permute-start(bf16[2,8,2,16,128]{4,3,2,1,0:T(8,128)(2,1)S(1)} %collective-permute-done.5.refs_7_), channel_id=1, source_target_pairs={{0,1},{1,0},{2,3},{3,2},{4,5},{5,4},{6,7},{7,6},{8,9},{9,8},{10,11... | collective-permute-start | bytes 393224 | tf_op jit(solution)/shard_map/ppermute | solution.py:333

commit v3 on v2

--- a/solution.py
+++ b/solution.py
@@ -124,6 +124,40 @@
     )(dots)
 
 
+def phase_kernel(total, slow, numbers, slow_cos, slow_sin, twist, out, slow_ramp, ids, sem):
+    fetch = pltpu.make_async_copy(numbers, ids, sem)
+    fetch.start()
+    slow_ramp[0] = slow_cos[...].T
+    slow_ramp[1] = slow_sin[...].T
+    fetch.wait()
+    for r in range(total):
+        back = lax.rem(LANES - ids[total + r], LANES)
+        for c in range(0, slow, 64):
+            rows_c = slice(c, c + 64)
+            tw_re = pltpu.roll(twist[rows_c, :LANES], back, 1)
+            tw_im = pltpu.roll(twist[rows_c, LANES:], back, 1)
+            u_re, u_im = slow_ramp[0, rows_c, r : r + 1], slow_ramp[1, rows_c, r : r + 1]
+            out[r, rows_c, :LANES] = tw_re * u_re - tw_im * u_im
+            out[r, rows_c, LANES:] = tw_re * u_im + tw_im * u_re
+
+
+def phases(numbers, slow_cos, slow_sin, twist, total, slow):
+    vm = pl.BlockSpec(memory_space=pltpu.VMEM)
+    return pl.pallas_call(
+        functools.partial(phase_kernel, total, slow),
+        in_specs=[vm] * 4,
+        out_specs=vm,
+        out_shape=jax.ShapeDtypeStruct((total, slow, 2 * LANES), jnp.float32),
+        scratch_shapes=[
+            pltpu.VMEM((2, slow, total), jnp.float32),
+            pltpu.SMEM(numbers.shape, jnp.int32),
+            pltpu.SemaphoreType.DMA,
+        ],
+        compiler_params=pltpu.CompilerParams(vmem_limit_bytes=4 * 1024 * 1024),
+        cost_estimate=pl.CostEstimate(flops=10**6, bytes_accessed=2 * 10**6, transcendentals=0),
+    )(numbers, slow_cos, slow_sin, twist)
+
+
 def turn_kernel(filters, out, turned):
     core = lax.axis_index("turn") % 2
     slabs = filters.shape[1]
@@ -157,16 +191,16 @@
     slabs, blocks = refs[0], refs[1 : 1 + sources]
     own = refs[1 + sources : 1 + sources + pieces]
     other = refs[1 + sources + pieces : 1 + sources + 2 * pieces]
-    slow_cos, slow_sin, fast_cos, fast_sin, first_dots_ref, dots, twist = refs[1 + sources + 2 * pieces :][:7]
-    rest = refs[8 + sources + 2 * pieces :]
+    phase, first_dots_ref, dots, twist = refs[1 + sources + 2 * pieces :][:4]
+    rest = refs[5 + sources + 2 * pieces :]
     images, out = rest[:earlier], rest[earlier]
-    s1, y1, s2, y2, s3, y3, s4, slow_ramp, filt, slab_ids, slab_sem = rest[earlier + 1 :][:11]
-    fetch = pltpu.make_async_copy(slabs, slab_ids, slab_sem)
+    s1, y1, s2, y2, s3, y3, s4, filt, ids, slab_sem = rest[earlier + 1 :][:10]
+    fetch = pltpu.make_async_copy(slabs, ids, slab_sem)
     fetch.start()
     tile = out
     writes = []
     if earlier:
-        tile, write_sem = rest[earlier + 12 :]
+        tile, write_sem = rest[earlier + 11 :]
         for k, source in enumerate((*images, tile)):
             for p in range(2):
                 writes.append(pltpu.make_async_copy(source.at[p], out.at[p, k], write_sem.at[2 * k + p]))
@@ -177,8 +211,6 @@
     for k in range(pieces):
         filt[core, k * per_zone : (k + 1) * per_zone] = own[k][...]
         filt[1 - core, k * per_zone : (k + 1) * per_zone] = other[k][...]
-    slow_ramp[0] = slow_cos[...].T
-    slow_ramp[1] = slow_sin[...].T
     half = slow // 2
     wide = 2 * LANES
     first = [[first_dots_ref.at[pl.ds((2 * e + k) * slow, slow)] for k in range(2)] for e in range(2)]
@@ -223,15 +255,14 @@
     def respond(pair):
         for i in range(2):
             r = row0 + 2 * pair + i
-            slab = slab_ids[r]
-            v_re, v_im = fast_cos[r : r + 1], fast_sin[r : r + 1]
+            slab = ids[r]
             for part in range(2):
                 rows_s = slice(i * slow + part * half, i * slow + (part + 1) * half)
                 re, im = s2[pair, rows_s, :LANES], s2[pair, rows_s, LANES:]
                 h_re = filt[part, slab, 0].astype(jnp.float32)
                 h_im = filt[part, slab, 1].astype(jnp.float32)
                 re, im = re * h_re - im * h_im, re * h_im + im * h_re
-                (rh, rl), (ih, il) = split(re * v_re - im * v_im), split(re * v_im + im * v_re)
+                (rh, rl), (ih, il) = split(re), split(im)
                 y2[pair, i, part * half : (part + 1) * half] = jnp.concatenate([rh, ih, rl, il], 1)
 
     def back_twist(pair):
@@ -243,10 +274,8 @@
                 rows_c = slice(part * half, (part + 1) * half)
                 rows_s = slice(i * slow + part * half, i * slow + (part + 1) * half)
                 re, im = s3[pair, rows_s, :LANES], s3[pair, rows_s, LANES:]
-                tw_re, tw_im = twist[rows_c, :LANES], twist[rows_c, LANES:]
-                re, im = re * tw_re - im * tw_im, re * tw_im + im * tw_re
-                u_re, u_im = slow_ramp[0, rows_c, r : r + 1], slow_ramp[1, rows_c, r : r + 1]
-                parts.append((re * u_re - im * u_im, re * u_im + im * u_re))
+                tw_re, tw_im = phase[r, rows_c, :LANES], phase[r, rows_c, LANES:]
+                parts.append((re * tw_re - im * tw_im, re * tw_im + im * tw_re))
             (a_re, a_im), (b_re, b_im) = parts
             for e, (re, im) in enumerate(((a_re + b_re, a_im + b_im), (a_re - b_re, a_im - b_im))):
                 (rh, rl), (ih, il) = split(re), split(im)
@@ -264,12 +293,12 @@
         count = out_slow // 2
         for i in range(2):
             r = (row0 + 2 * pair + i) % 8
+            turned = ids[ids.shape[0] // 2 + row0 + 2 * pair + i]
             for e in range(2):
+                lanes = pltpu.roll(s4[pair, e, :, i * LANES : (i + 1) * LANES], turned, 1)
                 for p in range(2):
                     for q in range(0, count, 8):
-                        tile[p, pl.ds((2 * q + e) * 8 + r, 8, stride=16), :] = s4[
-                            pair, e, p * count + q : p * count + q + 8, i * LANES : (i + 1) * LANES
-                        ]
+                        tile[p, pl.ds((2 * q + e) * 8 + r, 8, stride=16), :] = lanes[p * count + q : p * count + q + 8]
 
     steps = [
         first_dots,
@@ -293,7 +322,7 @@
         write.wait()
 
 
-def focus(blocks, bases, own, other, ramps, tables, slabs, images, rows, row0, total, slow, out_slow, final):
+def focus(blocks, bases, own, other, tables, slabs, images, rows, row0, total, slow, out_slow, final):
     slots, pieces = rows // 2, len(own)
 
     def full(a):
@@ -301,7 +330,7 @@
 
     image = (2, out_slow * 8, LANES)
     shape = (2, total // 8, *image[1:]) if final else image
-    operands = [slabs, *blocks, *own, *other, *ramps, *tables, *images]
+    operands = [slabs, *blocks, *own, *other, *tables, *images]
     extra = [pltpu.VMEM(image, jnp.float32), pltpu.SemaphoreType.DMA((total // 4,))] if final else []
     return pl.pallas_call(
         functools.partial(focus_kernel, tuple(bases), pieces, len(images), rows, row0, slow, out_slow),
@@ -317,7 +346,6 @@
             pltpu.VMEM((slots, 2 * slow, 2 * LANES), jnp.float32),
             pltpu.VMEM((slots, 2, 2, slow, 2 * LANES), jnp.bfloat16),
             pltpu.VMEM((slots, 2, out_slow, 2 * LANES), jnp.float32),
-            pltpu.VMEM((2, slow, total), jnp.float32),
             pltpu.VMEM((2, pieces * own[0].shape[0], *own[0].shape[1:]), jnp.bfloat16),
             pltpu.SMEM(slabs.shape, jnp.int32),
             pltpu.SemaphoreType.DMA,
@@ -347,16 +375,17 @@
     echoes, zone, behind = lax.optimization_barrier((echoes, zone, behind))
     dots = jnp.asarray(tables(length, sources, length // strips))
 
-    jobs = [[(0, 0, total), (1, 0, total)], []]
+    jobs = [[(0, 0, total)], [(1, 0, total)], []]
     starts = [sum(CHUNKS[:k]) for k in range(len(CHUNKS))]
     for k, rows in enumerate(CHUNKS):
-        jobs[min(k, 1)] += [(flip, starts[k], rows) for flip in range(2, turns)]
-    sent = pack(echoes, jobs[0], total, 8 * 10**6)
-    more = pack(echoes, jobs[1], total, 2 * 10**6)
+        jobs[min(k + 1, 2)] += [(flip, starts[k], rows) for flip in range(2, turns)]
+    sent = []
+    for k, cost in enumerate((4 * 10**6, 4 * 10**6, 2 * 10**6)):
+        sent += pack(echoes, jobs[k], total, cost)
     half = turn_filters(filters)
     first, twist = order_tables(dots, width, strips, slow)
     held = {}
-    for (flip, start, rows), block in zip(jobs[0] + jobs[1], [*sent, *more]):
+    for (flip, start, rows), block in zip(sum(jobs, []), sent):
         if flip:
             block = swap(block, "turn", flip)
         for ds in range(strips):
@@ -370,9 +399,9 @@
     c = jnp.arange(slow, dtype=jnp.int32)[None, :]
     offset = (shifts + behind) & (length - 1)
     c_angle = (offset[:, None] * c & (length - 1)).astype(jnp.float32) * (2.0 * math.pi / length)
-    d = jnp.arange(LANES, dtype=jnp.int32)[None, :]
-    d_angle = (d * shifts[:, None] & (LANES - 1)).astype(jnp.float32) * (2.0 * math.pi / LANES)
-    ramps = (jnp.cos(c_angle), -jnp.sin(c_angle), jnp.cos(d_angle), -jnp.sin(d_angle))
+    slow_ramp = (jnp.cos(c_angle), -jnp.sin(c_angle))
+    numbers = jnp.concatenate([local_slab, shifts & (LANES - 1)])
+    phase = phases(numbers, *slow_ramp, twist, total, slow)
 
     images = []
     for k, (start, rows) in enumerate(zip(starts, CHUNKS)):
@@ -383,7 +412,7 @@
             bases.append(start if whole else 0)
         final = k == len(CHUNKS) - 1
         image = focus(
-            blocks, bases, own, other, ramps, (first, dots, twist), local_slab, images, rows, start, total, slow, out_slow, final
+            blocks, bases, own, other, (phase, first, dots, twist), numbers, images, rows, start, total, slow, out_slow, final
         )
         images.append(image)
     image = image.reshape(2, total // 8, out_slow, 8, LANES).transpose(0, 1, 3, 2, 4)

time: 51.3 us -> 53 us (1.033)
  Pallas kernels: 11.6 us -> 13.8 us
  other arithmetic: 0.94 us -> 0.24 us
  starting transfers between devices: 18.2 us -> 17.5 us
    pallas_call x0 -> x1, Pallas kernels: none -> 2.84 us  [phases(): pl.pallas_call(functools.partial(phase_kernel, total, slow), in_specs=[vm...]
    ppermute x18, starting transfers between devices: 18.2 us -> 17.5 us  [swap(): return lax.ppermute(value, axis, [(a, a ^ flip) for a in range(size)])]
    and x1, other arithmetic: 0.66 us -> 0.01 us  [per_device(): offset = shifts + behind & length - 1]
    pallas_call x2, Pallas kernels: 10.2 us -> 9.61 us  [focus(): pl.pallas_call(functools.partial(focus_kernel, tuple(bases), pieces, len(...]
  transfers between devices with their start and end apart: 18 -> 18, of which waited for: 6 -> 6; matrix products, arithmetic and copies ran while one was open for 2% -> 0% of each run, Pallas kernels for 11% -> 16%
where the time goes in v3:
time: 53 us; the launch traced here: 52.4 us
  waiting for transfers between devices  18.5 us (35%)
  starting transfers between devices  17.5 us (33%)
  Pallas kernels  13.8 us (26%)
  local copies, waits for them, and re-layouts  2.18 us (4%)
    ppermute x18, waiting for transfers between devices, swap(): return lax.ppermute(value, axis, [(a, a ^ flip) for a in range(size)])  18.5 us
    ppermute x18, starting transfers between devices, swap(): return lax.ppermute(value, axis, [(a, a ^ flip) for a in range(size)])  17.5 us
    pallas_call x2, Pallas kernels, focus(): pl.pallas_call(functools.partial(focus_kernel, tuple(bases), pieces, len(...  9.61 us
    pallas_call x1, Pallas kernels, phases(): pl.pallas_call(functools.partial(phase_kernel, total, slow), in_specs=[vm...  2.84 us
    unnamed x10, local copies, waits for them, and re-layouts  2.18 us
  transfers between devices with their start and end apart: 18, of which 6 were waited for; matrix products, arithmetic and copies ran while one was open for 0% of the time, Pallas kernels for 16%

profile of v3, /device:TPU:0, one launch (start us, length us, event | category | flops | bytes accessed | tf_op | source)
XLA Modules:
  0.0 52.4 jit_solution(15702387008589385353)
XLA Ops:
  0.0 0.0 copy-start.2
  0.0 0.9 %copy-done.2 = bf16[2,2,32768]{2,1,0:T(2,128)(2,1)S(1)} copy-done((bf16[2,2,32768]{2,1,0:T(2,128)(2,1)S(1)}, bf16[2,2,32768]{2,1,0:T(2,128)(2,1)}, u32[]{:S(2)}) %copy-start.2) | copy-done | bytes 262168
  1.0 0.0 copy-start.3
  1.0 0.0 copy-start.4
  1.0 0.3 shard_map.58.refs_9_
  1.2 0.6 %collective-permute-start.10 = (bf16[2,2,128,128]{3,2,1,0:T(8,128)(2,1)S(1)}, bf16[2,2,128,128]{3,2,1,0:T(8,128)(2,1)S(1)}, u32[]{:S(2)}, u32[]{:S(2)}) collective-permute-start(bf16[2,2,128,128]{3,2,1,0:T(8,128)(2,1)S(1)} %shard_map.58.refs_9_), channel_id=1, source_target_pairs={{0,8},{8,0},{16,24},{24,16},{1,9},{9,1},{17,25},{25,17},{2,10},{10... | collective-permute-start | bytes 393224 | tf_op jit(solution)/shard_map/ppermute | solution.py:361
  1.8 4.7 %collective-permute-start.9 = (bf16[2,2,128,128]{3,2,1,0:T(8,128)(2,1)S(1)}, bf16[2,2,128,128]{3,2,1,0:T(8,128)(2,1)S(1)}, u32[]{:S(2)}, u32[]{:S(2)}) collective-permute-start(bf16[2,2,128,128]{3,2,1,0:T(8,128)(2,1)S(1)} %shard_map.58.refs_9_), channel_id=1, source_target_pairs={{0,6},{2,4},{4,2},{6,0},{1,7},{3,5},{5,3},{7,1},{8,14},{10,12},{12... | collective-permute-start | bytes 393224 | tf_op jit(solution)/shard_map/ppermute | solution.py:361
  6.4 0.0 collective-permute-start.8
  6.4 0.6 %collective-permute-start.7 = (bf16[2,2,128,128]{3,2,1,0:T(8,128)(2,1)S(1)}, bf16[2,2,128,128]{3,2,1,0:T(8,128)(2,1)S(1)}, u32[]{:S(2)}, u32[]{:S(2)}) collective-permute-start(bf16[2,2,128,128]{3,2,1,0:T(8,128)(2,1)S(1)} %shard_map.58.refs_9_), channel_id=1, source_target_pairs={{0,2},{2,0},{4,6},{6,4},{1,3},{3,1},{5,7},{7,5},{8,10},{10,8},{12,... | collective-permute-start | bytes 393224 | tf_op jit(solution)/shard_map/ppermute | solution.py:361
  7.1 0.0 copy-start
  7.1 1.2 %copy-done = bf16[2,64,4096]{2,1,0:T(8,128)(2,1)S(1)} copy-done((bf16[2,64,4096]{2,1,0:T(8,128)(2,1)S(1)}, bf16[2,64,4096]{2,1,0:T(8,128)(2,1)}, u32[]{:S(2)}) %copy-start) | copy-done | bytes 1048600
  8.3 0.0 copy-start.1
  8.3 0.2 shard_map.57
  8.5 1.7 %collective-permute-start.3 = (bf16[2,8,2,16,128]{4,3,2,1,0:T(8,128)(2,1)S(1)}, bf16[2,8,2,16,128]{4,3,2,1,0:T(8,128)(2,1)S(1)}, u32[]{:S(2)}, u32[]{:S(2)}) collective-permute-start(bf16[2,8,2,16,128]{4,3,2,1,0:T(8,128)(2,1)S(1)} %get-tuple-element.18), channel_id=1, source_target_pairs={{0,16},{8,24},{16,0},{24,8},{1,17},{9,25},{17,1},{25,9},{2,18},{10... | collective-permute-start | bytes 393224 | tf_op jit(solution)/shard_map/ppermute | solution.py:361
  10.2 0.4 shard_map.56
  10.6 0.0 collective-permute-done.10.refs_13_
  10.6 0.1 collective-permute-start.5
  10.7 0.2 collective-permute-done.9.refs_12_
  10.9 0.3 collective-permute-start.1
  11.1 0.0 copy-done.3
  11.1 0.2 shard_map.55.refs_1_
  11.3 6.8 %collective-permute-done.8.refs_11_ = bf16[2,2,128,128]{3,2,1,0:T(8,128)(2,1)S(1)} collective-permute-done((bf16[2,2,128,128]{3,2,1,0:T(8,128)(2,1)S(1)}, bf16[2,2,128,128]{3,2,1,0:T(8,128)(2,1)S(1)}, u32[]{:S(2)}, u32[]{:S(2)}) %collective-permute-start.8) | collective-permute-done | bytes 131104 | tf_op jit(solution)/shard_map/ppermute | solution.py:361
  18.1 1.5 %collective-permute-start.14 = (bf16[2,8,2,16,128]{4,3,2,1,0:T(8,128)(2,1)S(1)}, bf16[2,8,2,16,128]{4,3,2,1,0:T(8,128)(2,1)S(1)}, u32[]{:S(2)}, u32[]{:S(2)}) collective-permute-start(bf16[2,8,2,16,128]{4,3,2,1,0:T(8,128)(2,1)S(1)} %get-tuple-element.23), channel_id=1, source_target_pairs={{0,16},{8,24},{16,0},{24,8},{1,17},{9,25},{17,1},{25,9},{2,18},{10... | collective-permute-start | bytes 393224 | tf_op jit(solution)/shard_map/ppermute | solution.py:361
  19.6 0.0 collective-permute-done.7.refs_10_
  19.6 0.0 collective-permute-start.16
  19.6 0.0 collective-permute-done.3.refs_5_
  19.6 0.6 %collective-permute-start.13 = (bf16[2,2,128,128]{3,2,1,0:T(8,128)(2,1)S(1)}, bf16[2,2,128,128]{3,2,1,0:T(8,128)(2,1)S(1)}, u32[]{:S(2)}, u32[]{:S(2)}) collective-permute-start(bf16[2,2,128,128]{3,2,1,0:T(8,128)(2,1)S(1)} %collective-permute-done.9.refs_12_), channel_id=1, source_target_pairs={{0,8},{8,0},{16,24},{24,16},{1,9},{9,1},{17,25},{25,17},{2,10},{10... | collective-permute-start | bytes 393224 | tf_op jit(solution)/shard_map/ppermute | solution.py:361
  20.3 0.0 collective-permute-done.5.refs_7_
  20.3 0.1 collective-permute-start.12
  20.3 0.1 sine_negate_fusion
  20.5 3.1 %collective-permute-done.14.refs_5_ = bf16[2,8,2,16,128]{4,3,2,1,0:T(8,128)(2,1)S(1)} collective-permute-done((bf16[2,8,2,16,128]{4,3,2,1,0:T(8,128)(2,1)S(1)}, bf16[2,8,2,16,128]{4,3,2,1,0:T(8,128)(2,1)S(1)}, u32[]{:S(2)}, u32[]{:S(2)}) %collective-permute-start.14) | collective-permute-done | bytes 131104 | tf_op jit(solution)/shard_map/ppermute | solution.py:361
  23.5 1.5 %collective-permute-start = (bf16[2,16,2,16,128]{4,3,2,1,0:T(8,128)(2,1)S(1)}, bf16[2,16,2,16,128]{4,3,2,1,0:T(8,128)(2,1)S(1)}, u32[]{:S(2)}, u32[]{:S(2)}) collective-permute-start(bf16[2,16,2,16,128]{4,3,2,1,0:T(8,128)(2,1)S(1)} %shard_map.55.refs_1_), channel_id=1, source_target_pairs={{0,1},{1,0},{2,3},{3,2},{4,5},{5,4},{6,7},{7,6},{8,9},{9,8},{10,11... | collective-permute-start | bytes 786440 | tf_op jit(solution)/shard_map/ppermute | solution.py:361
  25.0 0.4 collective-permute-done.16.refs_7_
  25.4 0.3 collective-permute-start.11
  25.7 0.0 collective-permute-done.13.refs_16_
  25.7 1.5 %collective-permute-start.15 = (bf16[2,8,2,16,128]{4,3,2,1,0:T(8,128)(2,1)S(1)}, bf16[2,8,2,16,128]{4,3,2,1,0:T(8,128)(2,1)S(1)}, u32[]{:S(2)}, u32[]{:S(2)}) collective-permute-start(bf16[2,8,2,16,128]{4,3,2,1,0:T(8,128)(2,1)S(1)} %collective-permute-done.14.refs_5_), channel_id=1, source_target_pairs={{0,1},{1,0},{2,3},{3,2},{4,5},{5,4},{6,7},{7,6},{8,9},{9,8},{10,11... | collective-permute-start | bytes 393224 | tf_op jit(solution)/shard_map/ppermute | solution.py:361
  27.2 0.0 collective-permute-done.12.refs_15_
  27.2 0.5 %collective-permute-start.17 = (bf16[2,8,2,16,128]{4,3,2,1,0:T(8,128)(2,1)S(1)}, bf16[2,8,2,16,128]{4,3,2,1,0:T(8,128)(2,1)S(1)}, u32[]{:S(2)}, u32[]{:S(2)}) collective-permute-start(bf16[2,8,2,16,128]{4,3,2,1,0:T(8,128)(2,1)S(1)} %collective-permute-done.16.refs_7_), channel_id=1, source_target_pairs={{0,1},{1,0},{2,3},{3,2},{4,5},{5,4},{6,7},{7,6},{8,9},{9,8},{10,11... | collective-permute-start | bytes 393224 | tf_op jit(solution)/shard_map/ppermute | solution.py:361
  27.7 0.0 collective-permute-done.1.refs_3_
  27.7 1.5 %collective-permute-start.2 = (bf16[2,16,2,16,128]{4,3,2,1,0:T(8,128)(2,1)S(1)}, bf16[2,16,2,16,128]{4,3,2,1,0:T(8,128)(2,1)S(1)}, u32[]{:S(2)}, u32[]{:S(2)}) collective-permute-start(bf16[2,16,2,16,128]{4,3,2,1,0:T(8,128)(2,1)S(1)} %collective-permute-done.1.refs_3_), channel_id=1, source_target_pairs={{0,1},{1,0},{2,3},{3,2},{4,5},{5,4},{6,7},{7,6},{8,9},{9,8},{10,11... | collective-permute-start | bytes 786440 | tf_op jit(solution)/shard_map/ppermute | solution.py:361
  29.2 0.0 copy-done.4
  29.3 0.0 copy-done.1
  29.3 0.3 shard_map.59
  29.6 0.1 pad_add_fusion.numbers.refs_0_
  29.7 2.8 %shard_map.60.refs_17_ = f32[16,256,256]{2,1,0:T(8,128)S(1)} custom-call(s32[32]{0:T(128)S(1)} %pad_add_fusion.numbers.refs_0_, f32[16,256]{1,0:T(8,128)S(1)} %get-tuple-element.26.slow_cos, f32[16,256]{1,0:T(8,128)S(1)} %get-tuple-element.25.slow_sin, f32[256,256]{1,0:T(8,128)S(1)} %get-tuple-element.21.twist.refs_20_), custom_call_target="tpu_custom_call" | custom-call | flops 1000000 | bytes 2000000 | tf_op jit(solution)/shard_map/pallas_call | solution.py:146
  32.5 0.0 collective-permute-done.11.refs_14_
  32.5 0.6 %collective-permute-start.4 = (bf16[2,8,2,16,128]{4,3,2,1,0:T(8,128)(2,1)S(1)}, bf16[2,8,2,16,128]{4,3,2,1,0:T(8,128)(2,1)S(1)}, u32[]{:S(2)}, u32[]{:S(2)}) collective-permute-start(bf16[2,8,2,16,128]{4,3,2,1,0:T(8,128)(2,1)S(1)} %collective-permute-done.3.refs_5_), channel_id=1, source_target_pairs={{0,1},{1,0},{2,3},{3,2},{4,5},{5,4},{6,7},{7,6},{8,9},{9,8},{10,11... | collective-permute-start | bytes 393224 | tf_op jit(solution)/shard_map/ppermute | solution.py:361
  33.1 0.0 collective-permute-done.refs_2_
  33.1 1.5 %collective-permute-start.6 = (bf16[2,8,2,16,128]{4,3,2,1,0:T(8,128)(2,1)S(1)}, bf16[2,8,2,16,128]{4,3,2,1,0:T(8,128)(2,1)S(1)}, u32[]{:S(2)}, u32[]{:S(2)}) collective-permute-start(bf16[2,8,2,16,128]{4,3,2,1,0:T(8,128)(2,1)S(1)} %collective-permute-done.5.refs_7_), channel_id=1, source_target_pairs={{0,1},{1,0},{2,3},{3,2},{4,5},{5,4},{6,7},{7,6},{8,9},{9,8},{10,11... | collective-permute-start | bytes 393224 | tf_op jit(solution)/shard_map/ppermute | solution.py:361
  34.6 0.0 collective-permute-done.15.refs_6_
  34.6 2.5 %collective-permute-done.17.refs_8_ = bf16[2,8,2,16,128]{4,3,2,1,0:T(8,128)(2,1)S(1)} collective-permute-done((bf16[2,8,2,16,128]{4,3,2,1,0:T(8,128)(2,1)S(1)}, bf16[2,8,2,16,128]{4,3,2,1,0:T(8,128)(2,1)S(1)}, u32[]{:S(2)}, u32[]{:S(2)}) %collective-permute-start.17) | collective-permute-done | bytes 131104 | tf_op jit(solution)/shard_map/ppermute | solution.py:361
  37.1 5.6 %collective-permute-done.2.refs_4_ = bf16[2,16,2,16,128]{4,3,2,1,0:T(8,128)(2,1)S(1)} collective-permute-done((bf16[2,16,2,16,128]{4,3,2,1,0:T(8,128)(2,1)S(1)}, bf16[2,16,2,16,128]{4,3,2,1,0:T(8,128)(2,1)S(1)}, u32[]{:S(2)}, u32[]{:S(2)}) %collective-permute-start.2) | collective-permute-done | bytes 262176 | tf_op jit(solution)/shard_map/ppermute | solution.py:361
  42.7 4.3 %shard_map.61.refs_21_ = f32[2,1024,128]{2,1,0:T(8,128)S(1)} custom-call(s32[32]{0:T(128)S(1)} %pad_add_fusion.numbers.refs_0_, bf16[2,16,2,16,128]{4,3,2,1,0:T(8,128)(2,1)S(1)} %shard_map.55.refs_1_, bf16[2,16,2,16,128]{4,3,2,1,0:T(8,128)(2,1)S(1)} %collective-permute-done.refs_2_, bf16[2,16,2,16,128]{4,3,2,1,0:T(8,128)(2,1)S(1)} %collective-permute-done.1.refs_3_, ...), custom_call_target="tpu_custom_call" | custom-call | flops 3000000000 | bytes 8000000 | tf_op jit(solution)/shard_map/pallas_call | solution.py:335
  47.0 0.0 collective-permute-done.4.refs_6_
  47.0 0.0 collective-permute-done.6.refs_8_
  47.1 5.3 %shard_map.62 = f32[2,2,1024,128]{3,2,1,0:T(8,128)} custom-call(s32[32]{0:T(128)S(1)} %pad_add_fusion.numbers.refs_0_, bf16[2,16,2,16,128]{4,3,2,1,0:T(8,128)(2,1)S(1)} %shard_map.55.refs_1_, bf16[2,16,2,16,128]{4,3,2,1,0:T(8,128)(2,1)S(1)} %collective-permute-done.refs_2_, bf16[2,16,2,16,128]{4,3,2,1,0:T(8,128)(2,1)S(1)} %collective-permute-done.1.refs_3_, ...), custom_call_target="tpu_custom_call" | custom-call | flops 3000000000 | bytes 8000000 | tf_op jit(solution)/shard_map/pallas_call | solution.py:335
  (2 shorter events, 0.0 us)
Async XLA Ops:
  0.0 0.9 %copy-start.2 = (bf16[2,2,32768]{2,1,0:T(2,128)(2,1)S(1)}, bf16[2,2,32768]{2,1,0:T(2,128)(2,1)}, u32[]{:S(2)}) copy-start(bf16[2,2,32768]{2,1,0:T(2,128)(2,1)} %filters.1) | copy-start | bytes 786436
  1.0 10.2 %copy-start.3 = (s32[16]{0:T(128)S(1)}, s32[16]{0:T(128)}, u32[]{:S(2)}) copy-start(s32[16]{0:T(128)} %param.8) | copy-start | bytes 196
  1.0 28.3 %copy-start.4 = (s32[16]{0:T(128)S(1)}, s32[16]{0:T(128)}, u32[]{:S(2)}) copy-start(s32[16]{0:T(128)} %param.7) | copy-start | bytes 196
  1.2 9.4 %collective-permute-start.10 = (bf16[2,2,128,128]{3,2,1,0:T(8,128)(2,1)S(1)}, bf16[2,2,128,128]{3,2,1,0:T(8,128)(2,1)S(1)}, u32[]{:S(2)}, u32[]{:S(2)}) collective-permute-start(bf16[2,2,128,128]{3,2,1,0:T(8,128)(2,1)S(1)} %shard_map.58.refs_9_), channel_id=1, source_target_pairs={{0,8},{8,0},{16,24},{24,16},{1,9},{9,1},{17,25},{25,17},{2,10},{10... | collective-permute-start | bytes 393224 | tf_op jit(solution)/shard_map/ppermute | solution.py:361
  1.8 9.1 %collective-permute-start.9 = (bf16[2,2,128,128]{3,2,1,0:T(8,128)(2,1)S(1)}, bf16[2,2,128,128]{3,2,1,0:T(8,128)(2,1)S(1)}, u32[]{:S(2)}, u32[]{:S(2)}) collective-permute-start(bf16[2,2,128,128]{3,2,1,0:T(8,128)(2,1)S(1)} %shard_map.58.refs_9_), channel_id=1, source_target_pairs={{0,6},{2,4},{4,2},{6,0},{1,7},{3,5},{5,3},{7,1},{8,14},{10,12},{12... | collective-permute-start | bytes 393224 | tf_op jit(solution)/shard_map/ppermute | solution.py:361
  6.4 11.7 %collective-permute-start.8 = (bf16[2,2,128,128]{3,2,1,0:T(8,128)(2,1)S(1)}, bf16[2,2,128,128]{3,2,1,0:T(8,128)(2,1)S(1)}, u32[]{:S(2)}, u32[]{:S(2)}) collective-permute-start(bf16[2,2,128,128]{3,2,1,0:T(8,128)(2,1)S(1)} %shard_map.58.refs_9_), channel_id=1, source_target_pairs={{0,4},{2,6},{4,0},{6,2},{1,5},{3,7},{5,1},{7,3},{8,12},{10,14},{12... | collective-permute-start | bytes 393224 | tf_op jit(solution)/shard_map/ppermute | solution.py:361
  6.4 13.2 %collective-permute-start.7 = (bf16[2,2,128,128]{3,2,1,0:T(8,128)(2,1)S(1)}, bf16[2,2,128,128]{3,2,1,0:T(8,128)(2,1)S(1)}, u32[]{:S(2)}, u32[]{:S(2)}) collective-permute-start(bf16[2,2,128,128]{3,2,1,0:T(8,128)(2,1)S(1)} %shard_map.58.refs_9_), channel_id=1, source_target_pairs={{0,2},{2,0},{4,6},{6,4},{1,3},{3,1},{5,7},{7,5},{8,10},{10,8},{12,... | collective-permute-start | bytes 393224 | tf_op jit(solution)/shard_map/ppermute | solution.py:361
  7.1 1.2 %copy-start = (bf16[2,64,4096]{2,1,0:T(8,128)(2,1)S(1)}, bf16[2,64,4096]{2,1,0:T(8,128)(2,1)}, u32[]{:S(2)}) copy-start(bf16[2,64,4096]{2,1,0:T(8,128)(2,1)} %echoes.2) | copy-start | bytes 3145732
  8.3 21.0 %copy-start.1 = (bf16[3328,256]{1,0:T(8,128)(2,1)S(1)}, bf16[3328,256]{1,0:T(8,128)(2,1)}, u32[]{:S(2)}) copy-start(bf16[3328,256]{1,0:T(8,128)(2,1)} %constant.46.clone.dots.refs_19_) | copy-start | bytes 5111812
  8.5 11.1 %collective-permute-start.3 = (bf16[2,8,2,16,128]{4,3,2,1,0:T(8,128)(2,1)S(1)}, bf16[2,8,2,16,128]{4,3,2,1,0:T(8,128)(2,1)S(1)}, u32[]{:S(2)}, u32[]{:S(2)}) collective-permute-start(bf16[2,8,2,16,128]{4,3,2,1,0:T(8,128)(2,1)S(1)} %get-tuple-element.18), channel_id=1, source_target_pairs={{0,16},{8,24},{16,0},{24,8},{1,17},{9,25},{17,1},{25,9},{2,18},{10... | collective-permute-start | bytes 393224 | tf_op jit(solution)/shard_map/ppermute | solution.py:361
  10.6 9.7 %collective-permute-start.5 = (bf16[2,8,2,16,128]{4,3,2,1,0:T(8,128)(2,1)S(1)}, bf16[2,8,2,16,128]{4,3,2,1,0:T(8,128)(2,1)S(1)}, u32[]{:S(2)}, u32[]{:S(2)}) collective-permute-start(bf16[2,8,2,16,128]{4,3,2,1,0:T(8,128)(2,1)S(1)} %get-tuple-element.19), channel_id=1, source_target_pairs={{0,24},{8,16},{16,8},{24,0},{1,25},{9,17},{17,9},{25,1},{2,26},{10... | collective-permute-start | bytes 393224 | tf_op jit(solution)/shard_map/ppermute | solution.py:361
  10.9 16.9 %collective-permute-start.1 = (bf16[2,16,2,16,128]{4,3,2,1,0:T(8,128)(2,1)S(1)}, bf16[2,16,2,16,128]{4,3,2,1,0:T(8,128)(2,1)S(1)}, u32[]{:S(2)}, u32[]{:S(2)}) collective-permute-start(bf16[2,16,2,16,128]{4,3,2,1,0:T(8,128)(2,1)S(1)} %get-tuple-element.17), channel_id=1, source_target_pairs={{0,8},{8,0},{16,24},{24,16},{1,9},{9,1},{17,25},{25,17},{2,10},{10... | collective-permute-start | bytes 786440 | tf_op jit(solution)/shard_map/ppermute | solution.py:361
  18.1 5.4 %collective-permute-start.14 = (bf16[2,8,2,16,128]{4,3,2,1,0:T(8,128)(2,1)S(1)}, bf16[2,8,2,16,128]{4,3,2,1,0:T(8,128)(2,1)S(1)}, u32[]{:S(2)}, u32[]{:S(2)}) collective-permute-start(bf16[2,8,2,16,128]{4,3,2,1,0:T(8,128)(2,1)S(1)} %get-tuple-element.23), channel_id=1, source_target_pairs={{0,16},{8,24},{16,0},{24,8},{1,17},{9,25},{17,1},{25,9},{2,18},{10... | collective-permute-start | bytes 393224 | tf_op jit(solution)/shard_map/ppermute | solution.py:361
  19.6 5.8 %collective-permute-start.16 = (bf16[2,8,2,16,128]{4,3,2,1,0:T(8,128)(2,1)S(1)}, bf16[2,8,2,16,128]{4,3,2,1,0:T(8,128)(2,1)S(1)}, u32[]{:S(2)}, u32[]{:S(2)}) collective-permute-start(bf16[2,8,2,16,128]{4,3,2,1,0:T(8,128)(2,1)S(1)} %get-tuple-element.24), channel_id=1, source_target_pairs={{0,24},{8,16},{16,8},{24,0},{1,25},{9,17},{17,9},{25,1},{2,26},{10... | collective-permute-start | bytes 393224 | tf_op jit(solution)/shard_map/ppermute | solution.py:361
  19.6 6.1 %collective-permute-start.13 = (bf16[2,2,128,128]{3,2,1,0:T(8,128)(2,1)S(1)}, bf16[2,2,128,128]{3,2,1,0:T(8,128)(2,1)S(1)}, u32[]{:S(2)}, u32[]{:S(2)}) collective-permute-start(bf16[2,2,128,128]{3,2,1,0:T(8,128)(2,1)S(1)} %collective-permute-done.9.refs_12_), channel_id=1, source_target_pairs={{0,8},{8,0},{16,24},{24,16},{1,9},{9,1},{17,25},{25,17},{2,10},{10... | collective-permute-start | bytes 393224 | tf_op jit(solution)/shard_map/ppermute | solution.py:361
  20.3 6.9 %collective-permute-start.12 = (bf16[2,2,128,128]{3,2,1,0:T(8,128)(2,1)S(1)}, bf16[2,2,128,128]{3,2,1,0:T(8,128)(2,1)S(1)}, u32[]{:S(2)}, u32[]{:S(2)}) collective-permute-start(bf16[2,2,128,128]{3,2,1,0:T(8,128)(2,1)S(1)} %collective-permute-done.8.refs_11_), channel_id=1, source_target_pairs={{0,8},{8,0},{16,24},{24,16},{1,9},{9,1},{17,25},{25,17},{2,10},{10... | collective-permute-start | bytes 393224 | tf_op jit(solution)/shard_map/ppermute | solution.py:361
  23.5 9.6 %collective-permute-start = (bf16[2,16,2,16,128]{4,3,2,1,0:T(8,128)(2,1)S(1)}, bf16[2,16,2,16,128]{4,3,2,1,0:T(8,128)(2,1)S(1)}, u32[]{:S(2)}, u32[]{:S(2)}) collective-permute-start(bf16[2,16,2,16,128]{4,3,2,1,0:T(8,128)(2,1)S(1)} %shard_map.55.refs_1_), channel_id=1, source_target_pairs={{0,1},{1,0},{2,3},{3,2},{4,5},{5,4},{6,7},{7,6},{8,9},{9,8},{10,11... | collective-permute-start | bytes 786440 | tf_op jit(solution)/shard_map/ppermute | solution.py:361
  25.4 7.1 %collective-permute-start.11 = (bf16[2,2,128,128]{3,2,1,0:T(8,128)(2,1)S(1)}, bf16[2,2,128,128]{3,2,1,0:T(8,128)(2,1)S(1)}, u32[]{:S(2)}, u32[]{:S(2)}) collective-permute-start(bf16[2,2,128,128]{3,2,1,0:T(8,128)(2,1)S(1)} %collective-permute-done.7.refs_10_), channel_id=1, source_target_pairs={{0,8},{8,0},{16,24},{24,16},{1,9},{9,1},{17,25},{25,17},{2,10},{10... | collective-permute-start | bytes 393224 | tf_op jit(solution)/shard_map/ppermute | solution.py:361
  25.7 8.9 %collective-permute-start.15 = (bf16[2,8,2,16,128]{4,3,2,1,0:T(8,128)(2,1)S(1)}, bf16[2,8,2,16,128]{4,3,2,1,0:T(8,128)(2,1)S(1)}, u32[]{:S(2)}, u32[]{:S(2)}) collective-permute-start(bf16[2,8,2,16,128]{4,3,2,1,0:T(8,128)(2,1)S(1)} %collective-permute-done.14.refs_5_), channel_id=1, source_target_pairs={{0,1},{1,0},{2,3},{3,2},{4,5},{5,4},{6,7},{7,6},{8,9},{9,8},{10,11... | collective-permute-start | bytes 393224 | tf_op jit(solution)/shard_map/ppermute | solution.py:361
  27.2 9.9 %collective-permute-start.17 = (bf16[2,8,2,16,128]{4,3,2,1,0:T(8,128)(2,1)S(1)}, bf16[2,8,2,16,128]{4,3,2,1,0:T(8,128)(2,1)S(1)}, u32[]{:S(2)}, u32[]{:S(2)}) collective-permute-start(bf16[2,8,2,16,128]{4,3,2,1,0:T(8,128)(2,1)S(1)} %collective-permute-done.16.refs_7_), channel_id=1, source_target_pairs={{0,1},{1,0},{2,3},{3,2},{4,5},{5,4},{6,7},{7,6},{8,9},{9,8},{10,11... | collective-permute-start | bytes 393224 | tf_op jit(solution)/shard_map/ppermute | solution.py:361
  27.7 15.0 %collective-permute-start.2 = (bf16[2,16,2,16,128]{4,3,2,1,0:T(8,128)(2,1)S(1)}, bf16[2,16,2,16,128]{4,3,2,1,0:T(8,128)(2,1)S(1)}, u32[]{:S(2)}, u32[]{:S(2)}) collective-permute-start(bf16[2,16,2,16,128]{4,3,2,1,0:T(8,128)(2,1)S(1)} %collective-permute-done.1.refs_3_), channel_id=1, source_target_pairs={{0,1},{1,0},{2,3},{3,2},{4,5},{5,4},{6,7},{7,6},{8,9},{9,8},{10,11... | collective-permute-start | bytes 786440 | tf_op jit(solution)/shard_map/ppermute | solution.py:361
  32.5 14.5 %collective-permute-start.4 = (bf16[2,8,2,16,128]{4,3,2,1,0:T(8,128)(2,1)S(1)}, bf16[2,8,2,16,128]{4,3,2,1,0:T(8,128)(2,1)S(1)}, u32[]{:S(2)}, u32[]{:S(2)}) collective-permute-start(bf16[2,8,2,16,128]{4,3,2,1,0:T(8,128)(2,1)S(1)} %collective-permute-done.3.refs_5_), channel_id=1, source_target_pairs={{0,1},{1,0},{2,3},{3,2},{4,5},{5,4},{6,7},{7,6},{8,9},{9,8},{10,11... | collective-permute-start | bytes 393224 | tf_op jit(solution)/shard_map/ppermute | solution.py:361
  33.1 13.9 %collective-permute-start.6 = (bf16[2,8,2,16,128]{4,3,2,1,0:T(8,128)(2,1)S(1)}, bf16[2,8,2,16,128]{4,3,2,1,0:T(8,128)(2,1)S(1)}, u32[]{:S(2)}, u32[]{:S(2)}) collective-permute-start(bf16[2,8,2,16,128]{4,3,2,1,0:T(8,128)(2,1)S(1)} %collective-permute-done.5.refs_7_), channel_id=1, source_target_pairs={{0,1},{1,0},{2,3},{3,2},{4,5},{5,4},{6,7},{7,6},{8,9},{9,8},{10,11... | collective-permute-start | bytes 393224 | tf_op jit(solution)/shard_map/ppermute | solution.py:361

commit v4 on v3

--- a/solution.py
+++ b/solution.py
@@ -189,28 +189,30 @@
 def focus_kernel(bases, pieces, earlier, rows, row0, slow, out_slow, *refs):
     sources = len(bases)
     slabs, blocks = refs[0], refs[1 : 1 + sources]
-    own = refs[1 + sources : 1 + sources + pieces]
-    other = refs[1 + sources + pieces : 1 + sources + 2 * pieces]
-    phase, first_dots_ref, dots, twist = refs[1 + sources + 2 * pieces :][:4]
-    rest = refs[5 + sources + 2 * pieces :]
-    images, out = rest[:earlier], rest[earlier]
-    s1, y1, s2, y2, s3, y3, s4, filt, ids, slab_sem = rest[earlier + 1 :][:10]
+    count = 1 if earlier else 2 * pieces
+    filters, rest = refs[1 + sources : 1 + sources + count], refs[1 + sources + count :]
+    phase, first_dots_ref, dots, twist = rest[:4]
+    images, out, rest = rest[4 : 4 + earlier], rest[4 + earlier], rest[5 + earlier :]
+    filt, rest = (filters[0], rest) if earlier else (rest[0], rest[1:])
+    s1, y1, s2, y2, s3, y3, s4, ids, slab_sem = rest[:9]
     fetch = pltpu.make_async_copy(slabs, ids, slab_sem)
     fetch.start()
     tile = out
     writes = []
     if earlier:
-        tile, write_sem = rest[earlier + 11 :]
+        tile, write_sem = rest[9:]
         for k, source in enumerate((*images, tile)):
             for p in range(2):
                 writes.append(pltpu.make_async_copy(source.at[p], out.at[p, k], write_sem.at[2 * k + p]))
         for write in writes[:-2]:
             write.start()
     core = lax.axis_index("turn") % 2
-    per_zone = own[0].shape[0]
-    for k in range(pieces):
-        filt[core, k * per_zone : (k + 1) * per_zone] = own[k][...]
-        filt[1 - core, k * per_zone : (k + 1) * per_zone] = other[k][...]
+    if not earlier:
+        own, other = filters[:pieces], filters[pieces:]
+        per_zone = own[0].shape[0]
+        for k in range(pieces):
+            filt[core, k * per_zone : (k + 1) * per_zone] = own[k][...]
+            filt[1 - core, k * per_zone : (k + 1) * per_zone] = other[k][...]
     half = slow // 2
     wide = 2 * LANES
     first = [[first_dots_ref.at[pl.ds((2 * e + k) * slow, slow)] for k in range(2)] for e in range(2)]
@@ -229,7 +231,8 @@
                 ],
                 1,
             )
-            s1[pair, e] = dot(first[e][0][...], data) + dot(first[e][1][...], data)
+            both = dot(first_dots_ref[2 * e * slow : 2 * (e + 1) * slow], data)
+            s1[pair, e] = both[:slow] + both[slow:]
 
     def first_twist(pair):
         for i in range(2):
@@ -285,9 +288,8 @@
     def last_dots(pair):
         for e in range(2):
             high, low = y3[pair, e, 0], y3[pair, e, 1]
-            s4[pair, e] = (
-                dot(last[e][0][...], high) + dot(last[e][1][...], high) + dot(last[e][0][...], low)
-            )
+            both = dot(dots[base + 2 * e * out_slow : base + 2 * (e + 1) * out_slow], high)
+            s4[pair, e] = both[:out_slow] + both[out_slow:] + dot(last[e][0][...], low)
 
     def store(pair):
         count = out_slow // 2
@@ -310,10 +312,11 @@
         last_dots,
         store,
     ]
-    streams = [[(step, pair) for pair in range(k, rows // 2, 2) for step in range(8)] for k in range(2)]
+    count, late = 2, 1
+    streams = [[(step, pair) for pair in range(k, rows // 2, count) for step in range(8)] for k in range(count)]
     fetch.wait()
-    for t in range(len(streams[0]) + 1):
-        now = [s[t - k] for k, s in enumerate(streams) if 0 <= t - k < len(s)]
+    for t in range(len(streams[0]) + late * (count - 1)):
+        now = [s[t - late * k] for k, s in enumerate(streams) if 0 <= t - late * k < len(s)]
         for step, pair in sorted(now, key=lambda job: job[0] % 2):
             steps[step](pair)
     for write in writes[-2:]:
@@ -322,22 +325,27 @@
         write.wait()
 
 
-def focus(blocks, bases, own, other, tables, slabs, images, rows, row0, total, slow, out_slow, final):
-    slots, pieces = rows // 2, len(own)
+def focus(blocks, bases, filters, tables, slabs, images, rows, row0, total, slow, out_slow, final):
+    slots, pieces = rows // 2, len(filters) // 2
 
     def full(a):
-        return pl.BlockSpec(a.shape, lambda i: (0,) * a.ndim)
+        return pl.BlockSpec(a.shape, lambda i: (0,) * len(a.shape))
 
     image = (2, out_slow * 8, LANES)
     shape = (2, total // 8, *image[1:]) if final else image
-    operands = [slabs, *blocks, *own, *other, *tables, *images]
+    operands = [slabs, *blocks, *filters, *tables, *images]
+    out_shape = [jax.ShapeDtypeStruct(shape, jnp.float32)]
+    out_specs = [pl.BlockSpec(memory_space=pl.ANY)]
+    if not final:
+        out_shape.append(jax.ShapeDtypeStruct((2, pieces * filters[0].shape[0], *filters[0].shape[1:]), jnp.bfloat16))
+        out_specs = [full(a) for a in out_shape]
     extra = [pltpu.VMEM(image, jnp.float32), pltpu.SemaphoreType.DMA((total // 4,))] if final else []
     return pl.pallas_call(
         functools.partial(focus_kernel, tuple(bases), pieces, len(images), rows, row0, slow, out_slow),
         grid=(1,),
         in_specs=[full(a) for a in operands],
-        out_specs=pl.BlockSpec(memory_space=pl.ANY) if final else pl.BlockSpec(image, lambda i: (0, 0, 0)),
-        out_shape=jax.ShapeDtypeStruct(shape, jnp.float32),
+        out_specs=out_specs,
+        out_shape=out_shape,
         scratch_shapes=[
             pltpu.VMEM((slots, 2, slow, 2 * LANES), jnp.float32),
             pltpu.VMEM((slots, 2, slow, 4 * LANES), jnp.bfloat16),
@@ -346,7 +354,6 @@
             pltpu.VMEM((slots, 2 * slow, 2 * LANES), jnp.float32),
             pltpu.VMEM((slots, 2, 2, slow, 2 * LANES), jnp.bfloat16),
             pltpu.VMEM((slots, 2, out_slow, 2 * LANES), jnp.float32),
-            pltpu.VMEM((2, pieces * own[0].shape[0], *own[0].shape[1:]), jnp.bfloat16),
             pltpu.SMEM(slabs.shape, jnp.int32),
             pltpu.SemaphoreType.DMA,
             *extra,
@@ -403,7 +410,7 @@
     numbers = jnp.concatenate([local_slab, shifts & (LANES - 1)])
     phase = phases(numbers, *slow_ramp, twist, total, slow)
 
-    images = []
+    images, filt = [], [*own, *other]
     for k, (start, rows) in enumerate(zip(starts, CHUNKS)):
         blocks, bases = [], []
         for slot in range(sources):
@@ -411,10 +418,11 @@
             blocks.append(held[slot, 0 if whole else start])
             bases.append(start if whole else 0)
         final = k == len(CHUNKS) - 1
-        image = focus(
-            blocks, bases, own, other, (phase, first, dots, twist), numbers, images, rows, start, total, slow, out_slow, final
+        image, *given = focus(
+            blocks, bases, filt, (phase, first, dots, twist), numbers, images, rows, start, total, slow, out_slow, final
         )
         images.append(image)
+        filt = given
     image = image.reshape(2, total // 8, out_slow, 8, LANES).transpose(0, 1, 3, 2, 4)
     return image.reshape(2, total, out_slow * LANES)
 

time: 53 us -> 53 us (level)
  no operation moved by 1% of the time
where the time goes in v4:
time: 53 us; the launch traced here: 52.4 us
  waiting for transfers between devices  18.5 us (35%)
  starting transfers between devices  17.5 us (33%)
  Pallas kernels  13.8 us (26%)
  local copies, waits for them, and re-layouts  2.18 us (4%)
    ppermute x18, waiting for transfers between devices, swap(): return lax.ppermute(value, axis, [(a, a ^ flip) for a in range(size)])  18.5 us
    ppermute x18, starting transfers between devices, swap(): return lax.ppermute(value, axis, [(a, a ^ flip) for a in range(size)])  17.5 us
    pallas_call x2, Pallas kernels, focus(): pl.pallas_call(functools.partial(focus_kernel, tuple(bases), pieces, len(...  9.67 us
    pallas_call x1, Pallas kernels, phases(): pl.pallas_call(functools.partial(phase_kernel, total, slow), in_specs=[vm...  2.84 us
    unnamed x10, local copies, waits for them, and re-layouts  2.18 us
  transfers between devices with their start and end apart: 18, of which 6 were waited for; matrix products, arithmetic and copies ran while one was open for 0% of the time, Pallas kernels for 16%

profile of v4, /device:TPU:0, one launch (start us, length us, event | category | flops | bytes accessed | tf_op | source)
XLA Modules:
  0.0 52.4 jit_solution(9107452927079010984)
XLA Ops:
  0.0 0.0 copy-start.2
  0.0 0.9 %copy-done.2 = bf16[2,2,32768]{2,1,0:T(2,128)(2,1)S(1)} copy-done((bf16[2,2,32768]{2,1,0:T(2,128)(2,1)S(1)}, bf16[2,2,32768]{2,1,0:T(2,128)(2,1)}, u32[]{:S(2)}) %copy-start.2) | copy-done | bytes 262168
  1.0 0.0 copy-start.3
  1.0 0.0 copy-start.4
  1.0 0.3 shard_map.58.refs_9_
  1.2 0.6 %collective-permute-start.14 = (bf16[2,2,128,128]{3,2,1,0:T(8,128)(2,1)S(1)}, bf16[2,2,128,128]{3,2,1,0:T(8,128)(2,1)S(1)}, u32[]{:S(2)}, u32[]{:S(2)}) collective-permute-start(bf16[2,2,128,128]{3,2,1,0:T(8,128)(2,1)S(1)} %shard_map.58.refs_9_), channel_id=1, source_target_pairs={{0,8},{8,0},{16,24},{24,16},{1,9},{9,1},{17,25},{25,17},{2,10},{10... | collective-permute-start | bytes 393224 | tf_op jit(solution)/shard_map/ppermute | solution.py:368
  1.8 4.7 %collective-permute-start.13 = (bf16[2,2,128,128]{3,2,1,0:T(8,128)(2,1)S(1)}, bf16[2,2,128,128]{3,2,1,0:T(8,128)(2,1)S(1)}, u32[]{:S(2)}, u32[]{:S(2)}) collective-permute-start(bf16[2,2,128,128]{3,2,1,0:T(8,128)(2,1)S(1)} %shard_map.58.refs_9_), channel_id=1, source_target_pairs={{0,6},{2,4},{4,2},{6,0},{1,7},{3,5},{5,3},{7,1},{8,14},{10,12},{12... | collective-permute-start | bytes 393224 | tf_op jit(solution)/shard_map/ppermute | solution.py:368
  6.4 0.0 collective-permute-start.12
  6.4 0.6 %collective-permute-start.11 = (bf16[2,2,128,128]{3,2,1,0:T(8,128)(2,1)S(1)}, bf16[2,2,128,128]{3,2,1,0:T(8,128)(2,1)S(1)}, u32[]{:S(2)}, u32[]{:S(2)}) collective-permute-start(bf16[2,2,128,128]{3,2,1,0:T(8,128)(2,1)S(1)} %shard_map.58.refs_9_), channel_id=1, source_target_pairs={{0,2},{2,0},{4,6},{6,4},{1,3},{3,1},{5,7},{7,5},{8,10},{10,8},{12,... | collective-permute-start | bytes 393224 | tf_op jit(solution)/shard_map/ppermute | solution.py:368
  7.1 0.0 copy-start
  7.1 1.2 %copy-done = bf16[2,64,4096]{2,1,0:T(8,128)(2,1)S(1)} copy-done((bf16[2,64,4096]{2,1,0:T(8,128)(2,1)S(1)}, bf16[2,64,4096]{2,1,0:T(8,128)(2,1)}, u32[]{:S(2)}) %copy-start) | copy-done | bytes 1048600
  8.3 0.0 copy-start.1
  8.3 0.2 shard_map.57
  8.5 1.7 %collective-permute-start.3 = (bf16[2,8,2,16,128]{4,3,2,1,0:T(8,128)(2,1)S(1)}, bf16[2,8,2,16,128]{4,3,2,1,0:T(8,128)(2,1)S(1)}, u32[]{:S(2)}, u32[]{:S(2)}) collective-permute-start(bf16[2,8,2,16,128]{4,3,2,1,0:T(8,128)(2,1)S(1)} %get-tuple-element.20), channel_id=1, source_target_pairs={{0,16},{8,24},{16,0},{24,8},{1,17},{9,25},{17,1},{25,9},{2,18},{10... | collective-permute-start | bytes 393224 | tf_op jit(solution)/shard_map/ppermute | solution.py:368
  10.2 0.4 shard_map.56
  10.6 0.0 collective-permute-done.14.refs_13_
  10.6 0.1 collective-permute-start.5
  10.7 0.2 collective-permute-done.13.refs_12_
  10.9 0.3 collective-permute-start.1
  11.1 0.0 copy-done.3
  11.1 0.2 shard_map.55.refs_1_
  11.3 6.8 %collective-permute-done.12.refs_11_ = bf16[2,2,128,128]{3,2,1,0:T(8,128)(2,1)S(1)} collective-permute-done((bf16[2,2,128,128]{3,2,1,0:T(8,128)(2,1)S(1)}, bf16[2,2,128,128]{3,2,1,0:T(8,128)(2,1)S(1)}, u32[]{:S(2)}, u32[]{:S(2)}) %collective-permute-start.12) | collective-permute-done | bytes 131104 | tf_op jit(solution)/shard_map/ppermute | solution.py:368
  18.1 1.5 %collective-permute-start.7 = (bf16[2,8,2,16,128]{4,3,2,1,0:T(8,128)(2,1)S(1)}, bf16[2,8,2,16,128]{4,3,2,1,0:T(8,128)(2,1)S(1)}, u32[]{:S(2)}, u32[]{:S(2)}) collective-permute-start(bf16[2,8,2,16,128]{4,3,2,1,0:T(8,128)(2,1)S(1)} %get-tuple-element.22), channel_id=1, source_target_pairs={{0,16},{8,24},{16,0},{24,8},{1,17},{9,25},{17,1},{25,9},{2,18},{10... | collective-permute-start | bytes 393224 | tf_op jit(solution)/shard_map/ppermute | solution.py:368
  19.6 0.0 collective-permute-done.11.refs_10_
  19.6 0.0 collective-permute-start.9
  19.6 0.0 collective-permute-done.3.refs_5_
  19.6 0.6 %collective-permute-start.17 = (bf16[2,2,128,128]{3,2,1,0:T(8,128)(2,1)S(1)}, bf16[2,2,128,128]{3,2,1,0:T(8,128)(2,1)S(1)}, u32[]{:S(2)}, u32[]{:S(2)}) collective-permute-start(bf16[2,2,128,128]{3,2,1,0:T(8,128)(2,1)S(1)} %collective-permute-done.13.refs_12_), channel_id=1, source_target_pairs={{0,8},{8,0},{16,24},{24,16},{1,9},{9,1},{17,25},{25,17},{2,10},{10... | collective-permute-start | bytes 393224 | tf_op jit(solution)/shard_map/ppermute | solution.py:368
  20.3 0.0 collective-permute-done.5.refs_7_
  20.3 0.1 collective-permute-start.16
  20.3 0.1 sine_negate_fusion
  20.5 3.1 %collective-permute-done.7.refs_5_ = bf16[2,8,2,16,128]{4,3,2,1,0:T(8,128)(2,1)S(1)} collective-permute-done((bf16[2,8,2,16,128]{4,3,2,1,0:T(8,128)(2,1)S(1)}, bf16[2,8,2,16,128]{4,3,2,1,0:T(8,128)(2,1)S(1)}, u32[]{:S(2)}, u32[]{:S(2)}) %collective-permute-start.7) | collective-permute-done | bytes 131104 | tf_op jit(solution)/shard_map/ppermute | solution.py:368
  23.5 1.5 %collective-permute-start = (bf16[2,16,2,16,128]{4,3,2,1,0:T(8,128)(2,1)S(1)}, bf16[2,16,2,16,128]{4,3,2,1,0:T(8,128)(2,1)S(1)}, u32[]{:S(2)}, u32[]{:S(2)}) collective-permute-start(bf16[2,16,2,16,128]{4,3,2,1,0:T(8,128)(2,1)S(1)} %shard_map.55.refs_1_), channel_id=1, source_target_pairs={{0,1},{1,0},{2,3},{3,2},{4,5},{5,4},{6,7},{7,6},{8,9},{9,8},{10,11... | collective-permute-start | bytes 786440 | tf_op jit(solution)/shard_map/ppermute | solution.py:368
  25.0 0.4 collective-permute-done.9.refs_7_
  25.4 0.3 collective-permute-start.15
  25.7 0.0 collective-permute-done.17.refs_16_
  25.7 1.5 %collective-permute-start.8 = (bf16[2,8,2,16,128]{4,3,2,1,0:T(8,128)(2,1)S(1)}, bf16[2,8,2,16,128]{4,3,2,1,0:T(8,128)(2,1)S(1)}, u32[]{:S(2)}, u32[]{:S(2)}) collective-permute-start(bf16[2,8,2,16,128]{4,3,2,1,0:T(8,128)(2,1)S(1)} %collective-permute-done.7.refs_5_), channel_id=1, source_target_pairs={{0,1},{1,0},{2,3},{3,2},{4,5},{5,4},{6,7},{7,6},{8,9},{9,8},{10,11... | collective-permute-start | bytes 393224 | tf_op jit(solution)/shard_map/ppermute | solution.py:368
  27.2 0.0 collective-permute-done.16.refs_15_
  27.2 0.5 %collective-permute-start.10 = (bf16[2,8,2,16,128]{4,3,2,1,0:T(8,128)(2,1)S(1)}, bf16[2,8,2,16,128]{4,3,2,1,0:T(8,128)(2,1)S(1)}, u32[]{:S(2)}, u32[]{:S(2)}) collective-permute-start(bf16[2,8,2,16,128]{4,3,2,1,0:T(8,128)(2,1)S(1)} %collective-permute-done.9.refs_7_), channel_id=1, source_target_pairs={{0,1},{1,0},{2,3},{3,2},{4,5},{5,4},{6,7},{7,6},{8,9},{9,8},{10,11... | collective-permute-start | bytes 393224 | tf_op jit(solution)/shard_map/ppermute | solution.py:368
  27.7 0.0 collective-permute-done.1.refs_3_
  27.7 1.5 %collective-permute-start.2 = (bf16[2,16,2,16,128]{4,3,2,1,0:T(8,128)(2,1)S(1)}, bf16[2,16,2,16,128]{4,3,2,1,0:T(8,128)(2,1)S(1)}, u32[]{:S(2)}, u32[]{:S(2)}) collective-permute-start(bf16[2,16,2,16,128]{4,3,2,1,0:T(8,128)(2,1)S(1)} %collective-permute-done.1.refs_3_), channel_id=1, source_target_pairs={{0,1},{1,0},{2,3},{3,2},{4,5},{5,4},{6,7},{7,6},{8,9},{9,8},{10,11... | collective-permute-start | bytes 786440 | tf_op jit(solution)/shard_map/ppermute | solution.py:368
  29.2 0.0 copy-done.4
  29.3 0.0 copy-done.1
  29.3 0.3 shard_map.59
  29.6 0.1 pad_add_fusion.numbers.refs_0_
  29.7 2.8 %shard_map.60.refs_17_.refs_10_ = f32[16,256,256]{2,1,0:T(8,128)S(1)} custom-call(s32[32]{0:T(128)S(1)} %pad_add_fusion.numbers.refs_0_, f32[16,256]{1,0:T(8,128)S(1)} %get-tuple-element.30.slow_cos, f32[16,256]{1,0:T(8,128)S(1)} %get-tuple-element.29.slow_sin, f32[256,256]{1,0:T(8,128)S(1)} %get-tuple-element.25.twist.refs_20_.refs_13_), custom_call_target="tpu_custom_call" | custom-call | flops 1000000 | bytes 2000000 | tf_op jit(solution)/shard_map/pallas_call | solution.py:146
  32.5 0.0 collective-permute-done.15.refs_14_
  32.5 0.6 %collective-permute-start.4 = (bf16[2,8,2,16,128]{4,3,2,1,0:T(8,128)(2,1)S(1)}, bf16[2,8,2,16,128]{4,3,2,1,0:T(8,128)(2,1)S(1)}, u32[]{:S(2)}, u32[]{:S(2)}) collective-permute-start(bf16[2,8,2,16,128]{4,3,2,1,0:T(8,128)(2,1)S(1)} %collective-permute-done.3.refs_5_), channel_id=1, source_target_pairs={{0,1},{1,0},{2,3},{3,2},{4,5},{5,4},{6,7},{7,6},{8,9},{9,8},{10,11... | collective-permute-start | bytes 393224 | tf_op jit(solution)/shard_map/ppermute | solution.py:368
  33.1 0.0 collective-permute-done.refs_2_
  33.1 1.5 %collective-permute-start.6 = (bf16[2,8,2,16,128]{4,3,2,1,0:T(8,128)(2,1)S(1)}, bf16[2,8,2,16,128]{4,3,2,1,0:T(8,128)(2,1)S(1)}, u32[]{:S(2)}, u32[]{:S(2)}) collective-permute-start(bf16[2,8,2,16,128]{4,3,2,1,0:T(8,128)(2,1)S(1)} %collective-permute-done.5.refs_7_), channel_id=1, source_target_pairs={{0,1},{1,0},{2,3},{3,2},{4,5},{5,4},{6,7},{7,6},{8,9},{9,8},{10,11... | collective-permute-start | bytes 393224 | tf_op jit(solution)/shard_map/ppermute | solution.py:368
  34.6 0.0 collective-permute-done.8.refs_6_
  34.6 2.5 %collective-permute-done.10.refs_8_ = bf16[2,8,2,16,128]{4,3,2,1,0:T(8,128)(2,1)S(1)} collective-permute-done((bf16[2,8,2,16,128]{4,3,2,1,0:T(8,128)(2,1)S(1)}, bf16[2,8,2,16,128]{4,3,2,1,0:T(8,128)(2,1)S(1)}, u32[]{:S(2)}, u32[]{:S(2)}) %collective-permute-start.10) | collective-permute-done | bytes 131104 | tf_op jit(solution)/shard_map/ppermute | solution.py:368
  37.1 5.6 %collective-permute-done.2.refs_4_ = bf16[2,16,2,16,128]{4,3,2,1,0:T(8,128)(2,1)S(1)} collective-permute-done((bf16[2,16,2,16,128]{4,3,2,1,0:T(8,128)(2,1)S(1)}, bf16[2,16,2,16,128]{4,3,2,1,0:T(8,128)(2,1)S(1)}, u32[]{:S(2)}, u32[]{:S(2)}) %collective-permute-start.2) | collective-permute-done | bytes 262176 | tf_op jit(solution)/shard_map/ppermute | solution.py:368
  42.7 4.3 %shard_map.61 = (f32[2,1024,128]{2,1,0:T(8,128)S(1)}, bf16[2,8,2,128,128]{4,3,2,1,0:T(8,128)(2,1)S(1)}) custom-call(s32[32]{0:T(128)S(1)} %pad_add_fusion.numbers.refs_0_, bf16[2,16,2,16,128]{4,3,2,1,0:T(8,128)(2,1)S(1)} %shard_map.55.refs_1_, bf16[2,16,2,16,128]{4,3,2,1,0:T(8,128)(2,1)S(1)} %collective-permute-done.refs_2_, ...), custom_call_target="tpu_custom_call" | custom-call | flops 3000000000 | bytes 8000000 | tf_op jit(solution)/shard_map/pallas_call | solution.py:343
  47.0 0.0 collective-permute-done.4.refs_6_
  47.1 0.0 collective-permute-done.6.refs_8_
  47.1 5.3 %shard_map.62 = f32[2,2,1024,128]{3,2,1,0:T(8,128)} custom-call(s32[32]{0:T(128)S(1)} %pad_add_fusion.numbers.refs_0_, bf16[2,16,2,16,128]{4,3,2,1,0:T(8,128)(2,1)S(1)} %shard_map.55.refs_1_, bf16[2,16,2,16,128]{4,3,2,1,0:T(8,128)(2,1)S(1)} %collective-permute-done.refs_2_, bf16[2,16,2,16,128]{4,3,2,1,0:T(8,128)(2,1)S(1)} %collective-permute-done.1.refs_3_, ...), custom_call_target="tpu_custom_call" | custom-call | flops 3000000000 | bytes 8000000 | tf_op jit(solution)/shard_map/pallas_call | solution.py:343
  (2 shorter events, 0.0 us)
Async XLA Ops:
  0.0 0.9 %copy-start.2 = (bf16[2,2,32768]{2,1,0:T(2,128)(2,1)S(1)}, bf16[2,2,32768]{2,1,0:T(2,128)(2,1)}, u32[]{:S(2)}) copy-start(bf16[2,2,32768]{2,1,0:T(2,128)(2,1)} %filters.1) | copy-start | bytes 786436
  1.0 10.2 %copy-start.3 = (s32[16]{0:T(128)S(1)}, s32[16]{0:T(128)}, u32[]{:S(2)}) copy-start(s32[16]{0:T(128)} %param.8) | copy-start | bytes 196
  1.0 28.3 %copy-start.4 = (s32[16]{0:T(128)S(1)}, s32[16]{0:T(128)}, u32[]{:S(2)}) copy-start(s32[16]{0:T(128)} %param.7) | copy-start | bytes 196
  1.2 9.4 %collective-permute-start.14 = (bf16[2,2,128,128]{3,2,1,0:T(8,128)(2,1)S(1)}, bf16[2,2,128,128]{3,2,1,0:T(8,128)(2,1)S(1)}, u32[]{:S(2)}, u32[]{:S(2)}) collective-permute-start(bf16[2,2,128,128]{3,2,1,0:T(8,128)(2,1)S(1)} %shard_map.58.refs_9_), channel_id=1, source_target_pairs={{0,8},{8,0},{16,24},{24,16},{1,9},{9,1},{17,25},{25,17},{2,10},{10... | collective-permute-start | bytes 393224 | tf_op jit(solution)/shard_map/ppermute | solution.py:368
  1.8 9.1 %collective-permute-start.13 = (bf16[2,2,128,128]{3,2,1,0:T(8,128)(2,1)S(1)}, bf16[2,2,128,128]{3,2,1,0:T(8,128)(2,1)S(1)}, u32[]{:S(2)}, u32[]{:S(2)}) collective-permute-start(bf16[2,2,128,128]{3,2,1,0:T(8,128)(2,1)S(1)} %shard_map.58.refs_9_), channel_id=1, source_target_pairs={{0,6},{2,4},{4,2},{6,0},{1,7},{3,5},{5,3},{7,1},{8,14},{10,12},{12... | collective-permute-start | bytes 393224 | tf_op jit(solution)/shard_map/ppermute | solution.py:368
  6.4 11.7 %collective-permute-start.12 = (bf16[2,2,128,128]{3,2,1,0:T(8,128)(2,1)S(1)}, bf16[2,2,128,128]{3,2,1,0:T(8,128)(2,1)S(1)}, u32[]{:S(2)}, u32[]{:S(2)}) collective-permute-start(bf16[2,2,128,128]{3,2,1,0:T(8,128)(2,1)S(1)} %shard_map.58.refs_9_), channel_id=1, source_target_pairs={{0,4},{2,6},{4,0},{6,2},{1,5},{3,7},{5,1},{7,3},{8,12},{10,14},{12... | collective-permute-start | bytes 393224 | tf_op jit(solution)/shard_map/ppermute | solution.py:368
  6.4 13.2 %collective-permute-start.11 = (bf16[2,2,128,128]{3,2,1,0:T(8,128)(2,1)S(1)}, bf16[2,2,128,128]{3,2,1,0:T(8,128)(2,1)S(1)}, u32[]{:S(2)}, u32[]{:S(2)}) collective-permute-start(bf16[2,2,128,128]{3,2,1,0:T(8,128)(2,1)S(1)} %shard_map.58.refs_9_), channel_id=1, source_target_pairs={{0,2},{2,0},{4,6},{6,4},{1,3},{3,1},{5,7},{7,5},{8,10},{10,8},{12,... | collective-permute-start | bytes 393224 | tf_op jit(solution)/shard_map/ppermute | solution.py:368
  7.1 1.2 %copy-start = (bf16[2,64,4096]{2,1,0:T(8,128)(2,1)S(1)}, bf16[2,64,4096]{2,1,0:T(8,128)(2,1)}, u32[]{:S(2)}) copy-start(bf16[2,64,4096]{2,1,0:T(8,128)(2,1)} %echoes.2) | copy-start | bytes 3145732
  8.3 21.0 %copy-start.1 = (bf16[3328,256]{1,0:T(8,128)(2,1)S(1)}, bf16[3328,256]{1,0:T(8,128)(2,1)}, u32[]{:S(2)}) copy-start(bf16[3328,256]{1,0:T(8,128)(2,1)} %constant.46.clone.dots.refs_19_.refs_12_) | copy-start | bytes 5111812
  8.5 11.1 %collective-permute-start.3 = (bf16[2,8,2,16,128]{4,3,2,1,0:T(8,128)(2,1)S(1)}, bf16[2,8,2,16,128]{4,3,2,1,0:T(8,128)(2,1)S(1)}, u32[]{:S(2)}, u32[]{:S(2)}) collective-permute-start(bf16[2,8,2,16,128]{4,3,2,1,0:T(8,128)(2,1)S(1)} %get-tuple-element.20), channel_id=1, source_target_pairs={{0,16},{8,24},{16,0},{24,8},{1,17},{9,25},{17,1},{25,9},{2,18},{10... | collective-permute-start | bytes 393224 | tf_op jit(solution)/shard_map/ppermute | solution.py:368
  10.6 9.7 %collective-permute-start.5 = (bf16[2,8,2,16,128]{4,3,2,1,0:T(8,128)(2,1)S(1)}, bf16[2,8,2,16,128]{4,3,2,1,0:T(8,128)(2,1)S(1)}, u32[]{:S(2)}, u32[]{:S(2)}) collective-permute-start(bf16[2,8,2,16,128]{4,3,2,1,0:T(8,128)(2,1)S(1)} %get-tuple-element.21), channel_id=1, source_target_pairs={{0,24},{8,16},{16,8},{24,0},{1,25},{9,17},{17,9},{25,1},{2,26},{10... | collective-permute-start | bytes 393224 | tf_op jit(solution)/shard_map/ppermute | solution.py:368
  10.9 16.9 %collective-permute-start.1 = (bf16[2,16,2,16,128]{4,3,2,1,0:T(8,128)(2,1)S(1)}, bf16[2,16,2,16,128]{4,3,2,1,0:T(8,128)(2,1)S(1)}, u32[]{:S(2)}, u32[]{:S(2)}) collective-permute-start(bf16[2,16,2,16,128]{4,3,2,1,0:T(8,128)(2,1)S(1)} %get-tuple-element.19), channel_id=1, source_target_pairs={{0,8},{8,0},{16,24},{24,16},{1,9},{9,1},{17,25},{25,17},{2,10},{10... | collective-permute-start | bytes 786440 | tf_op jit(solution)/shard_map/ppermute | solution.py:368
  18.1 5.4 %collective-permute-start.7 = (bf16[2,8,2,16,128]{4,3,2,1,0:T(8,128)(2,1)S(1)}, bf16[2,8,2,16,128]{4,3,2,1,0:T(8,128)(2,1)S(1)}, u32[]{:S(2)}, u32[]{:S(2)}) collective-permute-start(bf16[2,8,2,16,128]{4,3,2,1,0:T(8,128)(2,1)S(1)} %get-tuple-element.22), channel_id=1, source_target_pairs={{0,16},{8,24},{16,0},{24,8},{1,17},{9,25},{17,1},{25,9},{2,18},{10... | collective-permute-start | bytes 393224 | tf_op jit(solution)/shard_map/ppermute | solution.py:368
  19.6 5.8 %collective-permute-start.9 = (bf16[2,8,2,16,128]{4,3,2,1,0:T(8,128)(2,1)S(1)}, bf16[2,8,2,16,128]{4,3,2,1,0:T(8,128)(2,1)S(1)}, u32[]{:S(2)}, u32[]{:S(2)}) collective-permute-start(bf16[2,8,2,16,128]{4,3,2,1,0:T(8,128)(2,1)S(1)} %get-tuple-element.23), channel_id=1, source_target_pairs={{0,24},{8,16},{16,8},{24,0},{1,25},{9,17},{17,9},{25,1},{2,26},{10... | collective-permute-start | bytes 393224 | tf_op jit(solution)/shard_map/ppermute | solution.py:368
  19.6 6.1 %collective-permute-start.17 = (bf16[2,2,128,128]{3,2,1,0:T(8,128)(2,1)S(1)}, bf16[2,2,128,128]{3,2,1,0:T(8,128)(2,1)S(1)}, u32[]{:S(2)}, u32[]{:S(2)}) collective-permute-start(bf16[2,2,128,128]{3,2,1,0:T(8,128)(2,1)S(1)} %collective-permute-done.13.refs_12_), channel_id=1, source_target_pairs={{0,8},{8,0},{16,24},{24,16},{1,9},{9,1},{17,25},{25,17},{2,10},{10... | collective-permute-start | bytes 393224 | tf_op jit(solution)/shard_map/ppermute | solution.py:368
  20.3 6.9 %collective-permute-start.16 = (bf16[2,2,128,128]{3,2,1,0:T(8,128)(2,1)S(1)}, bf16[2,2,128,128]{3,2,1,0:T(8,128)(2,1)S(1)}, u32[]{:S(2)}, u32[]{:S(2)}) collective-permute-start(bf16[2,2,128,128]{3,2,1,0:T(8,128)(2,1)S(1)} %collective-permute-done.12.refs_11_), channel_id=1, source_target_pairs={{0,8},{8,0},{16,24},{24,16},{1,9},{9,1},{17,25},{25,17},{2,10},{10... | collective-permute-start | bytes 393224 | tf_op jit(solution)/shard_map/ppermute | solution.py:368
  23.5 9.6 %collective-permute-start = (bf16[2,16,2,16,128]{4,3,2,1,0:T(8,128)(2,1)S(1)}, bf16[2,16,2,16,128]{4,3,2,1,0:T(8,128)(2,1)S(1)}, u32[]{:S(2)}, u32[]{:S(2)}) collective-permute-start(bf16[2,16,2,16,128]{4,3,2,1,0:T(8,128)(2,1)S(1)} %shard_map.55.refs_1_), channel_id=1, source_target_pairs={{0,1},{1,0},{2,3},{3,2},{4,5},{5,4},{6,7},{7,6},{8,9},{9,8},{10,11... | collective-permute-start | bytes 786440 | tf_op jit(solution)/shard_map/ppermute | solution.py:368
  25.4 7.1 %collective-permute-start.15 = (bf16[2,2,128,128]{3,2,1,0:T(8,128)(2,1)S(1)}, bf16[2,2,128,128]{3,2,1,0:T(8,128)(2,1)S(1)}, u32[]{:S(2)}, u32[]{:S(2)}) collective-permute-start(bf16[2,2,128,128]{3,2,1,0:T(8,128)(2,1)S(1)} %collective-permute-done.11.refs_10_), channel_id=1, source_target_pairs={{0,8},{8,0},{16,24},{24,16},{1,9},{9,1},{17,25},{25,17},{2,10},{10... | collective-permute-start | bytes 393224 | tf_op jit(solution)/shard_map/ppermute | solution.py:368
  25.7 8.9 %collective-permute-start.8 = (bf16[2,8,2,16,128]{4,3,2,1,0:T(8,128)(2,1)S(1)}, bf16[2,8,2,16,128]{4,3,2,1,0:T(8,128)(2,1)S(1)}, u32[]{:S(2)}, u32[]{:S(2)}) collective-permute-start(bf16[2,8,2,16,128]{4,3,2,1,0:T(8,128)(2,1)S(1)} %collective-permute-done.7.refs_5_), channel_id=1, source_target_pairs={{0,1},{1,0},{2,3},{3,2},{4,5},{5,4},{6,7},{7,6},{8,9},{9,8},{10,11... | collective-permute-start | bytes 393224 | tf_op jit(solution)/shard_map/ppermute | solution.py:368
  27.2 9.9 %collective-permute-start.10 = (bf16[2,8,2,16,128]{4,3,2,1,0:T(8,128)(2,1)S(1)}, bf16[2,8,2,16,128]{4,3,2,1,0:T(8,128)(2,1)S(1)}, u32[]{:S(2)}, u32[]{:S(2)}) collective-permute-start(bf16[2,8,2,16,128]{4,3,2,1,0:T(8,128)(2,1)S(1)} %collective-permute-done.9.refs_7_), channel_id=1, source_target_pairs={{0,1},{1,0},{2,3},{3,2},{4,5},{5,4},{6,7},{7,6},{8,9},{9,8},{10,11... | collective-permute-start | bytes 393224 | tf_op jit(solution)/shard_map/ppermute | solution.py:368
  27.7 15.0 %collective-permute-start.2 = (bf16[2,16,2,16,128]{4,3,2,1,0:T(8,128)(2,1)S(1)}, bf16[2,16,2,16,128]{4,3,2,1,0:T(8,128)(2,1)S(1)}, u32[]{:S(2)}, u32[]{:S(2)}) collective-permute-start(bf16[2,16,2,16,128]{4,3,2,1,0:T(8,128)(2,1)S(1)} %collective-permute-done.1.refs_3_), channel_id=1, source_target_pairs={{0,1},{1,0},{2,3},{3,2},{4,5},{5,4},{6,7},{7,6},{8,9},{9,8},{10,11... | collective-permute-start | bytes 786440 | tf_op jit(solution)/shard_map/ppermute | solution.py:368
  32.5 14.5 %collective-permute-start.4 = (bf16[2,8,2,16,128]{4,3,2,1,0:T(8,128)(2,1)S(1)}, bf16[2,8,2,16,128]{4,3,2,1,0:T(8,128)(2,1)S(1)}, u32[]{:S(2)}, u32[]{:S(2)}) collective-permute-start(bf16[2,8,2,16,128]{4,3,2,1,0:T(8,128)(2,1)S(1)} %collective-permute-done.3.refs_5_), channel_id=1, source_target_pairs={{0,1},{1,0},{2,3},{3,2},{4,5},{5,4},{6,7},{7,6},{8,9},{9,8},{10,11... | collective-permute-start | bytes 393224 | tf_op jit(solution)/shard_map/ppermute | solution.py:368
  33.1 13.9 %collective-permute-start.6 = (bf16[2,8,2,16,128]{4,3,2,1,0:T(8,128)(2,1)S(1)}, bf16[2,8,2,16,128]{4,3,2,1,0:T(8,128)(2,1)S(1)}, u32[]{:S(2)}, u32[]{:S(2)}) collective-permute-start(bf16[2,8,2,16,128]{4,3,2,1,0:T(8,128)(2,1)S(1)} %collective-permute-done.5.refs_7_), channel_id=1, source_target_pairs={{0,1},{1,0},{2,3},{3,2},{4,5},{5,4},{6,7},{7,6},{8,9},{9,8},{10,11... | collective-permute-start | bytes 393224 | tf_op jit(solution)/shard_map/ppermute | solution.py:368
